TPU v7x, 32 devices: a whole 2x2x4 slice. The times are simulated.
32 devices in a mesh: seq: 8 (over z, x), head: 4 (over y, core).
Axes of the slice: x: 2, y: 2, z: 4, core: 2. Of those that a mesh axis runs over, the one named last changes fastest.
Arguments:
- queries: bfloat16 [1024, 2048], P('seq', 'head'), may hold values from -5 to 5
- key_rows: bfloat16 [1024, 2048], P('seq', 'head'), may hold values from -5 to 5
- value_rows: bfloat16 [1024, 2048], P('seq', 'head'), may hold values from -6 to 6
- out_weight: bfloat16 [2048, 2048], P('head'), may hold values from -0.125 to 0.125
- grad_out: bfloat16 [1024, 2048], P('seq', 'head'), may hold values from -6 to 6
- pair_offsets: int32 [16], replicated, may hold values from 0 to 1
- far_head_offsets: int32 [16], replicated, may hold values from 0 to 3
Outputs:
- layer_out: bfloat16 [1024, 2048], P('seq')
- grad_queries: bfloat16 [1024, 2048], P('seq', 'head')
- grad_keys: bfloat16 [1024, 2048], P('seq', 'head')
- grad_values: bfloat16 [1024, 2048], P('seq', 'head')
All inputs are finite; a program needn't handle non-finite values.
Results may differ from a plain program's by a relative error of at most 0.009.
Values may be sent and summed in bfloat16 or wider, within the bound.
No kernel may reach another device: no remote copies, remote signals or barrier semaphores. Data moves between devices by JAX's collectives and lax.ppermute only.
A program may use at most 64 MiB of HBM per device.

v0:
```python
import jax
import jax.numpy as jnp
from jax import lax
from jax.sharding import PartitionSpec as P

HEAD_DIM = 128
SPAN = 512


masked_score = -1e30


def shortened(array):
    return jax.tree.map(lambda a: a.astype(jnp.bfloat16) if a.dtype == jnp.float32 else a, array)


def partner(value, axis, distance):
    mask = 2**distance
    pairs = [(source, source ^ mask) for source in range(lax.axis_size(axis))]
    return lax.ppermute(value, axis, pairs)


def select(tensor, token_stride, start_offset):
    head_count = tensor.shape[0]
    number = tensor.shape[1] // token_stride
    shaped = tensor.reshape((head_count, number, token_stride) + tensor.shape[2:])
    lane_ids = lax.broadcasted_iota(jnp.int32, shaped.shape, 2)
    chosen = start_offset.reshape((head_count, 1, 1) + (1,) * (tensor.ndim - 2))
    return jnp.sum(jnp.where(lane_ids == chosen, shaped, jnp.zeros((), tensor.dtype)), axis=2)


def spread(entries, token_stride, start_offset, filler):
    head_count = entries.shape[0]
    number = entries.shape[1]
    layout = (head_count, number, token_stride) + entries.shape[2:]
    lane_ids = lax.broadcasted_iota(jnp.int32, layout, 2)
    chosen = start_offset.reshape((head_count, 1, 1) + (1,) * (entries.ndim - 2))
    placed = jnp.where(lane_ids == chosen, jnp.expand_dims(entries, 2), filler)
    return placed.reshape((head_count, number * token_stride) + entries.shape[2:])


def product(left_side, right_side, pattern):
    return jnp.einsum(pattern, left_side, right_side, preferred_element_type=jnp.float32)


def masked(query_part, key_part, first_row, first_col, factor):
    scores = product(query_part, key_part, "hid,hjd->hij") * factor
    row_ids = first_row + lax.broadcasted_iota(jnp.int32, scores.shape, 1)
    col_ids = first_col + lax.broadcasted_iota(jnp.int32, scores.shape, 2)
    return jnp.where(row_ids >= col_ids, scores, masked_score)


def branch_stats(scores, value_part):
    branch_max = jnp.max(scores, axis=-1)
    weights = jnp.exp(scores - branch_max[..., None])
    numerator = product(weights.astype(jnp.bfloat16), value_part, "hij,hjd->hid")
    return (branch_max, jnp.sum(weights, axis=-1), numerator)


def score_grads(scores, row_max, row_sum, grad_part, value_part, row_delta):
    probability = jnp.exp(scores - row_max[..., None]) / row_sum[..., None]
    prob_grad = product(grad_part, value_part, "hid,hjd->hij")
    score_grad = (probability * (prob_grad - row_delta[..., None])).astype(jnp.bfloat16)
    return (probability.astype(jnp.bfloat16), score_grad)


def local(queries, key_rows, value_rows, out_weight, grad_out, pair_offsets, far_head_offsets):
    tokens = queries.shape[0]
    head_count = queries.shape[1] // HEAD_DIM
    factor = HEAD_DIM ** (-0.5)
    seq_count = lax.axis_size("seq")
    total = tokens * seq_count
    selected = min(SPAN, total // 4)
    local_group = selected // tokens
    local_levels = local_group.bit_length() - 1
    dilation = total // selected
    far_rows = tokens // dilation
    half_rows = tokens // 2
    position = lax.axis_index("seq")
    local_rank = position % local_group
    pair_rank = position % (2 * local_group)
    head_group = lax.axis_index("head")
    pair_branch_shift = lax.dynamic_slice_in_dim(pair_offsets, head_group * head_count, head_count)
    far_branch_shift = lax.dynamic_slice_in_dim(
        far_head_offsets, head_group * head_count, head_count
    )

    def by_head(tensor):
        return tensor.reshape(tokens, head_count, HEAD_DIM).transpose(1, 0, 2)

    def by_token(tensor):
        return tensor.transpose(1, 0, 2).reshape(tokens, head_count * HEAD_DIM)

    def stacked(mine, theirs, bit):
        high = position // 2**bit % 2 == 1
        lower = jnp.where(high, theirs, mine)
        upper = jnp.where(high, mine, theirs)
        return jnp.concatenate([lower, upper], axis=1)

    def joined(mine, theirs, bit):
        return tuple((stacked(first, second, bit) for first, second in zip(mine, theirs)))

    head_queries = by_head(queries)
    head_keys = by_head(key_rows)
    head_values = by_head(value_rows)
    parts = (head_keys, head_values)
    for bit in range(local_levels):
        parts = joined(
            parts,
            jax.tree.map(
                lambda part, own: part.astype(own.dtype),
                partner(shortened(parts), "seq", bit),
                parts,
            ),
            bit,
        )
    segment_key, segment_value = parts
    local_scores = masked(head_queries, segment_key, local_rank * tokens, 0, factor)
    local_stats = branch_stats(local_scores, segment_value)
    pair_query = select(head_queries, 2, pair_branch_shift)
    pair_key = select(head_keys, 2, pair_branch_shift)
    pair_value = select(head_values, 2, pair_branch_shift)
    nearby = (
        select(segment_key, 2, pair_branch_shift),
        select(segment_value, 2, pair_branch_shift),
    )
    pair_all_key, pair_all_value = joined(
        nearby, partner((nearby[0], nearby[1]), "seq", local_levels), local_levels
    )
    pair_scores = masked(pair_query, pair_all_key, pair_rank * half_rows, 0, factor)
    pair_stats = branch_stats(pair_scores, pair_all_value)
    far_query = select(head_queries, dilation, far_branch_shift)
    far_key = select(head_keys, dilation, far_branch_shift)
    far_value = select(head_values, dilation, far_branch_shift)
    every_key, every_value = (
        lax.all_gather(far_key, "seq", axis=1, tiled=True),
        lax.all_gather(far_value, "seq", axis=1, tiled=True),
    )
    far_scores = masked(far_query, every_key, position * far_rows, 0, factor)
    far_stats = branch_stats(far_scores, every_value)
    pair_spread = (
        spread(pair_stats[0], 2, pair_branch_shift, masked_score),
        spread(pair_stats[1], 2, pair_branch_shift, 0.0),
        spread(pair_stats[2], 2, pair_branch_shift, 0.0),
    )
    far_spread = (
        spread(far_stats[0], dilation, far_branch_shift, masked_score),
        spread(far_stats[1], dilation, far_branch_shift, 0.0),
        spread(far_stats[2], dilation, far_branch_shift, 0.0),
    )
    row_max = jnp.maximum(jnp.maximum(local_stats[0], pair_spread[0]), far_spread[0])
    row_sum = jnp.zeros_like(row_max)
    numerator = jnp.zeros_like(local_stats[2])
    for branch in (local_stats, pair_spread, far_spread):
        rescale = jnp.exp(branch[0] - row_max)
        row_sum = row_sum + branch[1] * rescale
        numerator = numerator + branch[2] * rescale[..., None]
    head_out = numerator / row_sum[..., None]
    attended = by_token(head_out).astype(jnp.bfloat16)
    partial_out = jnp.dot(attended, out_weight, preferred_element_type=jnp.float32)
    layer_out = lax.psum(partial_out.astype(jnp.bfloat16), "head")
    grad_attended = lax.dot_general(
        lax.all_gather(grad_out, "head", axis=1, tiled=True),
        out_weight,
        (((1,), (1,)), ((), ())),
        preferred_element_type=jnp.float32,
    )
    head_grads = by_head(grad_attended.astype(jnp.bfloat16))
    row_delta = jnp.sum(head_grads.astype(jnp.float32) * head_out, axis=-1)
    local_prob, local_dscore = score_grads(
        local_scores, row_max, row_sum, head_grads, segment_value, row_delta
    )
    query_grad = product(local_dscore, segment_key, "hij,hjd->hid") * factor
    parts = (head_queries, head_grads)
    for bit in range(local_levels):
        parts = joined(
            parts,
            jax.tree.map(
                lambda part, own: part.astype(own.dtype),
                partner(shortened(parts), "seq", bit),
                parts,
            ),
            bit,
        )
    group_query, group_grad = parts
    parts = (row_max, row_sum, row_delta)
    for bit in range(local_levels):
        parts = joined(parts, partner(parts, "seq", bit), bit)
    group_max, group_sum, group_delta = parts
    back_scores = masked(group_query, head_keys, 0, local_rank * tokens, factor)
    back_prob, back_dscore = score_grads(
        back_scores, group_max, group_sum, group_grad, head_values, group_delta
    )
    key_grad = product(back_dscore, group_query, "hij,hid->hjd") * factor
    value_grad = product(back_prob, group_grad, "hij,hid->hjd")
    pair_grad = select(head_grads, 2, pair_branch_shift)
    pair_max = select(row_max, 2, pair_branch_shift)
    pair_sum = select(row_sum, 2, pair_branch_shift)
    pair_delta = select(row_delta, 2, pair_branch_shift)
    pair_prob, pair_dscore = score_grads(
        pair_scores, pair_max, pair_sum, pair_grad, pair_all_value, pair_delta
    )
    pair_dq = product(pair_dscore, pair_all_key, "hij,hjd->hid") * factor
    near_rows = (
        select(group_query, 2, pair_branch_shift),
        select(group_grad, 2, pair_branch_shift),
    )
    near_moments = (
        select(group_max, 2, pair_branch_shift),
        select(group_sum, 2, pair_branch_shift),
        select(group_delta, 2, pair_branch_shift),
    )
    all_query, all_grad = joined(
        near_rows, partner((near_rows[0], near_rows[1]), "seq", local_levels), local_levels
    )
    all_max, all_sum, all_delta = joined(
        near_moments,
        partner((near_moments[0], near_moments[1], near_moments[2]), "seq", local_levels),
        local_levels,
    )
    pair_back = masked(all_query, pair_key, 0, pair_rank * half_rows, factor)
    pair_back_prob, pair_back_dscore = score_grads(
        pair_back, all_max, all_sum, all_grad, pair_value, all_delta
    )
    pair_dk = product(pair_back_dscore, all_query, "hij,hid->hjd") * factor
    pair_dv = product(pair_back_prob, all_grad, "hij,hid->hjd")
    query_grad = query_grad + spread(pair_dq, 2, pair_branch_shift, 0.0)
    key_grad = key_grad + spread(pair_dk, 2, pair_branch_shift, 0.0)
    value_grad = value_grad + spread(pair_dv, 2, pair_branch_shift, 0.0)
    far_grad = select(head_grads, dilation, far_branch_shift)
    far_max = select(row_max, dilation, far_branch_shift)
    far_sum = select(row_sum, dilation, far_branch_shift)
    far_delta = select(row_delta, dilation, far_branch_shift)
    far_prob, far_dscore = score_grads(
        far_scores, far_max, far_sum, far_grad, every_value, far_delta
    )
    far_dq = product(far_dscore, every_key, "hij,hjd->hid") * factor
    gathered_dk = product(far_dscore, far_query, "hij,hid->hjd") * factor
    gathered_dv = product(far_prob, far_grad, "hij,hid->hjd")
    far_dk, far_dv = (
        lax.psum_scatter(gathered_dk, "seq", scatter_dimension=1, tiled=True),
        lax.psum_scatter(gathered_dv, "seq", scatter_dimension=1, tiled=True),
    )
    query_grad = query_grad + spread(far_dq, dilation, far_branch_shift, 0.0)
    key_grad = key_grad + spread(far_dk, dilation, far_branch_shift, 0.0)
    value_grad = value_grad + spread(far_dv, dilation, far_branch_shift, 0.0)
    return (
        layer_out,
        by_token(query_grad).astype(jnp.bfloat16),
        by_token(key_grad).astype(jnp.bfloat16),
        by_token(value_grad).astype(jnp.bfloat16),
    )


def solution(mesh):
    placed = (
        P("seq", "head"),
        P("seq", "head"),
        P("seq", "head"),
        P("head", None),
        P("seq", "head"),
        P(),
        P(),
    )
    return jax.shard_map(
        local,
        mesh=mesh,
        in_specs=placed,
        out_specs=(P("seq", None), P("seq", "head"), P("seq", "head"), P("seq", "head")),
        check_vma=False,
    )
```

profile of v0, /device:TPU:0, one launch (start us, length us, event | category | flops | bytes accessed | tf_op | source)
XLA Modules:
  0.0 276.7 jit_solution(4491126883245976040)
XLA Ops:
  8.1 1.2 copy.117
  9.4 3.0 %collective-permute-start.1 = (bf16[4,128,128]{2,1,0:T(8,128)(2,1)S(1)}, bf16[4,128,128]{2,1,0:T(8,128)(2,1)S(1)}, u32[]{:S(2)}, u32[]{:S(2)}) collective-permute-start(bf16[4,128,128]{2,1,0:T(8,128)(2,1)S(1)} %bitcast.103), channel_id=1, source_target_pairs={{0,4},{4,0},{8,12},{12,8},{16,20},{20,16},{24,28},{28,24},{1,5},{5... | collective-permute-start | bytes 393224 | tf_op jit(solution)/shard_map/ppermute | solution.py:20
  14.8 2.1 collective-permute-start.4
  16.9 7.4 %all_gather.11 = bf16[128,2048]{1,0:T(8,128)(2,1)S(1)} all-gather(bf16[128,512]{1,0:T(8,128)(2,1)} %param.11), channel_id=1, replica_groups=mesh['seq'=8,'head'=4] {'head'}, dimensions={1}, use_global_device_ids=true | all-gather | bytes 655360 | tf_op jit(solution)/shard_map/all_gather | solution.py:163
  26.2 1.4 fusion.85
  27.6 31.1 %all_gather.10 = bf16[4,256,128]{2,1,0:T(8,128)(2,1)S(1)} all-gather(bf16[4,32,128]{2,1,0:T(8,128)(2,1)S(1)} %get-tuple-element.33), channel_id=1, replica_groups=mesh['seq'=8,'head'=4] {'seq'}, dimensions={1}, use_global_device_ids=true | all-gather | bytes 294912 | tf_op jit(solution)/shard_map/all_gather | solution.py:137
  58.7 30.9 %all_gather.9 = bf16[4,256,128]{2,1,0:T(8,128)(2,1)S(1)} all-gather(bf16[4,32,128]{2,1,0:T(8,128)(2,1)S(1)} %get-tuple-element.34), channel_id=1, replica_groups=mesh['seq'=8,'head'=4] {'seq'}, dimensions={1}, use_global_device_ids=true | all-gather | bytes 294912 | tf_op jit(solution)/shard_map/all_gather | solution.py:136
  91.0 2.2 fusion.95
  100.5 3.8 %fusion.76 = (bf16[4,128,128]{2,1,0:T(8,128)(2,1)}, bf16[4,128,128]{2,1,0:T(8,128)(2,1)}, bf16[4,128,128]{2,1,0:T(8,128)(2,1)}, bf16[4,128,128]{2,1,0:T(8,128)(2,1)}) fusion(bf16[4,128,2,128]{3,2,1,0:T(2,128)(2,1)S(1)} %bitcast.119, s32[4]{0:T(128)S(1)} %dynamic_slice.6, bf16[4,128,2,128]{3,2,1,0:T(2,128)(2,1)S(1)} %bitcast.116, ...), kind=kLoop, calls=%fused_computation.117 | loop fusion | flops 917504 | bytes 1572880 | tf_op jit(solution)/shard_map/reduce_sum | solution.py:29
  104.4 2.0 collective-permute-start.2
  108.2 1.1 fusion.51
  112.1 1.9 fusion.140
  114.0 1.1 fusion.77
  121.6 1.2 fusion.80
  122.8 1.3 fusion.124
  125.1 2.3 multiply_reduce_fusion
  128.2 1.8 fusion.119
  130.5 1.9 fusion.116
  134.5 1.4 iota.223
  135.9 1.4 copy.136
  137.3 1.4 copy.133
  139.3 1.4 collective-permute-start.9
  140.7 1.5 collective-permute-start.8
  142.7 1.4 copy.139
  144.1 1.7 copy.126
  145.8 1.5 collective-permute-start.5
  148.9 1.9 convolution_multiply_fusion
  151.8 2.1 select_reduce_fusion.5
  156.4 1.6 convolution_multiply_fusion.7
  158.1 2.1 fusion.39
  160.3 1.3 convolution_convert_fusion
  161.5 1.7 broadcast_in_dim.260
  163.2 1.6 broadcast_in_dim.266
  164.9 2.4 fusion.37
  170.0 1.6 broadcast_select_fusion.3
  174.2 1.2 select_reduce_fusion
  176.0 1.3 fusion.4
  177.3 1.5 collective-permute-start.11
  179.7 2.0 collective-permute-done.11
  184.4 1.3 pad_maximum_fusion.23
  186.4 1.2 fusion.26
  188.3 2.1 fusion.40
  190.4 5.7 %reduce-scatter.5.cloned.1.call-done = f32[4,32,128]{2,1,0:T(8,128)} async-done(((f32[4,256,128]{2,1,0:T(8,128)}), f32[4,32,128]{2,1,0:T(8,128)}) %reduce-scatter.5.cloned.1.call-update) | async-done | bytes 65552 | tf_op jit(solution)/shard_map/reduce_scatter | solution.py:242
  199.0 62.7 %reduce-scatter.3.cloned.1.call-done = f32[4,32,128]{2,1,0:T(8,128)} async-done(((f32[4,256,128]{2,1,0:T(8,128)}), f32[4,32,128]{2,1,0:T(8,128)}) %reduce-scatter.3.cloned.1.call-update) | async-done | bytes 65552 | tf_op jit(solution)/shard_map/reduce_scatter | solution.py:241
  261.7 1.7 broadcast_in_dim.271
  263.4 1.6 broadcast_in_dim.273
  264.9 1.5 fusion.38
  267.4 1.9 copy.174
  (206 shorter events, 49.0 us)
Async XLA Ops:
  8.0 16.3 %copy-start = (bf16[512,2048]{1,0:T(8,128)(2,1)S(1)}, bf16[512,2048]{1,0:T(8,128)(2,1)}, u32[]{:S(2)}) copy-start(bf16[512,2048]{1,0:T(8,128)(2,1)} %param.10) | copy-start | bytes 6291460
  8.0 188.1 %reduce-scatter.5.cloned.1.call-start = ((), (), s32[]{:S(2)}) async-start(), calls=%async_computation.4 | async-start | bytes 589824 | tf_op jit(solution)/shard_map/reduce_scatter | solution.py:242
  9.4 88.0 %collective-permute-start.1 = (bf16[4,128,128]{2,1,0:T(8,128)(2,1)S(1)}, bf16[4,128,128]{2,1,0:T(8,128)(2,1)S(1)}, u32[]{:S(2)}, u32[]{:S(2)}) collective-permute-start(bf16[4,128,128]{2,1,0:T(8,128)(2,1)S(1)} %bitcast.103), channel_id=1, source_target_pairs={{0,4},{4,0},{8,12},{12,8},{16,20},{20,16},{24,28},{28,24},{1,5},{5... | collective-permute-start | bytes 393224 | tf_op jit(solution)/shard_map/ppermute | solution.py:20
  13.6 84.9 %collective-permute-start = (bf16[4,128,128]{2,1,0:T(8,128)(2,1)S(1)}, bf16[4,128,128]{2,1,0:T(8,128)(2,1)}, u32[]{:S(2)}, u32[]{:S(2)}) collective-permute-start(bf16[4,128,128]{2,1,0:T(8,128)(2,1)S(1)} %bitcast.106), channel_id=1, source_target_pairs={{0,4},{4,0},{8,12},{12,8},{16,20},{20,16},{24,28},{28,24},{1,5},{5... | collective-permute-start | bytes 393224 | tf_op jit(solution)/shard_map/ppermute | solution.py:20
  14.7 11.3 %copy-start.42 = (s32[16]{0:T(128)S(1)}, s32[16]{0:T(128)}, u32[]{:S(2)}) copy-start(s32[16]{0:T(128)} %param.12) | copy-start | bytes 196
  14.7 11.4 %copy-start.43 = (s32[16]{0:T(128)S(1)}, s32[16]{0:T(128)}, u32[]{:S(2)}) copy-start(s32[16]{0:T(128)} %param.13) | copy-start | bytes 196
  14.8 82.5 %collective-permute-start.4 = (bf16[4,128,128]{2,1,0:T(8,128)(2,1)S(1)}, bf16[4,128,128]{2,1,0:T(8,128)(2,1)}, u32[]{:S(2)}, u32[]{:S(2)}) collective-permute-start(bf16[4,128,128]{2,1,0:T(8,128)(2,1)S(1)} %bitcast.112), channel_id=1, source_target_pairs={{0,4},{4,0},{8,12},{12,8},{16,20},{20,16},{24,28},{28,24},{1,5},{5... | collective-permute-start | bytes 393224 | tf_op jit(solution)/shard_map/ppermute | solution.py:20
  25.4 74.1 %collective-permute-start.7 = (bf16[4,128,128]{2,1,0:T(8,128)(2,1)S(1)}, bf16[4,128,128]{2,1,0:T(8,128)(2,1)}, u32[]{:S(2)}, u32[]{:S(2)}) collective-permute-start(bf16[4,128,128]{2,1,0:T(8,128)(2,1)S(1)} %bitcast.109), channel_id=1, source_target_pairs={{0,4},{4,0},{8,12},{12,8},{16,20},{20,16},{24,28},{28,24},{1,5},{5... | collective-permute-start | bytes 393224 | tf_op jit(solution)/shard_map/ppermute | solution.py:20
  26.1 74.4 %copy-start.29 = (s32[4]{0:T(128)}, s32[4]{0:T(128)S(1)}, u32[]{:S(2)}) copy-start(s32[4]{0:T(128)S(1)} %dynamic_slice.6) | copy-start | bytes 52
  26.2 63.5 %copy-start.34 = (s32[4]{0:T(128)}, s32[4]{0:T(128)S(1)}, u32[]{:S(2)}) copy-start(s32[4]{0:T(128)S(1)} %dynamic_slice.7) | copy-start | bytes 52
  27.6 69.8 %copy-start.21 = (bf16[4,32,128]{2,1,0:T(8,128)(2,1)}, bf16[4,32,128]{2,1,0:T(8,128)(2,1)S(1)}, u32[]{:S(2)}) copy-start(bf16[4,32,128]{2,1,0:T(8,128)(2,1)S(1)} %get-tuple-element.35) | copy-start | bytes 98308
  93.2 13.2 %copy-start.44 = (s32[128]{0:T(128)}, s32[128]{0:T(128)S(1)}, u32[]{:S(2)}) copy-start(s32[128]{0:T(128)S(1)} %iota_add_fusion.2) | copy-start | bytes 1540
  99.4 8.0 %copy-start.15 = (bf16[4,128,128]{2,1,0:T(8,128)(2,1)}, bf16[4,128,128]{2,1,0:T(8,128)(2,1)S(1)}, u32[]{:S(2)}) copy-start(bf16[4,128,128]{2,1,0:T(8,128)(2,1)S(1)} %get-tuple-element.58) | copy-start | bytes 393220
  99.4 8.0 %copy-start.17 = (bf16[4,128,128]{2,1,0:T(8,128)(2,1)}, bf16[4,128,128]{2,1,0:T(8,128)(2,1)S(1)}, u32[]{:S(2)}) copy-start(bf16[4,128,128]{2,1,0:T(8,128)(2,1)S(1)} %get-tuple-element.59) | copy-start | bytes 393220
  104.4 15.6 %collective-permute-start.3 = (bf16[4,128,128]{2,1,0:T(8,128)(2,1)}, bf16[4,128,128]{2,1,0:T(8,128)(2,1)}, u32[]{:S(2)}, u32[]{:S(2)}) collective-permute-start(bf16[4,128,128]{2,1,0:T(8,128)(2,1)} %get-tuple-element.25), channel_id=1, source_target_pairs={{0,8},{4,12},{8,0},{12,4},{16,24},{20,28},{24,16},{28,20},{1,9},{5... | collective-permute-start | bytes 393224 | tf_op jit(solution)/shard_map/ppermute | solution.py:20
  104.4 6.7 %collective-permute-start.2 = (bf16[4,128,128]{2,1,0:T(8,128)(2,1)}, bf16[4,128,128]{2,1,0:T(8,128)(2,1)}, u32[]{:S(2)}, u32[]{:S(2)}) collective-permute-start(bf16[4,128,128]{2,1,0:T(8,128)(2,1)} %get-tuple-element.26), channel_id=1, source_target_pairs={{0,8},{4,12},{8,0},{12,4},{16,24},{20,28},{24,16},{28,20},{1,9},{5... | collective-permute-start | bytes 393224 | tf_op jit(solution)/shard_map/ppermute | solution.py:20
  107.4 17.7 %copy-start.27 = (f32[4,128]{1,0:T(4,128)}, f32[4,128]{1,0:T(4,128)S(1)}, u32[]{:S(2)}) copy-start(f32[4,128]{1,0:T(4,128)S(1)} %get-tuple-element.76) | copy-start | bytes 6148
  109.3 15.8 %copy-start.28 = (f32[4,128]{1,0:T(4,128)}, f32[4,128]{1,0:T(4,128)S(1)}, u32[]{:S(2)}) copy-start(f32[4,128]{1,0:T(4,128)S(1)} %fusion.51) | copy-start | bytes 6148
  124.1 3.3 %copy-start.38 = (f32[4,128]{1,0:T(4,128)}, f32[4,128]{1,0:T(4,128)S(1)}, u32[]{:S(2)}) copy-start(f32[4,128]{1,0:T(4,128)S(1)} %get-tuple-element.37) | copy-start | bytes 6148
  125.1 14.2 %copy-start.2 = (bf16[4,128,128]{2,1,0:T(8,128)(2,1)S(1)}, bf16[4,128,128]{2,1,0:T(8,128)(2,1)}, u32[]{:S(2)}) copy-start(bf16[4,128,128]{2,1,0:T(8,128)(2,1)} %get-tuple-element.24) | copy-start | bytes 393220
  127.4 5.8 %copy-start.32 = (f32[4,128]{1,0:T(4,128)}, f32[4,128]{1,0:T(4,128)S(1)}, u32[]{:S(2)}) copy-start(f32[4,128]{1,0:T(4,128)S(1)} %get-tuple-element.46) | copy-start | bytes 6148
  130.0 3.2 %copy-start.36 = (f32[4,32]{1,0:T(4,128)}, f32[4,32]{1,0:T(4,128)S(1)}, u32[]{:S(2)}) copy-start(f32[4,32]{1,0:T(4,128)S(1)} %get-tuple-element.18) | copy-start | bytes 1540
  132.5 129.2 %reduce-scatter.3.cloned.1.call-start = ((), (), s32[]{:S(2)}) async-start(), calls=%async_computation.3 | async-start | bytes 589824 | tf_op jit(solution)/shard_map/reduce_scatter | solution.py:241
  133.9 17.2 %copy-start.26 = (f32[4,32]{0,1:T(8,128)S(1)}, f32[4,32]{0,1:T(8,128)}, u32[]{:S(2)}) copy-start(f32[4,32]{0,1:T(8,128)} %copy.137) | copy-start | bytes 1540
  138.7 30.4 %collective-permute-start.12 = (bf16[4,128,128]{2,1,0:T(8,128)(2,1)}, bf16[4,128,128]{2,1,0:T(8,128)(2,1)}, u32[]{:S(2)}, u32[]{:S(2)}) collective-permute-start(bf16[4,128,128]{2,1,0:T(8,128)(2,1)} %get-tuple-element.23), channel_id=1, source_target_pairs={{0,8},{4,12},{8,0},{12,4},{16,24},{20,28},{24,16},{28,20},{1,9},{5... | collective-permute-start | bytes 393224 | tf_op jit(solution)/shard_map/ppermute | solution.py:20
  139.3 30.7 %collective-permute-start.9 = (bf16[4,128,128]{2,1,0:T(8,128)(2,1)S(1)}, bf16[4,128,128]{2,1,0:T(8,128)(2,1)}, u32[]{:S(2)}, u32[]{:S(2)}) collective-permute-start(bf16[4,128,128]{2,1,0:T(8,128)(2,1)S(1)} %copy-done.2), channel_id=1, source_target_pairs={{0,8},{4,12},{8,0},{12,4},{16,24},{20,28},{24,16},{28,20},{1,9},{5... | collective-permute-start | bytes 393224 | tf_op jit(solution)/shard_map/ppermute | solution.py:20
  140.7 32.7 %collective-permute-start.8 = (f32[4,128]{1,0:T(4,128)}, f32[4,128]{1,0:T(4,128)}, u32[]{:S(2)}, u32[]{:S(2)}) collective-permute-start(f32[4,128]{1,0:T(4,128)} %copy-done.32), channel_id=1, source_target_pairs={{0,4},{4,0},{8,12},{12,8},{16,20},{20,16},{24,28},{28,24},{1,5},{5... | collective-permute-start | bytes 6152 | tf_op jit(solution)/shard_map/ppermute | solution.py:20
  142.2 30.2 %collective-permute-start.6 = (f32[4,128]{1,0:T(4,128)}, f32[4,128]{1,0:T(4,128)}, u32[]{:S(2)}, u32[]{:S(2)}) collective-permute-start(f32[4,128]{1,0:T(4,128)} %copy-done.38), channel_id=1, source_target_pairs={{0,4},{4,0},{8,12},{12,8},{16,20},{20,16},{24,28},{28,24},{1,5},{5... | collective-permute-start | bytes 6152 | tf_op jit(solution)/shard_map/ppermute | solution.py:20
  145.8 25.9 %collective-permute-start.5 = (f32[4,128]{1,0:T(4,128)}, f32[4,128]{1,0:T(4,128)}, u32[]{:S(2)}, u32[]{:S(2)}) collective-permute-start(f32[4,128]{1,0:T(4,128)} %get-tuple-element.41), channel_id=1, source_target_pairs={{0,4},{4,0},{8,12},{12,8},{16,20},{20,16},{24,28},{28,24},{1,5},{5... | collective-permute-start | bytes 6152 | tf_op jit(solution)/shard_map/ppermute | solution.py:20
  148.9 9.2 %copy-start.1 = (f32[4,64,256]{2,1,0:T(8,128)S(1)}, f32[4,64,256]{2,1,0:T(8,128)}, u32[]{:S(2)}) copy-start(f32[4,64,256]{2,1,0:T(8,128)} %get-tuple-element.73) | copy-start | bytes 786436
  148.9 9.2 %copy-start.5 = (bf16[4,128,128]{2,1,0:T(8,128)(2,1)S(1)}, bf16[4,128,128]{2,1,0:T(8,128)(2,1)}, u32[]{:S(2)}) copy-start(bf16[4,128,128]{2,1,0:T(8,128)(2,1)} %copy-done.4) | copy-start | bytes 393220
  150.8 116.6 %all-reduce.2.cloned.1.call-start = ((), (), s32[]{:S(2)}) async-start(), calls=%async_computation.2 | async-start | bytes 1048576 | tf_op jit(solution)/shard_map/psum | solution.py:161
  160.2 4.6 %copy-start.12 = (bf16[4,128,128]{2,1,0:T(8,128)(2,1)S(1)}, bf16[4,128,128]{2,1,0:T(8,128)(2,1)}, u32[]{:S(2)}) copy-start(bf16[4,128,128]{2,1,0:T(8,128)(2,1)} %copy-done.11) | copy-start | bytes 393220
  160.2 4.6 %copy-start.14 = (bf16[4,128,128]{2,1,0:T(8,128)(2,1)S(1)}, bf16[4,128,128]{2,1,0:T(8,128)(2,1)}, u32[]{:S(2)}) copy-start(bf16[4,128,128]{2,1,0:T(8,128)(2,1)} %copy-done.13) | copy-start | bytes 393220
  160.2 4.6 %copy-start.16 = (bf16[4,128,128]{2,1,0:T(8,128)(2,1)S(1)}, bf16[4,128,128]{2,1,0:T(8,128)(2,1)}, u32[]{:S(2)}) copy-start(bf16[4,128,128]{2,1,0:T(8,128)(2,1)} %copy-done.15) | copy-start | bytes 393220
  160.2 4.6 %copy-start.18 = (bf16[4,128,128]{2,1,0:T(8,128)(2,1)S(1)}, bf16[4,128,128]{2,1,0:T(8,128)(2,1)}, u32[]{:S(2)}) copy-start(bf16[4,128,128]{2,1,0:T(8,128)(2,1)} %copy-done.17) | copy-start | bytes 393220
  160.2 4.6 %copy-start.30 = (s32[4]{0:T(128)S(1)}, s32[4]{0:T(128)}, u32[]{:S(2)}) copy-start(s32[4]{0:T(128)} %copy-done.29) | copy-start | bytes 52
  160.2 4.6 %copy-start.33 = (f32[4,128]{1,0:T(4,128)S(1)}, f32[4,128]{1,0:T(4,128)}, u32[]{:S(2)}) copy-start(f32[4,128]{1,0:T(4,128)} %copy-done.32) | copy-start | bytes 6148
  160.2 4.6 %copy-start.35 = (s32[4]{0:T(128)S(1)}, s32[4]{0:T(128)}, u32[]{:S(2)}) copy-start(s32[4]{0:T(128)} %copy-done.34) | copy-start | bytes 52
  160.2 4.6 %copy-start.39 = (f32[4,128]{1,0:T(4,128)S(1)}, f32[4,128]{1,0:T(4,128)}, u32[]{:S(2)}) copy-start(f32[4,128]{1,0:T(4,128)} %copy-done.38) | copy-start | bytes 6148
  164.9 4.2 %copy-start.3 = (bf16[4,128,128]{2,1,0:T(8,128)(2,1)S(1)}, bf16[4,128,128]{2,1,0:T(8,128)(2,1)}, u32[]{:S(2)}) copy-start(bf16[4,128,128]{2,1,0:T(8,128)(2,1)} %get-tuple-element.23) | copy-start | bytes 393220
  167.2 4.4 %copy-start.40 = (f32[4,128]{1,0:T(4,128)S(1)}, f32[4,128]{1,0:T(4,128)}, u32[]{:S(2)}) copy-start(f32[4,128]{1,0:T(4,128)} %get-tuple-element.41) | copy-start | bytes 6148
  175.4 4.3 %collective-permute-start.13 = (f32[4,128]{0,1:T(8,128)S(1)}, f32[4,128]{0,1:T(8,128)S(1)}, u32[]{:S(2)}, u32[]{:S(2)}) collective-permute-start(f32[4,128]{0,1:T(8,128)S(1)} %get-tuple-element.20), channel_id=1, source_target_pairs={{0,8},{4,12},{8,0},{12,4},{16,24},{20,28},{24,16},{28,20},{1,9},{5... | collective-permute-start | bytes 6152 | tf_op jit(solution)/shard_map/ppermute | solution.py:20
  177.3 4.3 %collective-permute-start.11 = (f32[4,128]{0,1:T(8,128)S(1)}, f32[4,128]{0,1:T(8,128)S(1)}, u32[]{:S(2)}, u32[]{:S(2)}) collective-permute-start(f32[4,128]{0,1:T(8,128)S(1)} %get-tuple-element.21), channel_id=1, source_target_pairs={{0,8},{4,12},{8,0},{12,4},{16,24},{20,28},{24,16},{28,20},{1,9},{5... | collective-permute-start | bytes 6152 | tf_op jit(solution)/shard_map/ppermute | solution.py:20
  178.8 4.6 %collective-permute-start.10 = (f32[4,128]{0,1:T(8,128)}, f32[4,128]{0,1:T(8,128)}, u32[]{:S(2)}, u32[]{:S(2)}) collective-permute-start(f32[4,128]{0,1:T(8,128)} %get-tuple-element.22), channel_id=1, source_target_pairs={{0,8},{4,12},{8,0},{12,4},{16,24},{20,28},{24,16},{28,20},{1,9},{5... | collective-permute-start | bytes 6152 | tf_op jit(solution)/shard_map/ppermute | solution.py:20
  186.4 10.7 %copy-start.41 = (s32[128]{0:T(128)S(1)}, s32[128]{0:T(128)}, u32[]{:S(2)}) copy-start(s32[128]{0:T(128)} %iota.205) | copy-start | bytes 1540
  188.3 76.6 %copy-start.8 = (bf16[4,128,128]{2,1,0:T(8,128)(2,1)S(1)}, bf16[4,128,128]{2,1,0:T(8,128)(2,1)}, u32[]{:S(2)}) copy-start(bf16[4,128,128]{2,1,0:T(8,128)(2,1)} %copy-done.7) | copy-start | bytes 393220
  190.4 74.5 %copy-start.10 = (bf16[4,128,128]{2,1,0:T(8,128)(2,1)S(1)}, bf16[4,128,128]{2,1,0:T(8,128)(2,1)}, u32[]{:S(2)}) copy-start(bf16[4,128,128]{2,1,0:T(8,128)(2,1)} %copy-done.9) | copy-start | bytes 393220
  (14 other events, 22.7 us)
Sparse Core Ops, SparseCore 0:
  132.6 63.4 reduce-scatter.4
  199.4 62.1 reduce-scatter.2
Sparse Core Ops, SparseCore 1:
  169.2 32.6 all-reduce.1
where the time goes:
time: 279 us; the launch traced here: 277 us
  waiting for transfers between devices  72 us (26%)
  blocking collectives  69.5 us (25%)
  local copies, waits for them, and re-layouts  45.5 us (16%)
  other arithmetic  29.3 us (11%)
  matrix products  27.8 us (10%)
  starting transfers between devices  16.4 us (6%)
  between operations  16.2 us (6%)
    reduce_scatter x1, waiting for transfers between devices, local(): lax.psum_scatter(gathered_dk, 'seq', scatter_dimension=1, tiled=True)  62.7 us
    all_gather x1, blocking collectives, local(): lax.all_gather(far_value, 'seq', axis=1, tiled=True)  31.1 us
    all_gather x1, blocking collectives, local(): lax.all_gather(far_key, 'seq', axis=1, tiled=True)  30.9 us
    dot_general x18, matrix products, product(): jnp.einsum(pattern, left_side, right_side, preferred_element_type=jnp.flo...  25.6 us
    ppermute x14, starting transfers between devices, partner(): return lax.ppermute(value, axis, pairs)  16 us
    broadcast_in_dim x20, local copies, waits for them, and re-layouts, spread(): placed = jnp.where(lane_ids == chosen, jnp.expand_dims(entries, 2), filler)  14.8 us
    reduce_sum x6, other arithmetic, select(): jnp.sum(jnp.where(lane_ids == chosen, shaped, jnp.zeros((), tensor.dtype)...  12.6 us
    select_n x14, other arithmetic, stacked(): lower = jnp.where(high, theirs, mine)  10.4 us
  transfers between devices with their start and end apart: 17, of which 6 were waited for; matrix products, arithmetic and copies ran while one was open for 29% of the time, Pallas kernels for 0%

commit v1 on v0

--- a/solution.py
+++ b/solution.py
@@ -1,6 +1,8 @@
 import jax
 import jax.numpy as jnp
 from jax import lax
+from jax.experimental import pallas as pl
+from jax.experimental.pallas import tpu as pltpu
 from jax.sharding import PartitionSpec as P
 
 HEAD_DIM = 128
@@ -64,7 +66,7 @@
     return (probability.astype(jnp.bfloat16), score_grad)
 
 
-def local(queries, key_rows, value_rows, out_weight, grad_out, pair_offsets, far_head_offsets):
+def exchange_local(queries, key_rows, value_rows, out_weight, grad_out, pair_offsets, far_head_offsets):
     tokens = queries.shape[0]
     head_count = queries.shape[1] // HEAD_DIM
     factor = HEAD_DIM ** (-0.5)
@@ -167,7 +169,7 @@
     )
     head_grads = by_head(grad_attended.astype(jnp.bfloat16))
     row_delta = jnp.sum(head_grads.astype(jnp.float32) * head_out, axis=-1)
-    local_prob, local_dscore = score_grads(
+    _, local_dscore = score_grads(
         local_scores, row_max, row_sum, head_grads, segment_value, row_delta
     )
     query_grad = product(local_dscore, segment_key, "hij,hjd->hid") * factor
@@ -197,7 +199,7 @@
     pair_max = select(row_max, 2, pair_branch_shift)
     pair_sum = select(row_sum, 2, pair_branch_shift)
     pair_delta = select(row_delta, 2, pair_branch_shift)
-    pair_prob, pair_dscore = score_grads(
+    _, pair_dscore = score_grads(
         pair_scores, pair_max, pair_sum, pair_grad, pair_all_value, pair_delta
     )
     pair_dq = product(pair_dscore, pair_all_key, "hij,hjd->hid") * factor
@@ -252,6 +254,379 @@
     )
 
 
+def lanes(index):
+    return pl.ds(pl.multiple_of(index * HEAD_DIM, HEAD_DIM), HEAD_DIM)
+
+
+def rows(index, length):
+    return pl.ds(pl.multiple_of(index * length, length), length)
+
+
+def matmul(left, right, dims):
+    return lax.dot_general(left, right, (dims, ((), ())), preferred_element_type=jnp.float32)
+
+
+NN = ((1,), (0,))
+NT = ((1,), (1,))
+TN = ((0,), (0,))
+
+
+def call(body, out_shape, in_specs, scratch=(), flops=0):
+    vmem = pl.BlockSpec(memory_space=pltpu.VMEM)
+    return pl.pallas_call(
+        body,
+        out_shape=out_shape,
+        in_specs=in_specs,
+        out_specs=jax.tree.map(lambda _: vmem, out_shape),
+        scratch_shapes=list(scratch),
+        cost_estimate=pl.CostEstimate(flops=flops, bytes_accessed=0, transcendentals=0),
+        compiler_params=pltpu.CompilerParams(vmem_limit_bytes=40 * 2**20),
+    )
+
+
+def fast_local(plan, queries, key_rows, value_rows, out_weight, grad_out, pair_offsets, far_offsets):
+    tokens, heads, group, selected, dilation, head_groups = plan
+    factor = HEAD_DIM ** (-0.5)
+    width = heads * HEAD_DIM
+    model = out_weight.shape[1]
+    span = group * tokens
+    far_rows = tokens // dilation
+    far_span = span // dilation
+    bf16, f32 = jnp.bfloat16, jnp.float32
+    vmem = pl.BlockSpec(memory_space=pltpu.VMEM)
+    smem = pl.BlockSpec(memory_space=pltpu.SMEM)
+    dests = range(group)
+
+    def shape(extent, dtype=bf16):
+        return jax.ShapeDtypeStruct(extent, dtype)
+
+    def seq_rank():
+        return lax.rem(lax.axis_index("seq"), group)
+
+    def late_half():
+        return lax.axis_index("seq") // group
+
+    def my_head():
+        return lax.axis_index("head") * heads + seq_rank()
+
+    def swap(value, axis, mask):
+        return lax.ppermute(value, axis, [(s, s ^ mask) for s in range(lax.axis_size(axis))])
+
+    def swapped(blocks):
+        return [blocks[0]] + [swap(blocks[m], "seq", m) for m in dests if m]
+
+    grads = [grad_out] + [swap(grad_out, "head", m) for m in range(1, head_groups)]
+
+    def pack(fo, q, k, v, *refs):
+        outs, fars, wide = refs[:group], refs[group : 2 * group], refs[2 * group :]
+        rank = seq_rank()
+        base = lax.axis_index("head") * heads
+        for m in dests:
+            head = rank ^ m
+            key, value = k[:, lanes(head)], v[:, lanes(head)]
+            outs[m][:, :HEAD_DIM] = q[:, lanes(head)]
+            outs[m][:, HEAD_DIM : 2 * HEAD_DIM] = key
+            outs[m][:, 2 * HEAD_DIM :] = value
+            at = pl.ds(fo[base + head], far_rows, stride=dilation)
+            for slot, part in enumerate((key, value)):
+                wide[slot][...] = part.astype(f32)
+                cols = slice(slot * HEAD_DIM, (slot + 1) * HEAD_DIM)
+                fars[m][:, cols] = wide[slot][at, :].astype(bf16)
+
+    packed = call(
+        pack,
+        [shape((tokens, 3 * HEAD_DIM))] * group + [shape((far_rows, 2 * HEAD_DIM))] * group,
+        [smem, vmem, vmem, vmem],
+        [pltpu.VMEM((tokens, HEAD_DIM), f32)] * 2,
+        flops=10**7,
+    )(far_offsets, queries, key_rows, value_rows)
+    blocks = swapped(packed[:group])
+    early = [
+        lax.ppermute(packed[group + m], "seq", [(s, group + (s ^ m)) for s in range(group)])
+        for m in dests
+    ]
+
+    def project_grad(w, *refs):
+        parts, outs, (acc,) = refs[:head_groups], refs[head_groups:-1], refs[-1:]
+        me = lax.axis_index("head")
+        for m in range(head_groups):
+            cols = pl.ds(pl.multiple_of((me ^ m) * width, width), width)
+            term = matmul(parts[m][...], w[:, cols], NT)
+            if m == 0:
+                acc[...] = term
+            else:
+                acc[...] += term
+        rank = seq_rank()
+        for m in dests:
+            outs[m][...] = acc[:, lanes(rank ^ m)].astype(bf16)
+
+    grad_blocks = swapped(
+        call(
+            project_grad,
+            [shape((tokens, HEAD_DIM))] * group,
+            [vmem] * (1 + head_groups),
+            [pltpu.VMEM((tokens, width), f32)],
+            flops=10**8,
+        )(out_weight, *grads),
+    )
+
+    def branch_scores(query, key, mask):
+        return jnp.where(mask, matmul(query, key, NT) * factor, masked_score)
+
+    def causal(extent, shift=0):
+        row_ids = lax.broadcasted_iota(jnp.int32, extent, 0)
+        col_ids = lax.broadcasted_iota(jnp.int32, extent, 1)
+        return row_ids + shift >= col_ids
+
+    def far_mask():
+        extent = (far_span, 2 * far_span)
+        col_ids = lax.broadcasted_iota(jnp.int32, extent, 1)
+        open_cols = jnp.where(late_half() > 0, 0, far_span)
+        return causal(extent, far_span) & (col_ids >= open_cols)
+
+    def stats(scores, value):
+        top = jnp.max(scores, axis=-1, keepdims=True)
+        weights = jnp.exp(scores - top)
+        total = jnp.sum(weights, axis=-1, keepdims=True)
+        return top, total, matmul(weights.astype(bf16), value, NN)
+
+    def spread_lanes(column):
+        return jnp.broadcast_to(column, (column.shape[0], HEAD_DIM))
+
+    def forward(po, fo, *refs):
+        parts, fars = refs[:group], refs[group : 2 * group]
+        refs = refs[2 * group :]
+        outs, refs = refs[:group], refs[group:]
+        out_wide, lse, qb, kb, vb, early_kv, qf, kf, vf, top_all, sum_all = refs
+        rank = seq_rank()
+        for m in dests:
+            at = rows(rank ^ m, tokens)
+            for slot, (narrow, wide) in enumerate(((qb, qf), (kb, kf), (vb, vf))):
+                part = parts[m][:, slot * HEAD_DIM : (slot + 1) * HEAD_DIM]
+                narrow[at, :] = part
+                wide[at, :] = part.astype(f32)
+            early_kv[rows(rank ^ m, far_rows), :] = fars[m][...]
+        pair_at = pl.ds(po[my_head()], selected, stride=2)
+        far_at = pl.ds(fo[my_head()], far_span, stride=dilation)
+        mask = causal((selected, selected))
+        results = []
+        for first in range(0, span, selected):
+            at = pl.ds(first, selected)
+            results.append((at, stats(branch_scores(qb[at, :], kb[at, :], mask), vb[at, :])))
+        pick = lambda ref, at: ref[at, :].astype(bf16)
+        results.append(
+            (
+                pair_at,
+                stats(
+                    branch_scores(pick(qf, pair_at), pick(kf, pair_at), mask), pick(vf, pair_at)
+                ),
+            )
+        )
+        far_key = jnp.concatenate([early_kv[:, :HEAD_DIM], pick(kf, far_at)], axis=0)
+        far_value = jnp.concatenate([early_kv[:, HEAD_DIM:], pick(vf, far_at)], axis=0)
+        results.append(
+            (far_at, stats(branch_scores(pick(qf, far_at), far_key, far_mask()), far_value))
+        )
+        first_part = span // selected
+        for number, (at, (top, _, _)) in enumerate(results):
+            if number < first_part:
+                top_all[at, :] = spread_lanes(top)
+            else:
+                top_all[at, :] = jnp.maximum(top_all[at, :], spread_lanes(top))
+        for number, (at, (top, total, numerator)) in enumerate(results):
+            scale = jnp.exp(top - top_all[at, :])
+            if number < first_part:
+                sum_all[at, :] = total * scale
+                out_wide[at, :] = numerator * scale
+            else:
+                sum_all[at, :] += total * scale
+                out_wide[at, :] += numerator * scale
+        out_wide[...] = out_wide[...] / sum_all[...]
+        lse[...] = top_all[...] + jnp.log(sum_all[...])
+        for m in dests:
+            outs[m][...] = out_wide[rows(rank ^ m, tokens), :].astype(bf16)
+
+    wide = shape((span, HEAD_DIM), f32)
+    narrow = shape((span, HEAD_DIM))
+    scratch = pltpu.VMEM((span, HEAD_DIM), f32)
+    forward_out = call(
+        forward,
+        [shape((tokens, HEAD_DIM))] * group
+        + [wide, wide, narrow, narrow, narrow, shape((far_span, 2 * HEAD_DIM))],
+        [smem, smem] + [vmem] * (2 * group),
+        [scratch] * 5,
+        flops=3 * 10**8,
+    )(pair_offsets, far_offsets, *blocks, *early)
+    attended = swapped(forward_out[:group])
+
+    def backward(po, fo, out_wide, lse, qb, kb, vb, early_kv, *refs):
+        parts, refs = refs[:group], refs[group:]
+        outs, fars, refs = refs[:group], refs[group : 2 * group], refs[2 * group :]
+        qf, kf, vf, gf, gb, delta, dq, dk, dv, far_kv = refs
+        rank = seq_rank()
+        for m in dests:
+            at = rows(rank ^ m, tokens)
+            gb[at, :] = parts[m][...]
+            gf[at, :] = parts[m][...].astype(f32)
+        qf[...] = qb[...].astype(f32)
+        kf[...] = kb[...].astype(f32)
+        vf[...] = vb[...].astype(f32)
+        delta[...] = spread_lanes(jnp.sum(gf[...] * out_wide[...], axis=-1, keepdims=True))
+        pair_at = pl.ds(po[my_head()], selected, stride=2)
+        far_at = pl.ds(fo[my_head()], far_span, stride=dilation)
+
+        def grads_of(query, key, value, grad, row_lse, row_delta, mask):
+            scores = branch_scores(query, key, mask)
+            probability = jnp.exp(scores - row_lse[:, :1])
+            prob_grad = matmul(grad, value, NT)
+            score_grad = (probability * (prob_grad - row_delta[:, :1])).astype(bf16)
+            return (
+                matmul(score_grad, key, NN) * factor,
+                matmul(score_grad, query, TN) * factor,
+                matmul(probability.astype(bf16), grad, TN),
+            )
+
+        mask = causal((selected, selected))
+        for first in range(0, span, selected):
+            at = pl.ds(first, selected)
+            dq[at, :], dk[at, :], dv[at, :] = grads_of(
+                qb[at, :], kb[at, :], vb[at, :], gb[at, :], lse[at, :], delta[at, :], mask
+            )
+        pick = lambda ref, at: ref[at, :].astype(bf16)
+        pair_dq, pair_dk, pair_dv = grads_of(
+            pick(qf, pair_at),
+            pick(kf, pair_at),
+            pick(vf, pair_at),
+            pick(gf, pair_at),
+            lse[pair_at, :],
+            delta[pair_at, :],
+            mask,
+        )
+        dq[pair_at, :] += pair_dq
+        dk[pair_at, :] += pair_dk
+        dv[pair_at, :] += pair_dv
+        far_dq, far_dk, far_dv = grads_of(
+            pick(qf, far_at),
+            jnp.concatenate([early_kv[:, :HEAD_DIM], pick(kf, far_at)], axis=0),
+            jnp.concatenate([early_kv[:, HEAD_DIM:], pick(vf, far_at)], axis=0),
+            pick(gf, far_at),
+            lse[far_at, :],
+            delta[far_at, :],
+            far_mask(),
+        )
+        dq[far_at, :] += far_dq
+        dk[far_at, :] += far_dk[far_span:]
+        dv[far_at, :] += far_dv[far_span:]
+        far_kv[:, :HEAD_DIM] = far_dk[:far_span].astype(bf16)
+        far_kv[:, HEAD_DIM:] = far_dv[:far_span].astype(bf16)
+        for m in dests:
+            at = rows(rank ^ m, tokens)
+            for slot, ref in enumerate((dq, dk, dv)):
+                outs[m][:, slot * HEAD_DIM : (slot + 1) * HEAD_DIM] = ref[at, :].astype(bf16)
+            fars[m][...] = far_kv[rows(rank ^ m, far_rows), :]
+
+    backward_out = call(
+        backward,
+        [shape((tokens, 3 * HEAD_DIM))] * group + [shape((far_rows, 2 * HEAD_DIM))] * group,
+        [smem, smem] + [vmem] * (6 + group),
+        [scratch] * 4
+        + [pltpu.VMEM((span, HEAD_DIM), bf16)]
+        + [scratch] * 4
+        + [pltpu.VMEM((far_span, 2 * HEAD_DIM), bf16)],
+        flops=6 * 10**8,
+    )(pair_offsets, far_offsets, *forward_out[group:], *grad_blocks)
+    returned = swapped(backward_out[:group])
+    late = [
+        lax.ppermute(backward_out[group + m], "seq", [(group + s, s ^ m) for s in range(group)])
+        for m in dests
+    ]
+
+    half = model // 2
+
+    def columns(bit):
+        return pl.ds(pl.multiple_of(bit * half, half), half)
+
+    def my_half():
+        return lax.rem(lax.axis_index("head"), 2)
+
+    def project_theirs(w, *refs):
+        parts, (both, send) = refs[:group], refs[group:]
+        rank = seq_rank()
+        for m in dests:
+            both[:, lanes(rank ^ m)] = parts[m][...]
+        send[...] = matmul(both[...], w[:, columns(1 - my_half())], NN).astype(bf16)
+
+    both, theirs = call(
+        project_theirs,
+        [shape((tokens, width)), shape((tokens, half))],
+        [vmem] * (1 + group),
+        flops=10**8,
+    )(out_weight, *attended)
+    mate = swap(theirs, "head", 1)
+
+    def project_mine(w, both, mate, out):
+        mine = matmul(both[...], w[:, columns(my_half())], NN).astype(bf16).astype(f32)
+        out[...] = (mine + mate[...].astype(f32)).astype(bf16)
+
+    pair_sum = call(project_mine, shape((tokens, half)), [vmem] * 3, flops=10**8)(
+        out_weight, both, mate
+    )
+    across = swap(pair_sum, "head", 2)
+
+    def add(first, second, out):
+        out[...] = (first[...].astype(f32) + second[...].astype(f32)).astype(bf16)
+
+    total = call(add, shape((tokens, half)), [vmem] * 2, flops=10**6)(pair_sum, across)
+    other = swap(total, "head", 1)
+
+    def join(mine, theirs, out):
+        out[:, columns(my_half())] = mine[...]
+        out[:, columns(1 - my_half())] = theirs[...]
+
+    layer_out = call(join, shape((tokens, model)), [vmem] * 2, flops=10**6)(total, other)
+
+    def collect(fo, *refs):
+        parts, fars = refs[:group], refs[group : 2 * group]
+        outs, wide = refs[2 * group : 2 * group + 3], refs[2 * group + 3 :]
+        rank = seq_rank()
+        base = lax.axis_index("head") * heads
+        for m in dests:
+            head = rank ^ m
+            outs[0][:, lanes(head)] = parts[m][:, :HEAD_DIM]
+            at = pl.ds(fo[base + head], far_rows, stride=dilation)
+            for slot in range(2):
+                cols = slice((slot + 1) * HEAD_DIM, (slot + 2) * HEAD_DIM)
+                far_cols = slice(slot * HEAD_DIM, (slot + 1) * HEAD_DIM)
+                wide[slot][...] = parts[m][:, cols].astype(f32)
+                wide[slot][at, :] += fars[m][:, far_cols].astype(f32)
+                outs[1 + slot][:, lanes(head)] = wide[slot][...].astype(bf16)
+
+    gradients = call(
+        collect,
+        [shape((tokens, width))] * 3,
+        [smem] + [vmem] * (2 * group),
+        [pltpu.VMEM((tokens, HEAD_DIM), f32)] * 2,
+        flops=10**7,
+    )(far_offsets, *returned, *late)
+    return (layer_out, *gradients)
+
+
+def local(queries, key_rows, value_rows, out_weight, grad_out, pair_offsets, far_head_offsets):
+    tokens = queries.shape[0]
+    heads = queries.shape[1] // HEAD_DIM
+    seq_count = lax.axis_size("seq")
+    total = tokens * seq_count
+    selected = min(SPAN, total // 4)
+    group = 2 * selected // tokens
+    operands = (
+        queries, key_rows, value_rows, out_weight, grad_out, pair_offsets, far_head_offsets
+    )
+    if group == heads and seq_count == 2 * group and lax.axis_size("head") == 4:
+        plan = (tokens, heads, group, selected, total // selected, lax.axis_size("head"))
+        return fast_local(plan, *operands)
+    return exchange_local(*operands)
+
+
 def solution(mesh):
     placed = (
         P("seq", "head"),

time: 279 us -> 98.1 us (0.35)
  blocking collectives: 69.5 us -> 0 us
  local copies, waits for them, and re-layouts: 45.5 us -> 5.62 us
  other arithmetic: 29.3 us -> 0 us
  waiting for transfers between devices: 72 us -> 43.8 us
  matrix products: 27.8 us -> 0 us
  starting transfers between devices: 16.4 us -> 39.6 us
  between operations: 16.2 us -> 0.86 us
  Pallas kernels: 0 us -> 7.91 us
    all_gather x3 -> x0, blocking collectives: 69.5 us -> none  [the longest x1 31.1 us: local(): lax.all_gather(far_value, 'seq', axis=1, tiled=True)]
    reduce_scatter x2 -> x0, waiting for transfers between devices: 68.4 us -> none  [the longest x1 62.7 us: local(): lax.psum_scatter(gathered_dk, 'seq', scatter_dimension=1, tiled=True)]
    ppermute x14 -> x26, waiting for transfers between devices: 3.57 us -> 43.8 us  [the longest x4 24.5 us: fast_local(): lax.ppermute(backward_out[group + m], 'seq', [(group + s, s ^ m) for s in...]
    dot_general x20 -> x0, matrix products: 27.8 us -> none  [the longest x18 25.6 us: product(): jnp.einsum(pattern, left_side, right_side, preferred_element_type=jnp.flo...]
    ppermute x14 -> x26, starting transfers between devices: 16 us -> 39.6 us  [the longest x18 18.9 us: swap(): lax.ppermute(value, axis, [(s, s ^ mask) for s in range(lax.axis_size(axi...]
    reduce_sum x9 -> x0, other arithmetic: 15 us -> none  [the longest x6 12.6 us: select(): jnp.sum(jnp.where(lane_ids == chosen, shaped, jnp.zeros((), tensor.dtype)...]
    broadcast_in_dim x20 -> x0, local copies, waits for them, and re-layouts: 14.8 us -> none  [spread(): placed = jnp.where(lane_ids == chosen, jnp.expand_dims(entries, 2), filler)]
    select_n x14 -> x0, other arithmetic: 10.4 us -> none  [stacked(): lower = jnp.where(high, theirs, mine)]
  transfers between devices with their start and end apart: 17 -> 26, of which waited for: 6 -> 15; matrix products, arithmetic and copies ran while one was open for 29% -> 0% of each run, Pallas kernels for 0% -> 4%
where the time goes in v1:
time: 98.1 us; the launch traced here: 97.8 us
  waiting for transfers between devices  43.8 us (45%)
  starting transfers between devices  39.6 us (40%)
  Pallas kernels  7.91 us (8%)
  local copies, waits for them, and re-layouts  5.62 us (6%)
    ppermute x4, waiting for transfers between devices, fast_local(): lax.ppermute(backward_out[group + m], 'seq', [(group + s, s ^ m) for s in...  24.5 us
    ppermute x18, starting transfers between devices, swap(): lax.ppermute(value, axis, [(s, s ^ mask) for s in range(lax.axis_size(axi...  18.9 us
    ppermute x18, waiting for transfers between devices, swap(): lax.ppermute(value, axis, [(s, s ^ mask) for s in range(lax.axis_size(axi...  17.9 us
    ppermute x4, starting transfers between devices, fast_local(): lax.ppermute(packed[group + m], 'seq', [(s, group + (s ^ m)) for s in ran...  15.6 us
    unnamed x20, local copies, waits for them, and re-layouts  5.62 us
    ppermute x4, starting transfers between devices, fast_local(): lax.ppermute(backward_out[group + m], 'seq', [(group + s, s ^ m) for s in...  5.12 us
    pallas_call x1, Pallas kernels, fast_local(): call(backward, [shape((tokens, 3 * HEAD_DIM))] * group + [shape((far_rows...  1.98 us
  transfers between devices with their start and end apart: 26, of which 15 were waited for; matrix products, arithmetic and copies ran while one was open for 0% of the time, Pallas kernels for 4%

profile of v1, /device:TPU:0, one launch (start us, length us, event | category | flops | bytes accessed | tf_op | source)
XLA Modules:
  0.0 97.8 jit_solution(9513349754717214019)
XLA Ops:
  0.6 0.9 copy-done.3
  1.5 0.9 copy-done.4
  2.4 0.9 copy-done.5
  3.3 0.7 copy-done.6
  4.0 0.7 shard_map.102
  4.7 3.0 %collective-permute-start = (bf16[128,384]{1,0:T(8,128)(2,1)S(1)}, bf16[128,384]{1,0:T(8,128)(2,1)S(1)}, u32[]{:S(2)}, u32[]{:S(2)}) collective-permute-start(bf16[128,384]{1,0:T(8,128)(2,1)S(1)} %get-tuple-element.40), channel_id=1, source_target_pairs={{0,4},{4,0},{8,12},{12,8},{16,20},{20,16},{24,28},{28,24},{1,5},{5... | collective-permute-start | bytes 294920 | tf_op jit(solution)/shard_map/ppermute | solution.py:313
  7.7 1.6 %collective-permute-start.1 = (bf16[128,384]{1,0:T(8,128)(2,1)S(1)}, bf16[128,384]{1,0:T(8,128)(2,1)S(1)}, u32[]{:S(2)}, u32[]{:S(2)}) collective-permute-start(bf16[128,384]{1,0:T(8,128)(2,1)S(1)} %get-tuple-element.41), channel_id=1, source_target_pairs={{0,8},{4,12},{8,0},{12,4},{16,24},{20,28},{24,16},{28,20},{1,9},{5... | collective-permute-start | bytes 294920 | tf_op jit(solution)/shard_map/ppermute | solution.py:313
  9.3 4.9 %collective-permute-start.3 = (bf16[32,256]{1,0:T(8,128)(2,1)S(1)}, bf16[32,256]{1,0:T(8,128)(2,1)S(1)}, u32[]{:S(2)}, u32[]{:S(2)}) collective-permute-start(bf16[32,256]{1,0:T(8,128)(2,1)S(1)} %get-tuple-element.43), channel_id=1, source_target_pairs={{0,16},{4,20},{8,24},{12,28},{1,17},{5,21},{9,25},{13,29},{2,18},{... | collective-permute-start | bytes 49160 | tf_op jit(solution)/shard_map/ppermute | solution.py:345
  14.2 2.2 %collective-permute-start.4 = (bf16[32,256]{1,0:T(8,128)(2,1)S(1)}, bf16[32,256]{1,0:T(8,128)(2,1)S(1)}, u32[]{:S(2)}, u32[]{:S(2)}) collective-permute-start(bf16[32,256]{1,0:T(8,128)(2,1)S(1)} %get-tuple-element.44), channel_id=1, source_target_pairs={{0,20},{4,16},{8,28},{12,24},{1,21},{5,17},{9,29},{13,25},{2,22},{... | collective-permute-start | bytes 49160 | tf_op jit(solution)/shard_map/ppermute | solution.py:345
  16.4 5.6 %collective-permute-start.5 = (bf16[32,256]{1,0:T(8,128)(2,1)S(1)}, bf16[32,256]{1,0:T(8,128)(2,1)S(1)}, u32[]{:S(2)}, u32[]{:S(2)}) collective-permute-start(bf16[32,256]{1,0:T(8,128)(2,1)S(1)} %get-tuple-element.45), channel_id=1, source_target_pairs={{0,24},{4,28},{8,16},{12,20},{1,25},{5,29},{9,17},{13,21},{2,26},{... | collective-permute-start | bytes 49160 | tf_op jit(solution)/shard_map/ppermute | solution.py:345
  22.0 2.9 %collective-permute-start.6 = (bf16[32,256]{1,0:T(8,128)(2,1)S(1)}, bf16[32,256]{1,0:T(8,128)(2,1)S(1)}, u32[]{:S(2)}, u32[]{:S(2)}) collective-permute-start(bf16[32,256]{1,0:T(8,128)(2,1)S(1)} %get-tuple-element.46), channel_id=1, source_target_pairs={{0,28},{4,24},{8,20},{12,16},{1,29},{5,25},{9,21},{13,17},{2,30},{... | collective-permute-start | bytes 49160 | tf_op jit(solution)/shard_map/ppermute | solution.py:345
  24.9 1.4 %collective-permute-done.6.refs_7_ = bf16[32,256]{1,0:T(8,128)(2,1)S(1)} collective-permute-done((bf16[32,256]{1,0:T(8,128)(2,1)S(1)}, bf16[32,256]{1,0:T(8,128)(2,1)S(1)}, u32[]{:S(2)}, u32[]{:S(2)}) %collective-permute-start.6) | collective-permute-done | bytes 16416 | tf_op jit(solution)/shard_map/ppermute | solution.py:345
  26.4 0.6 copy-done.8
  27.0 1.5 %shard_map.103 = (bf16[128,128]{1,0:T(8,128)(2,1)S(1)}, bf16[128,128]{1,0:T(8,128)(2,1)S(1)}, bf16[128,128]{1,0:T(8,128)(2,1)S(1)}, bf16[128,128]{1,0:T(8,128)(2...) custom-call(s32[16]{0:T(128)S(1)} %copy-done.8, ...), custom_call_target="tpu_custom_call" | custom-call | flops 300000000 | tf_op jit(solution)/shard_map/pallas_call | solution.py:452
  28.5 0.6 collective-permute-start.7
  29.2 2.9 %collective-permute-start.9 = (bf16[128,128]{1,0:T(8,128)(2,1)S(1)}, bf16[128,128]{1,0:T(8,128)(2,1)S(1)}, u32[]{:S(2)}, u32[]{:S(2)}) collective-permute-start(bf16[128,128]{1,0:T(8,128)(2,1)S(1)} %get-tuple-element.50), channel_id=1, source_target_pairs={{0,12},{4,8},{8,4},{12,0},{16,28},{20,24},{24,20},{28,16},{1,13},{... | collective-permute-start | bytes 98312 | tf_op jit(solution)/shard_map/ppermute | solution.py:313
  32.1 0.4 collective-permute-done.7.refs_1_
  32.5 0.6 collective-permute-done.8.refs_2_
  33.1 1.3 %collective-permute-done.9.refs_3_ = bf16[128,128]{1,0:T(8,128)(2,1)S(1)} collective-permute-done((bf16[128,128]{1,0:T(8,128)(2,1)S(1)}, bf16[128,128]{1,0:T(8,128)(2,1)S(1)}, u32[]{:S(2)}, u32[]{:S(2)}) %collective-permute-start.9) | collective-permute-done | bytes 32800 | tf_op jit(solution)/shard_map/ppermute | solution.py:313
  34.3 1.6 %copy-done = bf16[512,2048]{1,0:T(8,128)(2,1)S(1)} copy-done((bf16[512,2048]{1,0:T(8,128)(2,1)S(1)}, bf16[512,2048]{1,0:T(8,128)(2,1)}, u32[]{:S(2)}) %copy-start) | copy-done | bytes 2097176
  36.3 1.5 %collective-permute-done.10.mate = bf16[128,1024]{1,0:T(8,128)(2,1)S(1)} collective-permute-done((bf16[128,1024]{1,0:T(8,128)(2,1)S(1)}, bf16[128,1024]{1,0:T(8,128)(2,1)S(1)}, u32[]{:S(2)}, u32[]{:S(2)}) %collective-permute-start.10) | collective-permute-done | bytes 262176 | tf_op jit(solution)/shard_map/ppermute | solution.py:313
  38.2 1.6 %collective-permute-start.11 = (bf16[128,1024]{1,0:T(8,128)(2,1)S(1)}, bf16[128,1024]{1,0:T(8,128)(2,1)S(1)}, u32[]{:S(2)}, u32[]{:S(2)}) collective-permute-start(bf16[128,1024]{1,0:T(8,128)(2,1)S(1)} %shard_map.105.first), channel_id=1, source_target_pairs={{0,2},{1,3},{2,0},{3,1},{4,6},{5,7},{6,4},{7,5},{8,10},{9,11},{10,... | collective-permute-start | bytes 786440 | tf_op jit(solution)/shard_map/ppermute | solution.py:313
  39.8 0.5 collective-permute-start.14
  40.3 1.4 %collective-permute-start.15 = (bf16[128,512]{1,0:T(8,128)(2,1)S(1)}, bf16[128,512]{1,0:T(8,128)(2,1)S(1)}, u32[]{:S(2)}, u32[]{:S(2)}) collective-permute-start(bf16[128,512]{1,0:T(8,128)(2,1)S(1)} %copy-done.2), channel_id=1, source_target_pairs={{0,3},{1,2},{2,1},{3,0},{4,7},{5,6},{6,5},{7,4},{8,11},{9,10},{10,... | collective-permute-start | bytes 393224 | tf_op jit(solution)/shard_map/ppermute | solution.py:313
  41.7 5.8 %collective-permute-done.11.second = bf16[128,1024]{1,0:T(8,128)(2,1)S(1)} collective-permute-done((bf16[128,1024]{1,0:T(8,128)(2,1)S(1)}, bf16[128,1024]{1,0:T(8,128)(2,1)S(1)}, u32[]{:S(2)}, u32[]{:S(2)}) %collective-permute-start.11) | collective-permute-done | bytes 262176 | tf_op jit(solution)/shard_map/ppermute | solution.py:313
  47.6 2.7 %collective-permute-done.14.refs_2_ = bf16[128,512]{1,0:T(8,128)(2,1)S(1)} collective-permute-done((bf16[128,512]{1,0:T(8,128)(2,1)S(1)}, bf16[128,512]{1,0:T(8,128)(2,1)S(1)}, u32[]{:S(2)}, u32[]{:S(2)}) %collective-permute-start.14) | collective-permute-done | bytes 131104 | tf_op jit(solution)/shard_map/ppermute | solution.py:313
  50.3 1.1 %collective-permute-done.15.refs_3_ = bf16[128,512]{1,0:T(8,128)(2,1)S(1)} collective-permute-done((bf16[128,512]{1,0:T(8,128)(2,1)S(1)}, bf16[128,512]{1,0:T(8,128)(2,1)S(1)}, u32[]{:S(2)}, u32[]{:S(2)}) %collective-permute-start.15) | collective-permute-done | bytes 131104 | tf_op jit(solution)/shard_map/ppermute | solution.py:313
  51.4 0.9 shard_map.108
  52.3 1.2 %collective-permute-start.16 = (bf16[128,128]{1,0:T(8,128)(2,1)S(1)}, bf16[128,128]{1,0:T(8,128)(2,1)S(1)}, u32[]{:S(2)}, u32[]{:S(2)}) collective-permute-start(bf16[128,128]{1,0:T(8,128)(2,1)S(1)} %get-tuple-element.60), channel_id=1, source_target_pairs={{0,4},{4,0},{8,12},{12,8},{16,20},{20,16},{24,28},{28,24},{1,5},{5... | collective-permute-start | bytes 98312 | tf_op jit(solution)/shard_map/ppermute | solution.py:313
  53.4 2.0 %collective-permute-start.17 = (bf16[128,128]{1,0:T(8,128)(2,1)S(1)}, bf16[128,128]{1,0:T(8,128)(2,1)S(1)}, u32[]{:S(2)}, u32[]{:S(2)}) collective-permute-start(bf16[128,128]{1,0:T(8,128)(2,1)S(1)} %get-tuple-element.61), channel_id=1, source_target_pairs={{0,8},{4,12},{8,0},{12,4},{16,24},{20,28},{24,16},{28,20},{1,9},{5... | collective-permute-start | bytes 98312 | tf_op jit(solution)/shard_map/ppermute | solution.py:313
  55.5 0.3 collective-permute-start.18
  55.8 0.5 collective-permute-done.16.refs_1_
  56.3 1.1 %collective-permute-done.17.refs_2_ = bf16[128,128]{1,0:T(8,128)(2,1)S(1)} collective-permute-done((bf16[128,128]{1,0:T(8,128)(2,1)S(1)}, bf16[128,128]{1,0:T(8,128)(2,1)S(1)}, u32[]{:S(2)}, u32[]{:S(2)}) %collective-permute-start.17) | collective-permute-done | bytes 32800 | tf_op jit(solution)/shard_map/ppermute | solution.py:313
  57.4 2.9 %collective-permute-done.18.refs_3_ = bf16[128,128]{1,0:T(8,128)(2,1)S(1)} collective-permute-done((bf16[128,128]{1,0:T(8,128)(2,1)S(1)}, bf16[128,128]{1,0:T(8,128)(2,1)S(1)}, u32[]{:S(2)}, u32[]{:S(2)}) %collective-permute-start.18) | collective-permute-done | bytes 32800 | tf_op jit(solution)/shard_map/ppermute | solution.py:313
  60.3 2.0 %shard_map.109 = (bf16[128,384]{1,0:T(8,128)(2,1)S(1)}, bf16[128,384]{1,0:T(8,128)(2,1)S(1)}, bf16[128,384]{1,0:T(8,128)(2,1)S(1)}, bf16[128,384]{1,0:T(8,128)(2...) custom-call(s32[16]{0:T(128)S(1)} %copy-done.9, ...), custom_call_target="tpu_custom_call" | custom-call | flops 600000000 | tf_op jit(solution)/shard_map/pallas_call | solution.py:528
  62.3 0.6 collective-permute-start.19
  62.9 0.5 collective-permute-start.20
  63.4 2.5 %collective-permute-start.21 = (bf16[128,384]{1,0:T(8,128)(2,1)S(1)}, bf16[128,384]{1,0:T(8,128)(2,1)S(1)}, u32[]{:S(2)}, u32[]{:S(2)}) collective-permute-start(bf16[128,384]{1,0:T(8,128)(2,1)S(1)} %get-tuple-element.66), channel_id=1, source_target_pairs={{0,12},{4,8},{8,4},{12,0},{16,28},{20,24},{24,20},{28,16},{1,13},{... | collective-permute-start | bytes 294920 | tf_op jit(solution)/shard_map/ppermute | solution.py:313
  65.8 1.3 %collective-permute-start.22 = (bf16[32,256]{1,0:T(8,128)(2,1)S(1)}, bf16[32,256]{1,0:T(8,128)(2,1)S(1)}, u32[]{:S(2)}, u32[]{:S(2)}) collective-permute-start(bf16[32,256]{1,0:T(8,128)(2,1)S(1)} %get-tuple-element.67), channel_id=1, source_target_pairs={{16,0},{20,4},{24,8},{28,12},{17,1},{21,5},{25,9},{29,13},{18,2},{... | collective-permute-start | bytes 49160 | tf_op jit(solution)/shard_map/ppermute | solution.py:540
  67.1 5.2 %collective-permute-done.22.refs_4_ = bf16[32,256]{1,0:T(8,128)(2,1)S(1)} collective-permute-done((bf16[32,256]{1,0:T(8,128)(2,1)S(1)}, bf16[32,256]{1,0:T(8,128)(2,1)S(1)}, u32[]{:S(2)}, u32[]{:S(2)}) %collective-permute-start.22) | collective-permute-done | bytes 16416 | tf_op jit(solution)/shard_map/ppermute | solution.py:540
  72.4 1.3 %collective-permute-start.23 = (bf16[32,256]{1,0:T(8,128)(2,1)S(1)}, bf16[32,256]{1,0:T(8,128)(2,1)S(1)}, u32[]{:S(2)}, u32[]{:S(2)}) collective-permute-start(bf16[32,256]{1,0:T(8,128)(2,1)S(1)} %get-tuple-element.68), channel_id=1, source_target_pairs={{16,4},{20,0},{24,12},{28,8},{17,5},{21,1},{25,13},{29,9},{18,6},{... | collective-permute-start | bytes 49160 | tf_op jit(solution)/shard_map/ppermute | solution.py:540
  73.7 6.1 %collective-permute-done.23.refs_5_ = bf16[32,256]{1,0:T(8,128)(2,1)S(1)} collective-permute-done((bf16[32,256]{1,0:T(8,128)(2,1)S(1)}, bf16[32,256]{1,0:T(8,128)(2,1)S(1)}, u32[]{:S(2)}, u32[]{:S(2)}) %collective-permute-start.23) | collective-permute-done | bytes 16416 | tf_op jit(solution)/shard_map/ppermute | solution.py:540
  79.8 1.3 %collective-permute-start.24 = (bf16[32,256]{1,0:T(8,128)(2,1)S(1)}, bf16[32,256]{1,0:T(8,128)(2,1)S(1)}, u32[]{:S(2)}, u32[]{:S(2)}) collective-permute-start(bf16[32,256]{1,0:T(8,128)(2,1)S(1)} %get-tuple-element.69), channel_id=1, source_target_pairs={{16,8},{20,12},{24,0},{28,4},{17,9},{21,13},{25,1},{29,5},{18,10},... | collective-permute-start | bytes 49160 | tf_op jit(solution)/shard_map/ppermute | solution.py:540
  81.1 6.1 %collective-permute-done.24.refs_6_ = bf16[32,256]{1,0:T(8,128)(2,1)S(1)} collective-permute-done((bf16[32,256]{1,0:T(8,128)(2,1)S(1)}, bf16[32,256]{1,0:T(8,128)(2,1)S(1)}, u32[]{:S(2)}, u32[]{:S(2)}) %collective-permute-start.24) | collective-permute-done | bytes 16416 | tf_op jit(solution)/shard_map/ppermute | solution.py:540
  87.2 1.3 %collective-permute-start.25 = (bf16[32,256]{1,0:T(8,128)(2,1)S(1)}, bf16[32,256]{1,0:T(8,128)(2,1)S(1)}, u32[]{:S(2)}, u32[]{:S(2)}) collective-permute-start(bf16[32,256]{1,0:T(8,128)(2,1)S(1)} %get-tuple-element.70), channel_id=1, source_target_pairs={{16,12},{20,8},{24,4},{28,0},{17,13},{21,9},{25,5},{29,1},{18,14},... | collective-permute-start | bytes 49160 | tf_op jit(solution)/shard_map/ppermute | solution.py:540
  88.5 7.0 %collective-permute-done.25.refs_7_ = bf16[32,256]{1,0:T(8,128)(2,1)S(1)} collective-permute-done((bf16[32,256]{1,0:T(8,128)(2,1)S(1)}, bf16[32,256]{1,0:T(8,128)(2,1)S(1)}, u32[]{:S(2)}, u32[]{:S(2)}) %collective-permute-start.25) | collective-permute-done | bytes 16416 | tf_op jit(solution)/shard_map/ppermute | solution.py:540
  95.5 1.4 %shard_map.110 = (bf16[128,512]{1,0:T(8,128)(2,1)}, bf16[128,512]{1,0:T(8,128)(2,1)}, bf16[128,512]{1,0:T(8,128)(2,1)}) custom-call(s32[16]{0:T(128)S(1)} %copy-done.7, bf16[128,384]{1,0:T(8,128)(2,1)S(1)} %get-tuple-element.63.refs_0_, bf16[128,384]{1,0:T(8,128)(2,1)S(1)} %collective-permute-done.19.refs_1_, ...), custom_call_target="tpu_custom_call" | custom-call | flops 10000000 | tf_op jit(solution)/shard_map/pallas_call | solution.py:604
  96.9 0.8 shard_map.107
  (33 shorter events, 0.9 us)
Async XLA Ops:
  0.6 0.9 copy-start.3
  1.5 0.9 copy-start.4
  2.4 0.9 copy-start.5
  3.3 0.7 copy-start.6
  4.7 21.7 %collective-permute-start = (bf16[128,384]{1,0:T(8,128)(2,1)S(1)}, bf16[128,384]{1,0:T(8,128)(2,1)S(1)}, u32[]{:S(2)}, u32[]{:S(2)}) collective-permute-start(bf16[128,384]{1,0:T(8,128)(2,1)S(1)} %get-tuple-element.40), channel_id=1, source_target_pairs={{0,4},{4,0},{8,12},{12,8},{16,20},{20,16},{24,28},{28,24},{1,5},{5... | collective-permute-start | bytes 294920 | tf_op jit(solution)/shard_map/ppermute | solution.py:313
  7.7 18.6 %collective-permute-start.1 = (bf16[128,384]{1,0:T(8,128)(2,1)S(1)}, bf16[128,384]{1,0:T(8,128)(2,1)S(1)}, u32[]{:S(2)}, u32[]{:S(2)}) collective-permute-start(bf16[128,384]{1,0:T(8,128)(2,1)S(1)} %get-tuple-element.41), channel_id=1, source_target_pairs={{0,8},{4,12},{8,0},{12,4},{16,24},{20,28},{24,16},{28,20},{1,9},{5... | collective-permute-start | bytes 294920 | tf_op jit(solution)/shard_map/ppermute | solution.py:313
  9.3 17.1 %collective-permute-start.2 = (bf16[128,384]{1,0:T(8,128)(2,1)S(1)}, bf16[128,384]{1,0:T(8,128)(2,1)S(1)}, u32[]{:S(2)}, u32[]{:S(2)}) collective-permute-start(bf16[128,384]{1,0:T(8,128)(2,1)S(1)} %get-tuple-element.42), channel_id=1, source_target_pairs={{0,12},{4,8},{8,4},{12,0},{16,28},{20,24},{24,20},{28,16},{1,13},{... | collective-permute-start | bytes 294920 | tf_op jit(solution)/shard_map/ppermute | solution.py:313
  9.3 7.1 %collective-permute-start.3 = (bf16[32,256]{1,0:T(8,128)(2,1)S(1)}, bf16[32,256]{1,0:T(8,128)(2,1)S(1)}, u32[]{:S(2)}, u32[]{:S(2)}) collective-permute-start(bf16[32,256]{1,0:T(8,128)(2,1)S(1)} %get-tuple-element.43), channel_id=1, source_target_pairs={{0,16},{4,20},{8,24},{12,28},{1,17},{5,21},{9,25},{13,29},{2,18},{... | collective-permute-start | bytes 49160 | tf_op jit(solution)/shard_map/ppermute | solution.py:345
  14.2 7.9 %collective-permute-start.4 = (bf16[32,256]{1,0:T(8,128)(2,1)S(1)}, bf16[32,256]{1,0:T(8,128)(2,1)S(1)}, u32[]{:S(2)}, u32[]{:S(2)}) collective-permute-start(bf16[32,256]{1,0:T(8,128)(2,1)S(1)} %get-tuple-element.44), channel_id=1, source_target_pairs={{0,20},{4,16},{8,28},{12,24},{1,21},{5,17},{9,29},{13,25},{2,22},{... | collective-permute-start | bytes 49160 | tf_op jit(solution)/shard_map/ppermute | solution.py:345
  16.4 8.5 %collective-permute-start.5 = (bf16[32,256]{1,0:T(8,128)(2,1)S(1)}, bf16[32,256]{1,0:T(8,128)(2,1)S(1)}, u32[]{:S(2)}, u32[]{:S(2)}) collective-permute-start(bf16[32,256]{1,0:T(8,128)(2,1)S(1)} %get-tuple-element.45), channel_id=1, source_target_pairs={{0,24},{4,28},{8,16},{12,20},{1,25},{5,29},{9,17},{13,21},{2,26},{... | collective-permute-start | bytes 49160 | tf_op jit(solution)/shard_map/ppermute | solution.py:345
  22.0 4.3 %collective-permute-start.6 = (bf16[32,256]{1,0:T(8,128)(2,1)S(1)}, bf16[32,256]{1,0:T(8,128)(2,1)S(1)}, u32[]{:S(2)}, u32[]{:S(2)}) collective-permute-start(bf16[32,256]{1,0:T(8,128)(2,1)S(1)} %get-tuple-element.46), channel_id=1, source_target_pairs={{0,28},{4,24},{8,20},{12,16},{1,29},{5,25},{9,21},{13,17},{2,30},{... | collective-permute-start | bytes 49160 | tf_op jit(solution)/shard_map/ppermute | solution.py:345
  26.3 0.7 copy-start.8
  28.5 4.0 %collective-permute-start.7 = (bf16[128,128]{1,0:T(8,128)(2,1)S(1)}, bf16[128,128]{1,0:T(8,128)(2,1)S(1)}, u32[]{:S(2)}, u32[]{:S(2)}) collective-permute-start(bf16[128,128]{1,0:T(8,128)(2,1)S(1)} %get-tuple-element.48), channel_id=1, source_target_pairs={{0,4},{4,0},{8,12},{12,8},{16,20},{20,16},{24,28},{28,24},{1,5},{5... | collective-permute-start | bytes 98312 | tf_op jit(solution)/shard_map/ppermute | solution.py:313
  29.2 3.9 %collective-permute-start.8 = (bf16[128,128]{1,0:T(8,128)(2,1)S(1)}, bf16[128,128]{1,0:T(8,128)(2,1)S(1)}, u32[]{:S(2)}, u32[]{:S(2)}) collective-permute-start(bf16[128,128]{1,0:T(8,128)(2,1)S(1)} %get-tuple-element.49), channel_id=1, source_target_pairs={{0,8},{4,12},{8,0},{12,4},{16,24},{20,28},{24,16},{28,20},{1,9},{5... | collective-permute-start | bytes 98312 | tf_op jit(solution)/shard_map/ppermute | solution.py:313
  29.2 5.2 %collective-permute-start.9 = (bf16[128,128]{1,0:T(8,128)(2,1)S(1)}, bf16[128,128]{1,0:T(8,128)(2,1)S(1)}, u32[]{:S(2)}, u32[]{:S(2)}) collective-permute-start(bf16[128,128]{1,0:T(8,128)(2,1)S(1)} %get-tuple-element.50), channel_id=1, source_target_pairs={{0,12},{4,8},{8,4},{12,0},{16,28},{20,24},{24,20},{28,16},{1,13},{... | collective-permute-start | bytes 98312 | tf_op jit(solution)/shard_map/ppermute | solution.py:313
  34.3 1.6 %copy-start = (bf16[512,2048]{1,0:T(8,128)(2,1)S(1)}, bf16[512,2048]{1,0:T(8,128)(2,1)}, u32[]{:S(2)}) copy-start(bf16[512,2048]{1,0:T(8,128)(2,1)} %w.5) | copy-start | bytes 6291460
  35.9 1.9 %copy-start.1 = (bf16[512,2048]{1,0:T(8,128)(2,1)S(1)}, bf16[512,2048]{1,0:T(8,128)(2,1)}, u32[]{:S(2)}) copy-start(bf16[512,2048]{1,0:T(8,128)(2,1)} %w.5) | copy-start | bytes 6291460
  35.9 3.9 %copy-start.2 = (bf16[128,512]{1,0:T(8,128)(2,1)S(1)}, bf16[128,512]{1,0:T(8,128)(2,1)}, u32[]{:S(2)}) copy-start(bf16[128,512]{1,0:T(8,128)(2,1)} %refs_0_.1) | copy-start | bytes 393220
  36.3 1.6 %collective-permute-start.10 = (bf16[128,1024]{1,0:T(8,128)(2,1)S(1)}, bf16[128,1024]{1,0:T(8,128)(2,1)S(1)}, u32[]{:S(2)}, u32[]{:S(2)}) collective-permute-start(bf16[128,1024]{1,0:T(8,128)(2,1)S(1)} %get-tuple-element.52), channel_id=1, source_target_pairs={{0,1},{1,0},{2,3},{3,2},{4,5},{5,4},{6,7},{7,6},{8,9},{9,8},{10,11... | collective-permute-start | bytes 786440 | tf_op jit(solution)/shard_map/ppermute | solution.py:313
  38.2 22.1 %copy-start.7 = (s32[16]{0:T(128)S(1)}, s32[16]{0:T(128)}, u32[]{:S(2)}) copy-start(s32[16]{0:T(128)} %fo.7) | copy-start | bytes 196
  38.2 22.1 %copy-start.9 = (s32[16]{0:T(128)S(1)}, s32[16]{0:T(128)}, u32[]{:S(2)}) copy-start(s32[16]{0:T(128)} %po.3) | copy-start | bytes 196
  38.2 9.2 %collective-permute-start.11 = (bf16[128,1024]{1,0:T(8,128)(2,1)S(1)}, bf16[128,1024]{1,0:T(8,128)(2,1)S(1)}, u32[]{:S(2)}, u32[]{:S(2)}) collective-permute-start(bf16[128,1024]{1,0:T(8,128)(2,1)S(1)} %shard_map.105.first), channel_id=1, source_target_pairs={{0,2},{1,3},{2,0},{3,1},{4,6},{5,7},{6,4},{7,5},{8,10},{9,11},{10,... | collective-permute-start | bytes 786440 | tf_op jit(solution)/shard_map/ppermute | solution.py:313
  39.8 7.8 %collective-permute-start.13 = (bf16[128,512]{1,0:T(8,128)(2,1)S(1)}, bf16[128,512]{1,0:T(8,128)(2,1)S(1)}, u32[]{:S(2)}, u32[]{:S(2)}) collective-permute-start(bf16[128,512]{1,0:T(8,128)(2,1)S(1)} %copy-done.2), channel_id=1, source_target_pairs={{0,1},{1,0},{2,3},{3,2},{4,5},{5,4},{6,7},{7,6},{8,9},{9,8},{10,11... | collective-permute-start | bytes 393224 | tf_op jit(solution)/shard_map/ppermute | solution.py:313
  39.8 10.5 %collective-permute-start.14 = (bf16[128,512]{1,0:T(8,128)(2,1)S(1)}, bf16[128,512]{1,0:T(8,128)(2,1)S(1)}, u32[]{:S(2)}, u32[]{:S(2)}) collective-permute-start(bf16[128,512]{1,0:T(8,128)(2,1)S(1)} %copy-done.2), channel_id=1, source_target_pairs={{0,2},{1,3},{2,0},{3,1},{4,6},{5,7},{6,4},{7,5},{8,10},{9,11},{10,... | collective-permute-start | bytes 393224 | tf_op jit(solution)/shard_map/ppermute | solution.py:313
  40.3 11.1 %collective-permute-start.15 = (bf16[128,512]{1,0:T(8,128)(2,1)S(1)}, bf16[128,512]{1,0:T(8,128)(2,1)S(1)}, u32[]{:S(2)}, u32[]{:S(2)}) collective-permute-start(bf16[128,512]{1,0:T(8,128)(2,1)S(1)} %copy-done.2), channel_id=1, source_target_pairs={{0,3},{1,2},{2,1},{3,0},{4,7},{5,6},{6,5},{7,4},{8,11},{9,10},{10,... | collective-permute-start | bytes 393224 | tf_op jit(solution)/shard_map/ppermute | solution.py:313
  47.5 49.4 %collective-permute-start.12 = (bf16[128,1024]{1,0:T(8,128)(2,1)S(1)}, bf16[128,1024]{1,0:T(8,128)(2,1)S(1)}, u32[]{:S(2)}, u32[]{:S(2)}) collective-permute-start(bf16[128,1024]{1,0:T(8,128)(2,1)S(1)} %shard_map.106.mine), channel_id=1, source_target_pairs={{0,1},{1,0},{2,3},{3,2},{4,5},{5,4},{6,7},{7,6},{8,9},{9,8},{10,11... | collective-permute-start | bytes 786440 | tf_op jit(solution)/shard_map/ppermute | solution.py:313
  52.3 4.0 %collective-permute-start.16 = (bf16[128,128]{1,0:T(8,128)(2,1)S(1)}, bf16[128,128]{1,0:T(8,128)(2,1)S(1)}, u32[]{:S(2)}, u32[]{:S(2)}) collective-permute-start(bf16[128,128]{1,0:T(8,128)(2,1)S(1)} %get-tuple-element.60), channel_id=1, source_target_pairs={{0,4},{4,0},{8,12},{12,8},{16,20},{20,16},{24,28},{28,24},{1,5},{5... | collective-permute-start | bytes 98312 | tf_op jit(solution)/shard_map/ppermute | solution.py:313
  53.4 4.0 %collective-permute-start.17 = (bf16[128,128]{1,0:T(8,128)(2,1)S(1)}, bf16[128,128]{1,0:T(8,128)(2,1)S(1)}, u32[]{:S(2)}, u32[]{:S(2)}) collective-permute-start(bf16[128,128]{1,0:T(8,128)(2,1)S(1)} %get-tuple-element.61), channel_id=1, source_target_pairs={{0,8},{4,12},{8,0},{12,4},{16,24},{20,28},{24,16},{28,20},{1,9},{5... | collective-permute-start | bytes 98312 | tf_op jit(solution)/shard_map/ppermute | solution.py:313
  55.5 4.8 %collective-permute-start.18 = (bf16[128,128]{1,0:T(8,128)(2,1)S(1)}, bf16[128,128]{1,0:T(8,128)(2,1)S(1)}, u32[]{:S(2)}, u32[]{:S(2)}) collective-permute-start(bf16[128,128]{1,0:T(8,128)(2,1)S(1)} %get-tuple-element.62), channel_id=1, source_target_pairs={{0,12},{4,8},{8,4},{12,0},{16,28},{20,24},{24,20},{28,16},{1,13},{... | collective-permute-start | bytes 98312 | tf_op jit(solution)/shard_map/ppermute | solution.py:313
  62.3 33.2 %collective-permute-start.19 = (bf16[128,384]{1,0:T(8,128)(2,1)S(1)}, bf16[128,384]{1,0:T(8,128)(2,1)S(1)}, u32[]{:S(2)}, u32[]{:S(2)}) collective-permute-start(bf16[128,384]{1,0:T(8,128)(2,1)S(1)} %get-tuple-element.64), channel_id=1, source_target_pairs={{0,4},{4,0},{8,12},{12,8},{16,20},{20,16},{24,28},{28,24},{1,5},{5... | collective-permute-start | bytes 294920 | tf_op jit(solution)/shard_map/ppermute | solution.py:313
  62.9 32.6 %collective-permute-start.20 = (bf16[128,384]{1,0:T(8,128)(2,1)S(1)}, bf16[128,384]{1,0:T(8,128)(2,1)S(1)}, u32[]{:S(2)}, u32[]{:S(2)}) collective-permute-start(bf16[128,384]{1,0:T(8,128)(2,1)S(1)} %get-tuple-element.65), channel_id=1, source_target_pairs={{0,8},{4,12},{8,0},{12,4},{16,24},{20,28},{24,16},{28,20},{1,9},{5... | collective-permute-start | bytes 294920 | tf_op jit(solution)/shard_map/ppermute | solution.py:313
  63.4 32.2 %collective-permute-start.21 = (bf16[128,384]{1,0:T(8,128)(2,1)S(1)}, bf16[128,384]{1,0:T(8,128)(2,1)S(1)}, u32[]{:S(2)}, u32[]{:S(2)}) collective-permute-start(bf16[128,384]{1,0:T(8,128)(2,1)S(1)} %get-tuple-element.66), channel_id=1, source_target_pairs={{0,12},{4,8},{8,4},{12,0},{16,28},{20,24},{24,20},{28,16},{1,13},{... | collective-permute-start | bytes 294920 | tf_op jit(solution)/shard_map/ppermute | solution.py:313
  65.8 6.5 %collective-permute-start.22 = (bf16[32,256]{1,0:T(8,128)(2,1)S(1)}, bf16[32,256]{1,0:T(8,128)(2,1)S(1)}, u32[]{:S(2)}, u32[]{:S(2)}) collective-permute-start(bf16[32,256]{1,0:T(8,128)(2,1)S(1)} %get-tuple-element.67), channel_id=1, source_target_pairs={{16,0},{20,4},{24,8},{28,12},{17,1},{21,5},{25,9},{29,13},{18,2},{... | collective-permute-start | bytes 49160 | tf_op jit(solution)/shard_map/ppermute | solution.py:540
  72.4 7.4 %collective-permute-start.23 = (bf16[32,256]{1,0:T(8,128)(2,1)S(1)}, bf16[32,256]{1,0:T(8,128)(2,1)S(1)}, u32[]{:S(2)}, u32[]{:S(2)}) collective-permute-start(bf16[32,256]{1,0:T(8,128)(2,1)S(1)} %get-tuple-element.68), channel_id=1, source_target_pairs={{16,4},{20,0},{24,12},{28,8},{17,5},{21,1},{25,13},{29,9},{18,6},{... | collective-permute-start | bytes 49160 | tf_op jit(solution)/shard_map/ppermute | solution.py:540
  79.8 7.4 %collective-permute-start.24 = (bf16[32,256]{1,0:T(8,128)(2,1)S(1)}, bf16[32,256]{1,0:T(8,128)(2,1)S(1)}, u32[]{:S(2)}, u32[]{:S(2)}) collective-permute-start(bf16[32,256]{1,0:T(8,128)(2,1)S(1)} %get-tuple-element.69), channel_id=1, source_target_pairs={{16,8},{20,12},{24,0},{28,4},{17,9},{21,13},{25,1},{29,5},{18,10},... | collective-permute-start | bytes 49160 | tf_op jit(solution)/shard_map/ppermute | solution.py:540
  87.2 8.3 %collective-permute-start.25 = (bf16[32,256]{1,0:T(8,128)(2,1)S(1)}, bf16[32,256]{1,0:T(8,128)(2,1)S(1)}, u32[]{:S(2)}, u32[]{:S(2)}) collective-permute-start(bf16[32,256]{1,0:T(8,128)(2,1)S(1)} %get-tuple-element.70), channel_id=1, source_target_pairs={{16,12},{20,8},{24,4},{28,0},{17,13},{21,9},{25,5},{29,1},{18,14},... | collective-permute-start | bytes 49160 | tf_op jit(solution)/shard_map/ppermute | solution.py:540

commit v2 on v0

--- a/solution.py
+++ b/solution.py
@@ -1,6 +1,8 @@
 import jax
 import jax.numpy as jnp
 from jax import lax
+from jax.experimental import pallas as pl
+from jax.experimental.pallas import tpu as pltpu
 from jax.sharding import PartitionSpec as P
 
 HEAD_DIM = 128
@@ -64,7 +66,7 @@
     return (probability.astype(jnp.bfloat16), score_grad)
 
 
-def local(queries, key_rows, value_rows, out_weight, grad_out, pair_offsets, far_head_offsets):
+def exchange_local(queries, key_rows, value_rows, out_weight, grad_out, pair_offsets, far_head_offsets):
     tokens = queries.shape[0]
     head_count = queries.shape[1] // HEAD_DIM
     factor = HEAD_DIM ** (-0.5)
@@ -167,7 +169,7 @@
     )
     head_grads = by_head(grad_attended.astype(jnp.bfloat16))
     row_delta = jnp.sum(head_grads.astype(jnp.float32) * head_out, axis=-1)
-    local_prob, local_dscore = score_grads(
+    _, local_dscore = score_grads(
         local_scores, row_max, row_sum, head_grads, segment_value, row_delta
     )
     query_grad = product(local_dscore, segment_key, "hij,hjd->hid") * factor
@@ -197,7 +199,7 @@
     pair_max = select(row_max, 2, pair_branch_shift)
     pair_sum = select(row_sum, 2, pair_branch_shift)
     pair_delta = select(row_delta, 2, pair_branch_shift)
-    pair_prob, pair_dscore = score_grads(
+    _, pair_dscore = score_grads(
         pair_scores, pair_max, pair_sum, pair_grad, pair_all_value, pair_delta
     )
     pair_dq = product(pair_dscore, pair_all_key, "hij,hjd->hid") * factor
@@ -252,6 +254,413 @@
     )
 
 
+def lanes(index):
+    return pl.ds(pl.multiple_of(index * HEAD_DIM, HEAD_DIM), HEAD_DIM)
+
+
+def rows(index, length):
+    return pl.ds(pl.multiple_of(index * length, length), length)
+
+
+def matmul(left, right, dims):
+    return lax.dot_general(left, right, (dims, ((), ())), preferred_element_type=jnp.float32)
+
+
+NN = ((1,), (0,))
+NT = ((1,), (1,))
+TN = ((0,), (0,))
+
+
+def call(body, out_shape, in_specs, scratch=(), flops=0, out_space=pltpu.VMEM, limit=40):
+    out_spec = pl.BlockSpec(memory_space=out_space)
+    return pl.pallas_call(
+        body,
+        out_shape=out_shape,
+        in_specs=in_specs,
+        out_specs=jax.tree.map(lambda _: out_spec, out_shape),
+        scratch_shapes=list(scratch),
+        cost_estimate=pl.CostEstimate(flops=flops, bytes_accessed=0, transcendentals=0),
+        compiler_params=pltpu.CompilerParams(vmem_limit_bytes=limit * 2**20 if limit else None),
+    )
+
+
+def fast_local(plan, queries, key_rows, value_rows, out_weight, grad_out, pair_offsets, far_offsets):
+    tokens, heads, group, selected, dilation, head_groups = plan
+    factor = HEAD_DIM ** (-0.5)
+    width = heads * HEAD_DIM
+    model = out_weight.shape[1]
+    span = group * tokens
+    far_span = span // dilation
+    bf16, f32 = jnp.bfloat16, jnp.float32
+    vmem = pl.BlockSpec(memory_space=pltpu.VMEM)
+    smem = pl.BlockSpec(memory_space=pltpu.SMEM)
+    dests = range(group)
+
+    def shape(extent, dtype=bf16):
+        return jax.ShapeDtypeStruct(extent, dtype)
+
+    def seq_rank():
+        return lax.rem(lax.axis_index("seq"), group)
+
+    def late_half():
+        return lax.axis_index("seq") // group
+
+    def my_head():
+        return lax.axis_index("head") * heads + seq_rank()
+
+    def swap(value, axis, mask):
+        pairs = [(s, s ^ mask) for s in range(lax.axis_size(axis))]
+        return lax.ppermute(value, axis, pairs)
+
+    def swapped(blocks):
+        return [blocks[0]] + [swap(blocks[m], "seq", m) for m in dests if m]
+
+    others = [swap(grad_out, "head", m) for m in range(1, head_groups)]
+
+    def opening(out):
+        out[...] = jnp.zeros_like(out)
+
+    opened = call(opening, shape((8, HEAD_DIM), f32), [], flops=2 * 10**10)()
+
+    def pack(opened, q, k, v, *outs):
+        rank = seq_rank()
+        for slot, ref in enumerate((q, k, v)):
+            for m in dests:
+                outs[m][:, slot * HEAD_DIM : (slot + 1) * HEAD_DIM] = ref[:, lanes(rank ^ m)]
+
+    packed = call(
+        pack, [shape((tokens, 3 * HEAD_DIM))] * group, [vmem] * 4, flops=10**9
+    )(opened, queries, key_rows, value_rows)
+    blocks = swapped(packed)
+
+    def project_grad(w, *refs):
+        parts, outs, (acc,) = refs[:head_groups], refs[head_groups:-1], refs[-1:]
+        me = lax.axis_index("head")
+        for m in range(head_groups):
+            cols = pl.ds(pl.multiple_of((me ^ m) * width, width), width)
+            term = matmul(parts[m][...], w[:, cols], NT)
+            if m == 0:
+                acc[...] = term
+            else:
+                acc[...] += term
+        rank = seq_rank()
+        for m in dests:
+            outs[m][...] = acc[:, lanes(rank ^ m)].astype(bf16)
+
+    grad_blocks = swapped(
+        call(
+            project_grad,
+            [shape((tokens, HEAD_DIM))] * group,
+            [vmem] * (1 + head_groups),
+            [pltpu.VMEM((tokens, width), f32)],
+            flops=10**8,
+        )(out_weight, grad_out, *others),
+    )
+
+    def branch_scores(query, key, mask):
+        return jnp.where(mask, matmul(query, key, NT) * factor, masked_score)
+
+    def causal(extent, shift=0):
+        row_ids = lax.broadcasted_iota(jnp.int32, extent, 0)
+        col_ids = lax.broadcasted_iota(jnp.int32, extent, 1)
+        return row_ids + shift >= col_ids
+
+    def far_mask():
+        extent = (far_span, 2 * far_span)
+        col_ids = lax.broadcasted_iota(jnp.int32, extent, 1)
+        open_cols = jnp.where(late_half() > 0, 0, far_span)
+        return causal(extent, far_span) & (col_ids >= open_cols)
+
+    def stats(scores, value):
+        top = jnp.max(scores, axis=-1, keepdims=True)
+        weights = jnp.exp(scores - top)
+        total = jnp.sum(weights, axis=-1, keepdims=True)
+        return top, total, matmul(weights.astype(bf16), value, NN)
+
+    def spread_lanes(column):
+        return jnp.broadcast_to(column, (column.shape[0], HEAD_DIM))
+
+    def pick(ref, at):
+        return ref[at, :].astype(bf16)
+
+    def pair_rows(po):
+        return pl.ds(po[my_head()], selected, stride=2)
+
+    def far_rows(fo):
+        return pl.ds(fo[my_head()], far_span, stride=dilation)
+
+    def with_early(early_kv, slot, ref, at):
+        cols = slice(slot * HEAD_DIM, (slot + 1) * HEAD_DIM)
+        return jnp.concatenate([early_kv[:, cols], pick(ref, at)], axis=0)
+
+    wide = shape((span, HEAD_DIM), f32)
+    far_pair = shape((far_span, 2 * HEAD_DIM))
+
+    def assemble(fo, *refs):
+        parts, (q, k, v, far_kv) = refs[:group], refs[group:]
+        rank = seq_rank()
+        for m in dests:
+            at = rows(rank ^ m, tokens)
+            for slot, ref in enumerate((q, k, v)):
+                part = parts[m][:, slot * HEAD_DIM : (slot + 1) * HEAD_DIM]
+                ref[at, :] = part.astype(f32)
+        far_at = far_rows(fo)
+        far_kv[:, :HEAD_DIM] = pick(k, far_at)
+        far_kv[:, HEAD_DIM:] = pick(v, far_at)
+
+    q, k, v, far_kv = call(
+        assemble, [wide] * 3 + [far_pair], [smem] + [vmem] * group, flops=10**7
+    )(far_offsets, *blocks)
+    early_kv = swap(far_kv, "seq", group)
+
+    def forward_near(po, q, k, v, top_all, sum_all, acc):
+        mask = causal((selected, selected))
+        for first in range(0, span, selected):
+            at = pl.ds(first, selected)
+            top, total, numerator = stats(
+                branch_scores(pick(q, at), pick(k, at), mask), pick(v, at)
+            )
+            top_all[at, :] = spread_lanes(top)
+            sum_all[at, :] = spread_lanes(total)
+            acc[at, :] = numerator
+        merge(
+            pair_rows(po),
+            stats(
+                branch_scores(pick(q, pair_rows(po)), pick(k, pair_rows(po)), mask),
+                pick(v, pair_rows(po)),
+            ),
+            (top_all, sum_all, acc),
+        )
+
+    def merge(at, branch, totals):
+        top, total, numerator = branch
+        top_all, sum_all, acc = totals
+        old_top = top_all[at, :]
+        new_top = jnp.maximum(old_top, spread_lanes(top))
+        old_scale, scale = jnp.exp(old_top - new_top), jnp.exp(top - new_top)
+        top_all[at, :] = new_top
+        sum_all[at, :] = sum_all[at, :] * old_scale + total * scale
+        acc[at, :] = acc[at, :] * old_scale + numerator * scale
+
+    near = call(forward_near, [wide] * 3, [smem] + [vmem] * 3, flops=2 * 10**8)(
+        pair_offsets, q, k, v
+    )
+
+    def forward_far(fo, q, k, v, early_kv, near_top, near_sum, near_acc, *refs):
+        outs, (out_wide, lse, top_all, sum_all) = refs[:group], refs[group:]
+        far_at = far_rows(fo)
+        top_all[...] = near_top[...]
+        sum_all[...] = near_sum[...]
+        out_wide[...] = near_acc[...]
+        key, value = with_early(early_kv, 0, k, far_at), with_early(early_kv, 1, v, far_at)
+        branch = stats(branch_scores(pick(q, far_at), key, far_mask()), value)
+        merge(far_at, branch, (top_all, sum_all, out_wide))
+        out_wide[...] = out_wide[...] / sum_all[...]
+        lse[...] = top_all[...] + jnp.log(sum_all[...])
+        rank = seq_rank()
+        for m in dests:
+            outs[m][...] = out_wide[rows(rank ^ m, tokens), :].astype(bf16)
+
+    scratch = pltpu.VMEM((span, HEAD_DIM), f32)
+    *out_blocks, out_wide, lse = call(
+        forward_far,
+        [shape((tokens, HEAD_DIM))] * group + [wide, wide],
+        [smem] + [vmem] * 7,
+        [scratch] * 2,
+        flops=10**8,
+    )(far_offsets, q, k, v, early_kv, *near)
+    attended = swapped(out_blocks)
+
+    def grads_of(query, key, value, grad, row_lse, row_delta, mask):
+        scores = branch_scores(query, key, mask)
+        probability = jnp.exp(scores - row_lse[:, :1])
+        prob_grad = matmul(grad, value, NT)
+        score_grad = (probability * (prob_grad - row_delta[:, :1])).astype(bf16)
+        return (
+            matmul(score_grad, key, NN) * factor,
+            matmul(score_grad, query, TN) * factor,
+            matmul(probability.astype(bf16), grad, TN),
+        )
+
+    def backward_far(fo, q, k, v, early_kv, out_wide, lse, *refs):
+        parts, (grad, delta, far_dq, far_dk, far_dv, far_kv) = refs[:group], refs[group:]
+        rank = seq_rank()
+        for m in dests:
+            grad[rows(rank ^ m, tokens), :] = parts[m][...].astype(f32)
+        delta[...] = spread_lanes(jnp.sum(grad[...] * out_wide[...], axis=-1, keepdims=True))
+        at = far_rows(fo)
+        far_dq[...], dk, dv = grads_of(
+            pick(q, at),
+            with_early(early_kv, 0, k, at),
+            with_early(early_kv, 1, v, at),
+            pick(grad, at),
+            lse[at, :],
+            delta[at, :],
+            far_mask(),
+        )
+        far_kv[:, :HEAD_DIM] = dk[:far_span].astype(bf16)
+        far_kv[:, HEAD_DIM:] = dv[:far_span].astype(bf16)
+        far_dk[...] = dk[far_span:]
+        far_dv[...] = dv[far_span:]
+
+    far_wide = shape((far_span, HEAD_DIM), f32)
+    grad, delta, far_dq, far_dk, far_dv, late_kv = call(
+        backward_far,
+        [wide, wide] + [far_wide] * 3 + [far_pair],
+        [smem] + [vmem] * (6 + group),
+        flops=2 * 10**8,
+    )(far_offsets, q, k, v, early_kv, out_wide, lse, *grad_blocks)
+    late = swap(late_kv, "seq", group)
+
+    def backward_near(po, fo, q, k, v, grad, lse, delta, *refs):
+        fars, near = refs[:3], refs[3:]
+        mask = causal((selected, selected))
+        for first in range(0, span, selected):
+            at = pl.ds(first, selected)
+            terms = grads_of(
+                pick(q, at), pick(k, at), pick(v, at), pick(grad, at), lse[at, :], delta[at, :], mask
+            )
+            for ref, term in zip(near, terms):
+                ref[at, :] = term
+        at = pair_rows(po)
+        terms = grads_of(
+            pick(q, at), pick(k, at), pick(v, at), pick(grad, at), lse[at, :], delta[at, :], mask
+        )
+        for ref, term in zip(near, terms):
+            ref[at, :] += term
+        for ref, far in zip(near, fars):
+            ref[far_rows(fo), :] += far[...]
+
+    dq, dk, dv = call(
+        backward_near, [wide] * 3, [smem, smem] + [vmem] * 9, flops=5 * 10**8
+    )(pair_offsets, far_offsets, q, k, v, grad, lse, delta, far_dq, far_dk, far_dv)
+
+    def finish(fo, dq, dk, dv, late, *refs):
+        outs, sums = refs[:group], refs[group:]
+        at = far_rows(fo)
+        for slot, (ref, part) in enumerate(zip(sums, (dk, dv))):
+            ref[...] = part[...]
+            ref[at, :] += late[:, slot * HEAD_DIM : (slot + 1) * HEAD_DIM].astype(f32)
+        rank = seq_rank()
+        for m in dests:
+            for slot, ref in enumerate((dq, *sums)):
+                cols = slice(slot * HEAD_DIM, (slot + 1) * HEAD_DIM)
+                outs[m][:, cols] = ref[rows(rank ^ m, tokens), :].astype(bf16)
+
+    returned = swapped(
+        call(
+            finish,
+            [shape((tokens, 3 * HEAD_DIM))] * group,
+            [smem] + [vmem] * 4,
+            [scratch] * 2,
+            flops=10**7,
+        )(far_offsets, dq, dk, dv, late),
+    )
+
+    half = model // 2
+
+    def columns(bit):
+        return pl.ds(pl.multiple_of(bit * half, half), half)
+
+    def my_half():
+        return lax.rem(lax.axis_index("head"), 2)
+
+    def project_theirs(w, *refs):
+        parts, (both, send) = refs[:group], refs[group:]
+        rank = seq_rank()
+        for m in dests:
+            both[:, lanes(rank ^ m)] = parts[m][...]
+        send[...] = matmul(both[...], w[:, columns(1 - my_half())], NN).astype(bf16)
+
+    half_out = shape((tokens, half))
+    both, theirs = call(
+        project_theirs,
+        [shape((tokens, width)), half_out],
+        [vmem] * (1 + group),
+        flops=10**8,
+    )(out_weight, *attended)
+    mate = swap(theirs, "head", 1)
+
+    def project_mine(w, both, out):
+        out[...] = matmul(both[...], w[:, columns(my_half())], NN).astype(bf16)
+
+    def add_mate(first, second, out):
+        out[...] = (first[...].astype(f32) + second[...].astype(f32)).astype(bf16)
+
+    def add_across(first, second, out):
+        add_mate(first, second, out)
+
+    mine = call(project_mine, half_out, [vmem] * 2, flops=10**8)(out_weight, both)
+    pair_sum = call(add_mate, half_out, [vmem] * 2, flops=10**6)(mine, mate)
+    across = swap(pair_sum, "head", 2)
+    total = call(add_across, half_out, [vmem] * 2, flops=10**6)(pair_sum, across)
+    other = swap(total, "head", 1)
+
+    def copy_all(copies):
+        for copy in copies:
+            copy.start()
+        for copy in copies:
+            copy.wait()
+
+    def join(mine, theirs, out, sems):
+        copy_all(
+            [
+                pltpu.make_async_copy(mine, out.at[:, columns(my_half())], sems.at[0]),
+                pltpu.make_async_copy(theirs, out.at[:, columns(1 - my_half())], sems.at[1]),
+            ]
+        )
+
+    layer_out = call(
+        join,
+        shape((tokens, model)),
+        [vmem] * 2,
+        [pltpu.SemaphoreType.DMA((2,))],
+        flops=10**6,
+        out_space=pltpu.HBM,
+    )(total, other)
+
+    def collect(*refs):
+        parts, outs, sems = refs[:group], refs[group : group + 3], refs[-1]
+        rank = seq_rank()
+        copy_all(
+            [
+                pltpu.make_async_copy(
+                    parts[m].at[:, slot * HEAD_DIM : (slot + 1) * HEAD_DIM],
+                    outs[slot].at[:, lanes(rank ^ m)],
+                    sems.at[m, slot],
+                )
+                for m in dests
+                for slot in range(3)
+            ]
+        )
+
+    gradients = call(
+        collect,
+        [shape((tokens, width))] * 3,
+        [vmem] * group,
+        [pltpu.SemaphoreType.DMA((group, 3))],
+        flops=10**7,
+        out_space=pltpu.HBM,
+    )(*returned)
+    return (layer_out, *gradients)
+
+
+def local(queries, key_rows, value_rows, out_weight, grad_out, pair_offsets, far_head_offsets):
+    tokens = queries.shape[0]
+    heads = queries.shape[1] // HEAD_DIM
+    seq_count = lax.axis_size("seq")
+    total = tokens * seq_count
+    selected = min(SPAN, total // 4)
+    group = 2 * selected // tokens
+    operands = (
+        queries, key_rows, value_rows, out_weight, grad_out, pair_offsets, far_head_offsets
+    )
+    if group == heads and seq_count == 2 * group and lax.axis_size("head") == 4:
+        plan = (tokens, heads, group, selected, total // selected, lax.axis_size("head"))
+        return fast_local(plan, *operands)
+    return exchange_local(*operands)
+
+
 def solution(mesh):
     placed = (
         P("seq", "head"),

time: 279 us -> 65.7 us (0.24)
  blocking collectives: 69.5 us -> 0 us
  local copies, waits for them, and re-layouts: 45.5 us -> 1.02 us
  waiting for transfers between devices: 72 us -> 30.4 us
  other arithmetic: 29.3 us -> 0 us
  matrix products: 27.8 us -> 0 us
  between operations: 16.2 us -> 0.82 us
  Pallas kernels: 0 us -> 9.72 us
  starting transfers between devices: 16.4 us -> 23.6 us
    all_gather x3 -> x0, blocking collectives: 69.5 us -> none  [the longest x1 31.1 us: local(): lax.all_gather(far_value, 'seq', axis=1, tiled=True)]
    reduce_scatter x2 -> x0, waiting for transfers between devices: 68.4 us -> none  [the longest x1 62.7 us: local(): lax.psum_scatter(gathered_dk, 'seq', scatter_dimension=1, tiled=True)]
    dot_general x20 -> x0, matrix products: 27.8 us -> none  [the longest x18 25.6 us: product(): jnp.einsum(pattern, left_side, right_side, preferred_element_type=jnp.flo...]
    ppermute x14 -> x20, waiting for transfers between devices: 3.57 us -> 30.4 us  [swap(): return lax.ppermute(value, axis, pairs)]
    reduce_sum x9 -> x0, other arithmetic: 15 us -> none  [the longest x6 12.6 us: select(): jnp.sum(jnp.where(lane_ids == chosen, shaped, jnp.zeros((), tensor.dtype)...]
    broadcast_in_dim x20 -> x0, local copies, waits for them, and re-layouts: 14.8 us -> none  [spread(): placed = jnp.where(lane_ids == chosen, jnp.expand_dims(entries, 2), filler)]
    select_n x14 -> x0, other arithmetic: 10.4 us -> none  [stacked(): lower = jnp.where(high, theirs, mine)]
    pallas_call x0 -> x15, Pallas kernels: none -> 9.72 us  [the longest x1 1.74 us: fast_local(): call(backward_near, [wide] * 3, [smem, smem] + [vmem] * 9, flops=5 * 10 *...]
  transfers between devices with their start and end apart: 17 -> 20, of which waited for: 6 -> 17; matrix products, arithmetic and copies ran while one was open for 29% -> 0% of each run, Pallas kernels for 0% -> 10%
where the time goes in v2:
time: 65.7 us; the launch traced here: 65.6 us
  waiting for transfers between devices  30.4 us (46%)
  starting transfers between devices  23.6 us (36%)
  Pallas kernels  9.72 us (15%)
  local copies, waits for them, and re-layouts  1.02 us (2%)
  between operations  0.82 us (1%)
    ppermute x20, waiting for transfers between devices, swap(): return lax.ppermute(value, axis, pairs)  30.4 us
    ppermute x20, starting transfers between devices, swap(): return lax.ppermute(value, axis, pairs)  23.6 us
    pallas_call x1, Pallas kernels, fast_local(): call(backward_near, [wide] * 3, [smem, smem] + [vmem] * 9, flops=5 * 10 *...  1.74 us
  transfers between devices with their start and end apart: 20, of which 17 were waited for; matrix products, arithmetic and copies ran while one was open for 0% of the time, Pallas kernels for 10%

profile of v2, /device:TPU:0, one launch (start us, length us, event | category | flops | bytes accessed | tf_op | source)
XLA Modules:
  0.0 65.6 jit_solution(12603135874478666142)
XLA Ops:
  0.7 0.9 %copy-done.4 = bf16[128,512]{1,0:T(8,128)(2,1)S(1)} copy-done((bf16[128,512]{1,0:T(8,128)(2,1)S(1)}, bf16[128,512]{1,0:T(8,128)(2,1)}, u32[]{:S(2)}) %copy-start.4) | copy-done | bytes 131096
  1.7 0.1 shard_map.103
  1.8 3.0 %collective-permute-start = (bf16[128,384]{1,0:T(8,128)(2,1)S(1)}, bf16[128,384]{1,0:T(8,128)(2,1)S(1)}, u32[]{:S(2)}, u32[]{:S(2)}) collective-permute-start(bf16[128,384]{1,0:T(8,128)(2,1)S(1)} %get-tuple-element.44), channel_id=1, source_target_pairs={{0,4},{4,0},{8,12},{12,8},{16,20},{20,16},{24,28},{28,24},{1,5},{5... | collective-permute-start | bytes 294920 | tf_op jit(solution)/shard_map/ppermute | solution.py:313
  4.8 1.6 %collective-permute-start.1 = (bf16[128,384]{1,0:T(8,128)(2,1)S(1)}, bf16[128,384]{1,0:T(8,128)(2,1)S(1)}, u32[]{:S(2)}, u32[]{:S(2)}) collective-permute-start(bf16[128,384]{1,0:T(8,128)(2,1)S(1)} %get-tuple-element.45), channel_id=1, source_target_pairs={{0,8},{4,12},{8,0},{12,4},{16,24},{20,28},{24,16},{28,20},{1,9},{5... | collective-permute-start | bytes 294920 | tf_op jit(solution)/shard_map/ppermute | solution.py:313
  6.4 1.2 %collective-permute-done.refs_1_ = bf16[128,384]{1,0:T(8,128)(2,1)S(1)} collective-permute-done((bf16[128,384]{1,0:T(8,128)(2,1)S(1)}, bf16[128,384]{1,0:T(8,128)(2,1)S(1)}, u32[]{:S(2)}, u32[]{:S(2)}) %collective-permute-start) | collective-permute-done | bytes 98336 | tf_op jit(solution)/shard_map/ppermute | solution.py:313
  7.6 2.7 %collective-permute-done.1.refs_2_ = bf16[128,384]{1,0:T(8,128)(2,1)S(1)} collective-permute-done((bf16[128,384]{1,0:T(8,128)(2,1)S(1)}, bf16[128,384]{1,0:T(8,128)(2,1)S(1)}, u32[]{:S(2)}, u32[]{:S(2)}) %collective-permute-start.1) | collective-permute-done | bytes 98336 | tf_op jit(solution)/shard_map/ppermute | solution.py:313
  10.3 1.6 %collective-permute-done.2.refs_3_ = bf16[128,384]{1,0:T(8,128)(2,1)S(1)} collective-permute-done((bf16[128,384]{1,0:T(8,128)(2,1)S(1)}, bf16[128,384]{1,0:T(8,128)(2,1)S(1)}, u32[]{:S(2)}, u32[]{:S(2)}) %collective-permute-start.2) | collective-permute-done | bytes 98336 | tf_op jit(solution)/shard_map/ppermute | solution.py:313
  11.9 0.6 shard_map.104
  12.5 2.7 %collective-permute-start.3 = (bf16[128,256]{1,0:T(8,128)(2,1)S(1)}, bf16[128,256]{1,0:T(8,128)(2,1)S(1)}, u32[]{:S(2)}, u32[]{:S(2)}) collective-permute-start(bf16[128,256]{1,0:T(8,128)(2,1)S(1)} %get-tuple-element.50), channel_id=1, source_target_pairs={{0,16},{4,20},{8,24},{12,28},{16,0},{20,4},{24,8},{28,12},{1,17},{... | collective-permute-start | bytes 196616 | tf_op jit(solution)/shard_map/ppermute | solution.py:313
  15.2 1.3 %shard_map.105 = (f32[512,128]{1,0:T(8,128)S(1)}, f32[512,128]{1,0:T(8,128)S(1)}, f32[512,128]{1,0:T(8,128)S(1)}) custom-call(s32[16]{0:T(128)S(1)} %copy-done.3, f32[512,128]{1,0:T(8,128)S(1)} %get-tuple-element.47.q, f32[512,128]{1,0:T(8,128)S(1)} %get-tuple-element.48.k, f32[512,128]{1,0:T(8,128)S(1)} %get-tuple-element.49.v), custom_call_target="tpu_custom_call" | custom-call | flops 200000000 | tf_op jit(solution)/shard_map/pallas_call | solution.py:445
  16.5 2.0 %collective-permute-done.3.early_kv = bf16[128,256]{1,0:T(8,128)(2,1)S(1)} collective-permute-done((bf16[128,256]{1,0:T(8,128)(2,1)S(1)}, bf16[128,256]{1,0:T(8,128)(2,1)S(1)}, u32[]{:S(2)}, u32[]{:S(2)}) %collective-permute-start.3) | collective-permute-done | bytes 65568 | tf_op jit(solution)/shard_map/ppermute | solution.py:313
  18.4 1.0 %shard_map.106 = (bf16[128,128]{1,0:T(8,128)(2,1)S(1)}, bf16[128,128]{1,0:T(8,128)(2,1)S(1)}, bf16[128,128]{1,0:T(8,128)(2,1)S(1)}, bf16[128,128]{1,0:T(8,128)(2...) custom-call(s32[16]{0:T(128)S(1)} %copy-done.2, f32[512,128]{1,0:T(8,128)S(1)} %get-tuple-element.47.q, ...), custom_call_target="tpu_custom_call" | custom-call | flops 100000000 | tf_op jit(solution)/shard_map/pallas_call | solution.py:465
  19.5 0.3 collective-permute-start.4
  19.8 1.4 %collective-permute-start.5 = (bf16[128,128]{1,0:T(8,128)(2,1)S(1)}, bf16[128,128]{1,0:T(8,128)(2,1)S(1)}, u32[]{:S(2)}, u32[]{:S(2)}) collective-permute-start(bf16[128,128]{1,0:T(8,128)(2,1)S(1)} %get-tuple-element.56), channel_id=1, source_target_pairs={{0,8},{4,12},{8,0},{12,4},{16,24},{20,28},{24,16},{28,20},{1,9},{5... | collective-permute-start | bytes 98312 | tf_op jit(solution)/shard_map/ppermute | solution.py:313
  21.1 1.9 %collective-permute-start.6 = (bf16[128,128]{1,0:T(8,128)(2,1)S(1)}, bf16[128,128]{1,0:T(8,128)(2,1)S(1)}, u32[]{:S(2)}, u32[]{:S(2)}) collective-permute-start(bf16[128,128]{1,0:T(8,128)(2,1)S(1)} %get-tuple-element.57), channel_id=1, source_target_pairs={{0,12},{4,8},{8,4},{12,0},{16,28},{20,24},{24,20},{28,16},{1,13},{... | collective-permute-start | bytes 98312 | tf_op jit(solution)/shard_map/ppermute | solution.py:313
  23.0 0.4 collective-permute-done.4.refs_1_
  23.4 0.2 collective-permute-done.5.refs_2_
  23.7 2.3 %collective-permute-done.6.refs_3_ = bf16[128,128]{1,0:T(8,128)(2,1)S(1)} collective-permute-done((bf16[128,128]{1,0:T(8,128)(2,1)S(1)}, bf16[128,128]{1,0:T(8,128)(2,1)S(1)}, u32[]{:S(2)}, u32[]{:S(2)}) %collective-permute-start.6) | collective-permute-done | bytes 32800 | tf_op jit(solution)/shard_map/ppermute | solution.py:313
  26.0 0.3 shard_map.107
  26.3 0.1 collective-permute-start.7
  26.4 0.3 shard_map.108.first
  26.7 1.2 %collective-permute-done.7.second = bf16[128,1024]{1,0:T(8,128)(2,1)S(1)} collective-permute-done((bf16[128,1024]{1,0:T(8,128)(2,1)S(1)}, bf16[128,1024]{1,0:T(8,128)(2,1)S(1)}, u32[]{:S(2)}, u32[]{:S(2)}) %collective-permute-start.7) | collective-permute-done | bytes 262176 | tf_op jit(solution)/shard_map/ppermute | solution.py:313
  28.0 1.6 %collective-permute-start.8 = (bf16[128,1024]{1,0:T(8,128)(2,1)S(1)}, bf16[128,1024]{1,0:T(8,128)(2,1)S(1)}, u32[]{:S(2)}, u32[]{:S(2)}) collective-permute-start(bf16[128,1024]{1,0:T(8,128)(2,1)S(1)} %shard_map.109.first), channel_id=1, source_target_pairs={{0,2},{1,3},{2,0},{3,1},{4,6},{5,7},{6,4},{7,5},{8,10},{9,11},{10,... | collective-permute-start | bytes 786440 | tf_op jit(solution)/shard_map/ppermute | solution.py:313
  29.5 0.5 collective-permute-start.11
  30.0 1.4 %collective-permute-start.12 = (bf16[128,512]{1,0:T(8,128)(2,1)S(1)}, bf16[128,512]{1,0:T(8,128)(2,1)S(1)}, u32[]{:S(2)}, u32[]{:S(2)}) collective-permute-start(bf16[128,512]{1,0:T(8,128)(2,1)S(1)} %copy-done.1), channel_id=1, source_target_pairs={{0,3},{1,2},{2,1},{3,0},{4,7},{5,6},{6,5},{7,4},{8,11},{9,10},{10,... | collective-permute-start | bytes 393224 | tf_op jit(solution)/shard_map/ppermute | solution.py:313
  31.4 5.8 %collective-permute-done.8.second = bf16[128,1024]{1,0:T(8,128)(2,1)S(1)} collective-permute-done((bf16[128,1024]{1,0:T(8,128)(2,1)S(1)}, bf16[128,1024]{1,0:T(8,128)(2,1)S(1)}, u32[]{:S(2)}, u32[]{:S(2)}) %collective-permute-start.8) | collective-permute-done | bytes 262176 | tf_op jit(solution)/shard_map/ppermute | solution.py:313
  37.3 0.1 collective-permute-start.9
  37.3 2.7 %collective-permute-done.11.refs_2_ = bf16[128,512]{1,0:T(8,128)(2,1)S(1)} collective-permute-done((bf16[128,512]{1,0:T(8,128)(2,1)S(1)}, bf16[128,512]{1,0:T(8,128)(2,1)S(1)}, u32[]{:S(2)}, u32[]{:S(2)}) %collective-permute-start.11) | collective-permute-done | bytes 131104 | tf_op jit(solution)/shard_map/ppermute | solution.py:313
  40.0 1.1 %collective-permute-done.12.refs_3_ = bf16[128,512]{1,0:T(8,128)(2,1)S(1)} collective-permute-done((bf16[128,512]{1,0:T(8,128)(2,1)S(1)}, bf16[128,512]{1,0:T(8,128)(2,1)S(1)}, u32[]{:S(2)}, u32[]{:S(2)}) %collective-permute-start.12) | collective-permute-done | bytes 131104 | tf_op jit(solution)/shard_map/ppermute | solution.py:313
  41.1 0.9 %shard_map.112 = (bf16[128,128]{1,0:T(8,128)(2,1)S(1)}, bf16[128,128]{1,0:T(8,128)(2,1)S(1)}, bf16[128,128]{1,0:T(8,128)(2,1)S(1)}, bf16[128,128]{1,0:T(8,128)(2,1)S(1)}) custom-call(bf16[512,2048]{1,0:T(8,128)(2,1)S(1)} %copy-done, bf16[128,512]{1,0:T(8,128)(2,1)S(1)} %copy-done.1, bf16[128,512]{1,0:T(8,128)(2,1)S(1)} %collective-permute-done.10.refs_1_, ...), custom_call_target="tpu_custom_call" | custom-call | flops 100000000 | tf_op jit(solution)/shard_map/pallas_call | solution.py:351
  42.0 0.8 %collective-permute-start.13 = (bf16[128,128]{1,0:T(8,128)(2,1)S(1)}, bf16[128,128]{1,0:T(8,128)(2,1)S(1)}, u32[]{:S(2)}, u32[]{:S(2)}) collective-permute-start(bf16[128,128]{1,0:T(8,128)(2,1)S(1)} %get-tuple-element.63), channel_id=1, source_target_pairs={{0,4},{4,0},{8,12},{12,8},{16,20},{20,16},{24,28},{28,24},{1,5},{5... | collective-permute-start | bytes 98312 | tf_op jit(solution)/shard_map/ppermute | solution.py:313
  42.8 1.8 %collective-permute-start.14 = (bf16[128,128]{1,0:T(8,128)(2,1)S(1)}, bf16[128,128]{1,0:T(8,128)(2,1)S(1)}, u32[]{:S(2)}, u32[]{:S(2)}) collective-permute-start(bf16[128,128]{1,0:T(8,128)(2,1)S(1)} %get-tuple-element.64), channel_id=1, source_target_pairs={{0,8},{4,12},{8,0},{12,4},{16,24},{20,28},{24,16},{28,20},{1,9},{5... | collective-permute-start | bytes 98312 | tf_op jit(solution)/shard_map/ppermute | solution.py:313
  44.5 1.0 %collective-permute-start.15 = (bf16[128,128]{1,0:T(8,128)(2,1)S(1)}, bf16[128,128]{1,0:T(8,128)(2,1)S(1)}, u32[]{:S(2)}, u32[]{:S(2)}) collective-permute-start(bf16[128,128]{1,0:T(8,128)(2,1)S(1)} %get-tuple-element.65), channel_id=1, source_target_pairs={{0,12},{4,8},{8,4},{12,0},{16,28},{20,24},{24,20},{28,16},{1,13},{... | collective-permute-start | bytes 98312 | tf_op jit(solution)/shard_map/ppermute | solution.py:313
  45.6 0.5 collective-permute-done.13.refs_1_
  46.0 0.7 %collective-permute-done.14.refs_2_ = bf16[128,128]{1,0:T(8,128)(2,1)S(1)} collective-permute-done((bf16[128,128]{1,0:T(8,128)(2,1)S(1)}, bf16[128,128]{1,0:T(8,128)(2,1)S(1)}, u32[]{:S(2)}, u32[]{:S(2)}) %collective-permute-start.14) | collective-permute-done | bytes 32800 | tf_op jit(solution)/shard_map/ppermute | solution.py:313
  46.7 2.7 %collective-permute-done.15.refs_3_ = bf16[128,128]{1,0:T(8,128)(2,1)S(1)} collective-permute-done((bf16[128,128]{1,0:T(8,128)(2,1)S(1)}, bf16[128,128]{1,0:T(8,128)(2,1)S(1)}, u32[]{:S(2)}, u32[]{:S(2)}) %collective-permute-start.15) | collective-permute-done | bytes 32800 | tf_op jit(solution)/shard_map/ppermute | solution.py:313
  49.3 1.0 %shard_map.113 = (f32[512,128]{1,0:T(8,128)S(1)}, f32[512,128]{1,0:T(8,128)S(1)}, f32[128,128]{1,0:T(8,128)S(1)}, f32[128,128]{1,0:T(8,128)S(1)}, f32[128,128]{1,0:T(8,128)S(1)}, /*index=5*/bf16[128,256]{1,0:T(8,128)(2,1)S(1)}) custom-call(s32[16]{0:T(128)S(1)} %copy-done.2, f32[512,128]{1,0:T(8,128)S(1)} %get-tuple-element.47.q, ...), custom_call_target="tpu_custom_call" | custom-call | flops 200000000 | tf_op jit(solution)/shard_map/pallas_call | solution.py:507
  50.4 2.0 %collective-permute-start.16 = (bf16[128,256]{1,0:T(8,128)(2,1)S(1)}, bf16[128,256]{1,0:T(8,128)(2,1)S(1)}, u32[]{:S(2)}, u32[]{:S(2)}) collective-permute-start(bf16[128,256]{1,0:T(8,128)(2,1)S(1)} %get-tuple-element.74), channel_id=1, source_target_pairs={{0,16},{4,20},{8,24},{12,28},{16,0},{20,4},{24,8},{28,12},{1,17},{... | collective-permute-start | bytes 196616 | tf_op jit(solution)/shard_map/ppermute | solution.py:313
  52.4 1.7 %shard_map.114 = (f32[512,128]{1,0:T(8,128)S(1)}, f32[512,128]{1,0:T(8,128)S(1)}, f32[512,128]{1,0:T(8,128)S(1)}) custom-call(s32[16]{0:T(128)S(1)} %copy-done.3, s32[16]{0:T(128)S(1)} %copy-done.2, f32[512,128]{1,0:T(8,128)S(1)} %get-tuple-element.47.q, f32[512,128]{1,0:T(8,128)S(1)} %get-tuple-element.48.k, f32[512,128]{1,0:T(8,128)S(1)} %get-tuple-element.49.v, ...), custom_call_target="tpu_custom_call" | custom-call | flops 500000000 | tf_op jit(solution)/shard_map/pallas_call | solution.py:534
  54.2 1.8 %collective-permute-done.16.late = bf16[128,256]{1,0:T(8,128)(2,1)S(1)} collective-permute-done((bf16[128,256]{1,0:T(8,128)(2,1)S(1)}, bf16[128,256]{1,0:T(8,128)(2,1)S(1)}, u32[]{:S(2)}, u32[]{:S(2)}) %collective-permute-start.16) | collective-permute-done | bytes 65568 | tf_op jit(solution)/shard_map/ppermute | solution.py:313
  56.0 0.6 shard_map.115
  56.7 0.1 collective-permute-start.17
  56.8 1.6 %collective-permute-start.18 = (bf16[128,384]{1,0:T(8,128)(2,1)S(1)}, bf16[128,384]{1,0:T(8,128)(2,1)S(1)}, u32[]{:S(2)}, u32[]{:S(2)}) collective-permute-start(bf16[128,384]{1,0:T(8,128)(2,1)S(1)} %get-tuple-element.77), channel_id=1, source_target_pairs={{0,8},{4,12},{8,0},{12,4},{16,24},{20,28},{24,16},{28,20},{1,9},{5... | collective-permute-start | bytes 294920 | tf_op jit(solution)/shard_map/ppermute | solution.py:313
  58.3 1.9 %collective-permute-start.19 = (bf16[128,384]{1,0:T(8,128)(2,1)S(1)}, bf16[128,384]{1,0:T(8,128)(2,1)S(1)}, u32[]{:S(2)}, u32[]{:S(2)}) collective-permute-start(bf16[128,384]{1,0:T(8,128)(2,1)S(1)} %get-tuple-element.78), channel_id=1, source_target_pairs={{0,12},{4,8},{8,4},{12,0},{16,28},{20,24},{24,20},{28,16},{1,13},{... | collective-permute-start | bytes 294920 | tf_op jit(solution)/shard_map/ppermute | solution.py:313
  60.2 1.5 %collective-permute-done.17.refs_1_ = bf16[128,384]{1,0:T(8,128)(2,1)S(1)} collective-permute-done((bf16[128,384]{1,0:T(8,128)(2,1)S(1)}, bf16[128,384]{1,0:T(8,128)(2,1)S(1)}, u32[]{:S(2)}, u32[]{:S(2)}) %collective-permute-start.17) | collective-permute-done | bytes 98336 | tf_op jit(solution)/shard_map/ppermute | solution.py:313
  61.8 2.1 %collective-permute-done.19.refs_3_ = bf16[128,384]{1,0:T(8,128)(2,1)S(1)} collective-permute-done((bf16[128,384]{1,0:T(8,128)(2,1)S(1)}, bf16[128,384]{1,0:T(8,128)(2,1)S(1)}, u32[]{:S(2)}, u32[]{:S(2)}) %collective-permute-start.19) | collective-permute-done | bytes 98336 | tf_op jit(solution)/shard_map/ppermute | solution.py:313
  63.9 0.8 %shard_map.116 = (bf16[128,512]{1,0:T(8,128)(2,1)}, bf16[128,512]{1,0:T(8,128)(2,1)}, bf16[128,512]{1,0:T(8,128)(2,1)}) custom-call(bf16[128,384]{1,0:T(8,128)(2,1)S(1)} %get-tuple-element.75.refs_0_, bf16[128,384]{1,0:T(8,128)(2,1)S(1)} %collective-permute-done.17.refs_1_, bf16[128,384]{1,0:T(8,128)(2,1)S(1)} %collective-permute-done.18.refs_2_, ...), custom_call_target="tpu_custom_call" | custom-call | flops 10000000 | tf_op jit(solution)/shard_map/pallas_call | solution.py:637
  64.7 0.8 %shard_map.111 = bf16[128,2048]{1,0:T(8,128)(2,1)} custom-call(bf16[128,1024]{1,0:T(8,128)(2,1)S(1)} %shard_map.110.mine, bf16[128,1024]{1,0:T(8,128)(2,1)S(1)} %collective-permute-done.9.theirs), custom_call_target="tpu_custom_call" | custom-call | flops 1000000 | tf_op jit(solution)/shard_map/pallas_call | solution.py:613
  (21 shorter events, 0.3 us)
Async XLA Ops:
  0.6 0.9 %copy-start.4 = (bf16[128,512]{1,0:T(8,128)(2,1)S(1)}, bf16[128,512]{1,0:T(8,128)(2,1)}, u32[]{:S(2)}) copy-start(bf16[128,512]{1,0:T(8,128)(2,1)} %q.1) | copy-start | bytes 393220
  0.6 1.0 %copy-start.5 = (bf16[128,512]{1,0:T(8,128)(2,1)S(1)}, bf16[128,512]{1,0:T(8,128)(2,1)}, u32[]{:S(2)}) copy-start(bf16[128,512]{1,0:T(8,128)(2,1)} %k.1) | copy-start | bytes 393220
  0.7 1.0 %copy-start.6 = (bf16[128,512]{1,0:T(8,128)(2,1)S(1)}, bf16[128,512]{1,0:T(8,128)(2,1)}, u32[]{:S(2)}) copy-start(bf16[128,512]{1,0:T(8,128)(2,1)} %v.1) | copy-start | bytes 393220
  1.7 10.2 %copy-start.2 = (s32[16]{0:T(128)S(1)}, s32[16]{0:T(128)}, u32[]{:S(2)}) copy-start(s32[16]{0:T(128)} %fo.9) | copy-start | bytes 196
  1.7 13.5 %copy-start.3 = (s32[16]{0:T(128)S(1)}, s32[16]{0:T(128)}, u32[]{:S(2)}) copy-start(s32[16]{0:T(128)} %po.3) | copy-start | bytes 196
  1.7 24.2 %copy-start = (bf16[512,2048]{1,0:T(8,128)(2,1)S(1)}, bf16[512,2048]{1,0:T(8,128)(2,1)}, u32[]{:S(2)}) copy-start(bf16[512,2048]{1,0:T(8,128)(2,1)} %w.5) | copy-start | bytes 6291460
  1.8 5.8 %collective-permute-start = (bf16[128,384]{1,0:T(8,128)(2,1)S(1)}, bf16[128,384]{1,0:T(8,128)(2,1)S(1)}, u32[]{:S(2)}, u32[]{:S(2)}) collective-permute-start(bf16[128,384]{1,0:T(8,128)(2,1)S(1)} %get-tuple-element.44), channel_id=1, source_target_pairs={{0,4},{4,0},{8,12},{12,8},{16,20},{20,16},{24,28},{28,24},{1,5},{5... | collective-permute-start | bytes 294920 | tf_op jit(solution)/shard_map/ppermute | solution.py:313
  4.8 5.5 %collective-permute-start.1 = (bf16[128,384]{1,0:T(8,128)(2,1)S(1)}, bf16[128,384]{1,0:T(8,128)(2,1)S(1)}, u32[]{:S(2)}, u32[]{:S(2)}) collective-permute-start(bf16[128,384]{1,0:T(8,128)(2,1)S(1)} %get-tuple-element.45), channel_id=1, source_target_pairs={{0,8},{4,12},{8,0},{12,4},{16,24},{20,28},{24,16},{28,20},{1,9},{5... | collective-permute-start | bytes 294920 | tf_op jit(solution)/shard_map/ppermute | solution.py:313
  6.4 5.5 %collective-permute-start.2 = (bf16[128,384]{1,0:T(8,128)(2,1)S(1)}, bf16[128,384]{1,0:T(8,128)(2,1)S(1)}, u32[]{:S(2)}, u32[]{:S(2)}) collective-permute-start(bf16[128,384]{1,0:T(8,128)(2,1)S(1)} %get-tuple-element.46), channel_id=1, source_target_pairs={{0,12},{4,8},{8,4},{12,0},{16,28},{20,24},{24,20},{28,16},{1,13},{... | collective-permute-start | bytes 294920 | tf_op jit(solution)/shard_map/ppermute | solution.py:313
  12.5 5.9 %collective-permute-start.3 = (bf16[128,256]{1,0:T(8,128)(2,1)S(1)}, bf16[128,256]{1,0:T(8,128)(2,1)S(1)}, u32[]{:S(2)}, u32[]{:S(2)}) collective-permute-start(bf16[128,256]{1,0:T(8,128)(2,1)S(1)} %get-tuple-element.50), channel_id=1, source_target_pairs={{0,16},{4,20},{8,24},{12,28},{16,0},{20,4},{24,8},{28,12},{1,17},{... | collective-permute-start | bytes 196616 | tf_op jit(solution)/shard_map/ppermute | solution.py:313
  19.5 4.0 %collective-permute-start.4 = (bf16[128,128]{1,0:T(8,128)(2,1)S(1)}, bf16[128,128]{1,0:T(8,128)(2,1)S(1)}, u32[]{:S(2)}, u32[]{:S(2)}) collective-permute-start(bf16[128,128]{1,0:T(8,128)(2,1)S(1)} %get-tuple-element.55), channel_id=1, source_target_pairs={{0,4},{4,0},{8,12},{12,8},{16,20},{20,16},{24,28},{28,24},{1,5},{5... | collective-permute-start | bytes 98312 | tf_op jit(solution)/shard_map/ppermute | solution.py:313
  19.8 3.9 %collective-permute-start.5 = (bf16[128,128]{1,0:T(8,128)(2,1)S(1)}, bf16[128,128]{1,0:T(8,128)(2,1)S(1)}, u32[]{:S(2)}, u32[]{:S(2)}) collective-permute-start(bf16[128,128]{1,0:T(8,128)(2,1)S(1)} %get-tuple-element.56), channel_id=1, source_target_pairs={{0,8},{4,12},{8,0},{12,4},{16,24},{20,28},{24,16},{28,20},{1,9},{5... | collective-permute-start | bytes 98312 | tf_op jit(solution)/shard_map/ppermute | solution.py:313
  21.1 4.8 %collective-permute-start.6 = (bf16[128,128]{1,0:T(8,128)(2,1)S(1)}, bf16[128,128]{1,0:T(8,128)(2,1)S(1)}, u32[]{:S(2)}, u32[]{:S(2)}) collective-permute-start(bf16[128,128]{1,0:T(8,128)(2,1)S(1)} %get-tuple-element.57), channel_id=1, source_target_pairs={{0,12},{4,8},{8,4},{12,0},{16,28},{20,24},{24,20},{28,16},{1,13},{... | collective-permute-start | bytes 98312 | tf_op jit(solution)/shard_map/ppermute | solution.py:313
  26.3 3.3 %copy-start.1 = (bf16[128,512]{1,0:T(8,128)(2,1)S(1)}, bf16[128,512]{1,0:T(8,128)(2,1)}, u32[]{:S(2)}) copy-start(bf16[128,512]{1,0:T(8,128)(2,1)} %refs_0_.1) | copy-start | bytes 393220
  26.3 1.6 %collective-permute-start.7 = (bf16[128,1024]{1,0:T(8,128)(2,1)S(1)}, bf16[128,1024]{1,0:T(8,128)(2,1)S(1)}, u32[]{:S(2)}, u32[]{:S(2)}) collective-permute-start(bf16[128,1024]{1,0:T(8,128)(2,1)S(1)} %get-tuple-element.59), channel_id=1, source_target_pairs={{0,1},{1,0},{2,3},{3,2},{4,5},{5,4},{6,7},{7,6},{8,9},{9,8},{10,11... | collective-permute-start | bytes 786440 | tf_op jit(solution)/shard_map/ppermute | solution.py:313
  28.0 9.2 %collective-permute-start.8 = (bf16[128,1024]{1,0:T(8,128)(2,1)S(1)}, bf16[128,1024]{1,0:T(8,128)(2,1)S(1)}, u32[]{:S(2)}, u32[]{:S(2)}) collective-permute-start(bf16[128,1024]{1,0:T(8,128)(2,1)S(1)} %shard_map.109.first), channel_id=1, source_target_pairs={{0,2},{1,3},{2,0},{3,1},{4,6},{5,7},{6,4},{7,5},{8,10},{9,11},{10,... | collective-permute-start | bytes 786440 | tf_op jit(solution)/shard_map/ppermute | solution.py:313
  29.5 7.8 %collective-permute-start.10 = (bf16[128,512]{1,0:T(8,128)(2,1)S(1)}, bf16[128,512]{1,0:T(8,128)(2,1)S(1)}, u32[]{:S(2)}, u32[]{:S(2)}) collective-permute-start(bf16[128,512]{1,0:T(8,128)(2,1)S(1)} %copy-done.1), channel_id=1, source_target_pairs={{0,1},{1,0},{2,3},{3,2},{4,5},{5,4},{6,7},{7,6},{8,9},{9,8},{10,11... | collective-permute-start | bytes 393224 | tf_op jit(solution)/shard_map/ppermute | solution.py:313
  29.5 10.5 %collective-permute-start.11 = (bf16[128,512]{1,0:T(8,128)(2,1)S(1)}, bf16[128,512]{1,0:T(8,128)(2,1)S(1)}, u32[]{:S(2)}, u32[]{:S(2)}) collective-permute-start(bf16[128,512]{1,0:T(8,128)(2,1)S(1)} %copy-done.1), channel_id=1, source_target_pairs={{0,2},{1,3},{2,0},{3,1},{4,6},{5,7},{6,4},{7,5},{8,10},{9,11},{10,... | collective-permute-start | bytes 393224 | tf_op jit(solution)/shard_map/ppermute | solution.py:313
  30.0 11.1 %collective-permute-start.12 = (bf16[128,512]{1,0:T(8,128)(2,1)S(1)}, bf16[128,512]{1,0:T(8,128)(2,1)S(1)}, u32[]{:S(2)}, u32[]{:S(2)}) collective-permute-start(bf16[128,512]{1,0:T(8,128)(2,1)S(1)} %copy-done.1), channel_id=1, source_target_pairs={{0,3},{1,2},{2,1},{3,0},{4,7},{5,6},{6,5},{7,4},{8,11},{9,10},{10,... | collective-permute-start | bytes 393224 | tf_op jit(solution)/shard_map/ppermute | solution.py:313
  37.3 27.5 %collective-permute-start.9 = (bf16[128,1024]{1,0:T(8,128)(2,1)S(1)}, bf16[128,1024]{1,0:T(8,128)(2,1)S(1)}, u32[]{:S(2)}, u32[]{:S(2)}) collective-permute-start(bf16[128,1024]{1,0:T(8,128)(2,1)S(1)} %shard_map.110.mine), channel_id=1, source_target_pairs={{0,1},{1,0},{2,3},{3,2},{4,5},{5,4},{6,7},{7,6},{8,9},{9,8},{10,11... | collective-permute-start | bytes 786440 | tf_op jit(solution)/shard_map/ppermute | solution.py:313
  42.0 4.0 %collective-permute-start.13 = (bf16[128,128]{1,0:T(8,128)(2,1)S(1)}, bf16[128,128]{1,0:T(8,128)(2,1)S(1)}, u32[]{:S(2)}, u32[]{:S(2)}) collective-permute-start(bf16[128,128]{1,0:T(8,128)(2,1)S(1)} %get-tuple-element.63), channel_id=1, source_target_pairs={{0,4},{4,0},{8,12},{12,8},{16,20},{20,16},{24,28},{28,24},{1,5},{5... | collective-permute-start | bytes 98312 | tf_op jit(solution)/shard_map/ppermute | solution.py:313
  42.8 3.9 %collective-permute-start.14 = (bf16[128,128]{1,0:T(8,128)(2,1)S(1)}, bf16[128,128]{1,0:T(8,128)(2,1)S(1)}, u32[]{:S(2)}, u32[]{:S(2)}) collective-permute-start(bf16[128,128]{1,0:T(8,128)(2,1)S(1)} %get-tuple-element.64), channel_id=1, source_target_pairs={{0,8},{4,12},{8,0},{12,4},{16,24},{20,28},{24,16},{28,20},{1,9},{5... | collective-permute-start | bytes 98312 | tf_op jit(solution)/shard_map/ppermute | solution.py:313
  44.5 4.8 %collective-permute-start.15 = (bf16[128,128]{1,0:T(8,128)(2,1)S(1)}, bf16[128,128]{1,0:T(8,128)(2,1)S(1)}, u32[]{:S(2)}, u32[]{:S(2)}) collective-permute-start(bf16[128,128]{1,0:T(8,128)(2,1)S(1)} %get-tuple-element.65), channel_id=1, source_target_pairs={{0,12},{4,8},{8,4},{12,0},{16,28},{20,24},{24,20},{28,16},{1,13},{... | collective-permute-start | bytes 98312 | tf_op jit(solution)/shard_map/ppermute | solution.py:313
  50.4 5.6 %collective-permute-start.16 = (bf16[128,256]{1,0:T(8,128)(2,1)S(1)}, bf16[128,256]{1,0:T(8,128)(2,1)S(1)}, u32[]{:S(2)}, u32[]{:S(2)}) collective-permute-start(bf16[128,256]{1,0:T(8,128)(2,1)S(1)} %get-tuple-element.74), channel_id=1, source_target_pairs={{0,16},{4,20},{8,24},{12,28},{16,0},{20,4},{24,8},{28,12},{1,17},{... | collective-permute-start | bytes 196616 | tf_op jit(solution)/shard_map/ppermute | solution.py:313
  56.7 5.1 %collective-permute-start.17 = (bf16[128,384]{1,0:T(8,128)(2,1)S(1)}, bf16[128,384]{1,0:T(8,128)(2,1)S(1)}, u32[]{:S(2)}, u32[]{:S(2)}) collective-permute-start(bf16[128,384]{1,0:T(8,128)(2,1)S(1)} %get-tuple-element.76), channel_id=1, source_target_pairs={{0,4},{4,0},{8,12},{12,8},{16,20},{20,16},{24,28},{28,24},{1,5},{5... | collective-permute-start | bytes 294920 | tf_op jit(solution)/shard_map/ppermute | solution.py:313
  56.8 5.0 %collective-permute-start.18 = (bf16[128,384]{1,0:T(8,128)(2,1)S(1)}, bf16[128,384]{1,0:T(8,128)(2,1)S(1)}, u32[]{:S(2)}, u32[]{:S(2)}) collective-permute-start(bf16[128,384]{1,0:T(8,128)(2,1)S(1)} %get-tuple-element.77), channel_id=1, source_target_pairs={{0,8},{4,12},{8,0},{12,4},{16,24},{20,28},{24,16},{28,20},{1,9},{5... | collective-permute-start | bytes 294920 | tf_op jit(solution)/shard_map/ppermute | solution.py:313
  58.3 5.6 %collective-permute-start.19 = (bf16[128,384]{1,0:T(8,128)(2,1)S(1)}, bf16[128,384]{1,0:T(8,128)(2,1)S(1)}, u32[]{:S(2)}, u32[]{:S(2)}) collective-permute-start(bf16[128,384]{1,0:T(8,128)(2,1)S(1)} %get-tuple-element.78), channel_id=1, source_target_pairs={{0,12},{4,8},{8,4},{12,0},{16,28},{20,24},{24,20},{28,16},{1,13},{... | collective-permute-start | bytes 294920 | tf_op jit(solution)/shard_map/ppermute | solution.py:313

commit v3 on v2

--- a/solution.py
+++ b/solution.py
@@ -285,7 +285,7 @@
 
 
 def fast_local(plan, queries, key_rows, value_rows, out_weight, grad_out, pair_offsets, far_offsets):
-    tokens, heads, group, selected, dilation, head_groups = plan
+    tokens, heads, group, selected, dilation, _ = plan
     factor = HEAD_DIM ** (-0.5)
     width = heads * HEAD_DIM
     model = out_weight.shape[1]
@@ -315,7 +315,9 @@
     def swapped(blocks):
         return [blocks[0]] + [swap(blocks[m], "seq", m) for m in dests if m]
 
-    others = [swap(grad_out, "head", m) for m in range(1, head_groups)]
+    mates = swap(grad_out, "head", 1)
+    facing = swap(grad_out, "head", 2)
+    relayed = swap(facing, "head", 1)
 
     def opening(out):
         out[...] = jnp.zeros_like(out)
@@ -333,28 +335,40 @@
     )(opened, queries, key_rows, value_rows)
     blocks = swapped(packed)
 
+    def locate(po, fo, pair_start, far_start):
+        pair_start[...] = jnp.full(pair_start.shape, po[my_head()], jnp.int32)
+        far_start[...] = jnp.full(far_start.shape, fo[my_head()], jnp.int32)
+
+    pair_start, far_start = call(
+        locate, [shape((8, HEAD_DIM), jnp.int32)] * 2, [smem, smem], flops=10**6
+    )(pair_offsets, far_offsets)
+
+    def grad_term(w, part, mask):
+        cols = lax.axis_index("head") ^ mask
+        return matmul(part[...], w[:, pl.ds(pl.multiple_of(cols * width, width), width)], NT)
+
     def project_grad(w, *refs):
-        parts, outs, (acc,) = refs[:head_groups], refs[head_groups:-1], refs[-1:]
-        me = lax.axis_index("head")
-        for m in range(head_groups):
-            cols = pl.ds(pl.multiple_of((me ^ m) * width, width), width)
-            term = matmul(parts[m][...], w[:, cols], NT)
-            if m == 0:
-                acc[...] = term
-            else:
-                acc[...] += term
+        parts, acc = refs[:-1], refs[-1]
+        acc[...] = sum(grad_term(w, part, mask) for mask, part in enumerate(parts))
+
+    def project_last(w, acc, facing, relayed, *refs):
+        outs, (total,) = refs[:group], refs[group:]
+        total[...] = acc[...] + grad_term(w, facing, 2) + grad_term(w, relayed, 3)
         rank = seq_rank()
         for m in dests:
-            outs[m][...] = acc[:, lanes(rank ^ m)].astype(bf16)
-
+            outs[m][...] = total[:, lanes(rank ^ m)].astype(bf16)
+
+    partial_grad = call(
+        project_grad, shape((tokens, width), f32), [vmem] * 3, flops=10**8
+    )(out_weight, grad_out, mates)
     grad_blocks = swapped(
         call(
-            project_grad,
+            project_last,
             [shape((tokens, HEAD_DIM))] * group,
-            [vmem] * (1 + head_groups),
+            [vmem] * 4,
             [pltpu.VMEM((tokens, width), f32)],
             flops=10**8,
-        )(out_weight, grad_out, *others),
+        )(out_weight, partial_grad, facing, relayed),
     )
 
     def branch_scores(query, key, mask):
@@ -384,10 +398,10 @@
         return ref[at, :].astype(bf16)
 
     def pair_rows(po):
-        return pl.ds(po[my_head()], selected, stride=2)
+        return pl.ds(po[...][0, 0], selected, stride=2)
 
     def far_rows(fo):
-        return pl.ds(fo[my_head()], far_span, stride=dilation)
+        return pl.ds(fo[...][0, 0], far_span, stride=dilation)
 
     def with_early(early_kv, slot, ref, at):
         cols = slice(slot * HEAD_DIM, (slot + 1) * HEAD_DIM)
@@ -409,8 +423,8 @@
         far_kv[:, HEAD_DIM:] = pick(v, far_at)
 
     q, k, v, far_kv = call(
-        assemble, [wide] * 3 + [far_pair], [smem] + [vmem] * group, flops=10**7
-    )(far_offsets, *blocks)
+        assemble, [wide] * 3 + [far_pair], [vmem] + [vmem] * group, flops=10**7
+    )(far_start, *blocks)
     early_kv = swap(far_kv, "seq", group)
 
     def forward_near(po, q, k, v, top_all, sum_all, acc):
@@ -442,8 +456,8 @@
         sum_all[at, :] = sum_all[at, :] * old_scale + total * scale
         acc[at, :] = acc[at, :] * old_scale + numerator * scale
 
-    near = call(forward_near, [wide] * 3, [smem] + [vmem] * 3, flops=2 * 10**8)(
-        pair_offsets, q, k, v
+    near = call(forward_near, [wide] * 3, [vmem] + [vmem] * 3, flops=2 * 10**8)(
+        pair_start, q, k, v
     )
 
     def forward_far(fo, q, k, v, early_kv, near_top, near_sum, near_acc, *refs):
@@ -465,10 +479,10 @@
     *out_blocks, out_wide, lse = call(
         forward_far,
         [shape((tokens, HEAD_DIM))] * group + [wide, wide],
-        [smem] + [vmem] * 7,
+        [vmem] + [vmem] * 7,
         [scratch] * 2,
         flops=10**8,
-    )(far_offsets, q, k, v, early_kv, *near)
+    )(far_start, q, k, v, early_kv, *near)
     attended = swapped(out_blocks)
 
     def grads_of(query, key, value, grad, row_lse, row_delta, mask):
@@ -507,33 +521,39 @@
     grad, delta, far_dq, far_dk, far_dv, late_kv = call(
         backward_far,
         [wide, wide] + [far_wide] * 3 + [far_pair],
-        [smem] + [vmem] * (6 + group),
+        [vmem] + [vmem] * (6 + group),
         flops=2 * 10**8,
-    )(far_offsets, q, k, v, early_kv, out_wide, lse, *grad_blocks)
+    )(far_start, q, k, v, early_kv, out_wide, lse, *grad_blocks)
     late = swap(late_kv, "seq", group)
 
-    def backward_near(po, fo, q, k, v, grad, lse, delta, *refs):
-        fars, near = refs[:3], refs[3:]
+    def near_grads(q, k, v, grad, lse, delta, at):
         mask = causal((selected, selected))
+        return grads_of(
+            pick(q, at), pick(k, at), pick(v, at), pick(grad, at), lse[at, :], delta[at, :], mask
+        )
+
+    def backward_pair(po, q, k, v, grad, lse, delta, *outs):
+        for ref, term in zip(outs, near_grads(q, k, v, grad, lse, delta, pair_rows(po))):
+            ref[...] = term
+
+    pair_wide = shape((selected, HEAD_DIM), f32)
+    pair_grads = call(backward_pair, [pair_wide] * 3, [vmem] * 7, flops=2 * 10**8)(
+        pair_start, q, k, v, grad, lse, delta
+    )
+
+    def backward_local(po, fo, q, k, v, grad, lse, delta, *refs):
+        pairs, fars, near = refs[:3], refs[3:6], refs[6:]
         for first in range(0, span, selected):
             at = pl.ds(first, selected)
-            terms = grads_of(
-                pick(q, at), pick(k, at), pick(v, at), pick(grad, at), lse[at, :], delta[at, :], mask
-            )
-            for ref, term in zip(near, terms):
+            for ref, term in zip(near, near_grads(q, k, v, grad, lse, delta, at)):
                 ref[at, :] = term
-        at = pair_rows(po)
-        terms = grads_of(
-            pick(q, at), pick(k, at), pick(v, at), pick(grad, at), lse[at, :], delta[at, :], mask
-        )
-        for ref, term in zip(near, terms):
-            ref[at, :] += term
-        for ref, far in zip(near, fars):
+        for ref, pair, far in zip(near, pairs, fars):
+            ref[pair_rows(po), :] += pair[...]
             ref[far_rows(fo), :] += far[...]
 
-    dq, dk, dv = call(
-        backward_near, [wide] * 3, [smem, smem] + [vmem] * 9, flops=5 * 10**8
-    )(pair_offsets, far_offsets, q, k, v, grad, lse, delta, far_dq, far_dk, far_dv)
+    dq, dk, dv = call(backward_local, [wide] * 3, [vmem] * 14, flops=4 * 10**8)(
+        pair_start, far_start, q, k, v, grad, lse, delta, *pair_grads, far_dq, far_dk, far_dv
+    )
 
     def finish(fo, dq, dk, dv, late, *refs):
         outs, sums = refs[:group], refs[group:]
@@ -551,10 +571,10 @@
         call(
             finish,
             [shape((tokens, 3 * HEAD_DIM))] * group,
-            [smem] + [vmem] * 4,
+            [vmem] + [vmem] * 4,
             [scratch] * 2,
             flops=10**7,
-        )(far_offsets, dq, dk, dv, late),
+        )(far_start, dq, dk, dv, late),
     )
 
     half = model // 2
@@ -602,47 +622,38 @@
         for copy in copies:
             copy.wait()
 
-    def join(mine, theirs, out, sems):
+    def close(mine, theirs, *refs):
+        parts, out, outs, sems = refs[:group], refs[group], refs[group + 1 : group + 4], refs[-1]
+        rank = seq_rank()
+        copies = [
+            (mine, out.at[:, columns(my_half())]),
+            (theirs, out.at[:, columns(1 - my_half())]),
+        ]
+        copies += [
+            (
+                parts[m].at[:, slot * HEAD_DIM : (slot + 1) * HEAD_DIM],
+                outs[slot].at[:, lanes(rank ^ m)],
+            )
+            for m in dests
+            for slot in range(3)
+        ]
         copy_all(
             [
-                pltpu.make_async_copy(mine, out.at[:, columns(my_half())], sems.at[0]),
-                pltpu.make_async_copy(theirs, out.at[:, columns(1 - my_half())], sems.at[1]),
+                pltpu.make_async_copy(source, target, sems.at[number])
+                for number, (source, target) in enumerate(copies)
             ]
         )
 
-    layer_out = call(
-        join,
-        shape((tokens, model)),
-        [vmem] * 2,
-        [pltpu.SemaphoreType.DMA((2,))],
-        flops=10**6,
-        out_space=pltpu.HBM,
-    )(total, other)
-
-    def collect(*refs):
-        parts, outs, sems = refs[:group], refs[group : group + 3], refs[-1]
-        rank = seq_rank()
-        copy_all(
-            [
-                pltpu.make_async_copy(
-                    parts[m].at[:, slot * HEAD_DIM : (slot + 1) * HEAD_DIM],
-                    outs[slot].at[:, lanes(rank ^ m)],
-                    sems.at[m, slot],
-                )
-                for m in dests
-                for slot in range(3)
-            ]
-        )
-
-    gradients = call(
-        collect,
-        [shape((tokens, width))] * 3,
-        [vmem] * group,
-        [pltpu.SemaphoreType.DMA((group, 3))],
-        flops=10**7,
-        out_space=pltpu.HBM,
-    )(*returned)
-    return (layer_out, *gradients)
+    return tuple(
+        call(
+            close,
+            [shape((tokens, model))] + [shape((tokens, width))] * 3,
+            [vmem] * (2 + group),
+            [pltpu.SemaphoreType.DMA((2 + 3 * group,))],
+            flops=10**7,
+            out_space=pltpu.HBM,
+        )(total, other, *returned)
+    )
 
 
 def local(queries, key_rows, value_rows, out_weight, grad_out, pair_offsets, far_head_offsets):

time: 65.7 us -> 62 us (0.944)
  Pallas kernels: 9.72 us -> 6.92 us
  starting transfers between devices: 23.6 us -> 22.7 us
    pallas_call x9 -> x11, Pallas kernels: 8.89 us -> 6.09 us  [the longest x1 1.03 us: fast_local(): call(close, [shape((tokens, model))] + [shape((tokens, width))] * 3, [vme...]
    ppermute x20, starting transfers between devices: 23.6 us -> 22.7 us  [swap(): return lax.ppermute(value, axis, pairs)]
  transfers between devices with their start and end apart: 20 -> 20, of which waited for: 17 -> 17; matrix products, arithmetic and copies ran while one was open for 0% -> 0% of each run, Pallas kernels for 10% -> 8%
where the time goes in v3:
time: 62 us; the launch traced here: 61.9 us
  waiting for transfers between devices  30.4 us (49%)
  starting transfers between devices  22.7 us (37%)
  Pallas kernels  6.92 us (11%)
  local copies, waits for them, and re-layouts  1.02 us (2%)
  between operations  0.81 us (1%)
    ppermute x20, waiting for transfers between devices, swap(): return lax.ppermute(value, axis, pairs)  30.4 us
    ppermute x20, starting transfers between devices, swap(): return lax.ppermute(value, axis, pairs)  22.7 us
  transfers between devices with their start and end apart: 20, of which 17 were waited for; matrix products, arithmetic and copies ran while one was open for 0% of the time, Pallas kernels for 8%

profile of v3, /device:TPU:0, one launch (start us, length us, event | category | flops | bytes accessed | tf_op | source)
XLA Modules:
  0.0 61.9 jit_solution(12380838111458933126)
XLA Ops:
  0.7 0.9 %copy-done.2 = bf16[128,512]{1,0:T(8,128)(2,1)S(1)} copy-done((bf16[128,512]{1,0:T(8,128)(2,1)S(1)}, bf16[128,512]{1,0:T(8,128)(2,1)}, u32[]{:S(2)}) %copy-start.2) | copy-done | bytes 131096
  1.8 3.0 %collective-permute-start = (bf16[128,384]{1,0:T(8,128)(2,1)S(1)}, bf16[128,384]{1,0:T(8,128)(2,1)S(1)}, u32[]{:S(2)}, u32[]{:S(2)}) collective-permute-start(bf16[128,384]{1,0:T(8,128)(2,1)S(1)} %get-tuple-element.47), channel_id=1, source_target_pairs={{0,4},{4,0},{8,12},{12,8},{16,20},{20,16},{24,28},{28,24},{1,5},{5... | collective-permute-start | bytes 294920 | tf_op jit(solution)/shard_map/ppermute | solution.py:313
  4.8 1.6 %collective-permute-start.1 = (bf16[128,384]{1,0:T(8,128)(2,1)S(1)}, bf16[128,384]{1,0:T(8,128)(2,1)S(1)}, u32[]{:S(2)}, u32[]{:S(2)}) collective-permute-start(bf16[128,384]{1,0:T(8,128)(2,1)S(1)} %get-tuple-element.48), channel_id=1, source_target_pairs={{0,8},{4,12},{8,0},{12,4},{16,24},{20,28},{24,16},{28,20},{1,9},{5... | collective-permute-start | bytes 294920 | tf_op jit(solution)/shard_map/ppermute | solution.py:313
  6.4 0.6 shard_map.102
  6.9 0.6 %collective-permute-done.refs_1_ = bf16[128,384]{1,0:T(8,128)(2,1)S(1)} collective-permute-done((bf16[128,384]{1,0:T(8,128)(2,1)S(1)}, bf16[128,384]{1,0:T(8,128)(2,1)S(1)}, u32[]{:S(2)}, u32[]{:S(2)}) %collective-permute-start) | collective-permute-done | bytes 98336 | tf_op jit(solution)/shard_map/ppermute | solution.py:313
  7.6 2.7 %collective-permute-done.1.refs_2_ = bf16[128,384]{1,0:T(8,128)(2,1)S(1)} collective-permute-done((bf16[128,384]{1,0:T(8,128)(2,1)S(1)}, bf16[128,384]{1,0:T(8,128)(2,1)S(1)}, u32[]{:S(2)}, u32[]{:S(2)}) %collective-permute-start.1) | collective-permute-done | bytes 98336 | tf_op jit(solution)/shard_map/ppermute | solution.py:313
  10.3 1.6 %collective-permute-done.2.refs_3_ = bf16[128,384]{1,0:T(8,128)(2,1)S(1)} collective-permute-done((bf16[128,384]{1,0:T(8,128)(2,1)S(1)}, bf16[128,384]{1,0:T(8,128)(2,1)S(1)}, u32[]{:S(2)}, u32[]{:S(2)}) %collective-permute-start.2) | collective-permute-done | bytes 98336 | tf_op jit(solution)/shard_map/ppermute | solution.py:313
  11.9 0.1 shard_map.105
  12.0 2.7 %collective-permute-start.3 = (bf16[128,256]{1,0:T(8,128)(2,1)S(1)}, bf16[128,256]{1,0:T(8,128)(2,1)S(1)}, u32[]{:S(2)}, u32[]{:S(2)}) collective-permute-start(bf16[128,256]{1,0:T(8,128)(2,1)S(1)} %get-tuple-element.53), channel_id=1, source_target_pairs={{0,16},{4,20},{8,24},{12,28},{16,0},{20,4},{24,8},{28,12},{1,17},{... | collective-permute-start | bytes 196616 | tf_op jit(solution)/shard_map/ppermute | solution.py:313
  14.6 0.8 %shard_map.106 = (f32[512,128]{1,0:T(8,128)S(1)}, f32[512,128]{1,0:T(8,128)S(1)}, f32[512,128]{1,0:T(8,128)S(1)}) custom-call(s32[8,128]{1,0:T(8,128)S(1)} %get-tuple-element.54.po, f32[512,128]{1,0:T(8,128)S(1)} %get-tuple-element.50.q, f32[512,128]{1,0:T(8,128)S(1)} %get-tuple-element.51.k, f32[512,128]{1,0:T(8,128)S(1)} %get-tuple-element.52.v), custom_call_target="tpu_custom_call" | custom-call | flops 200000000 | tf_op jit(solution)/shard_map/pallas_call | solution.py:459
  15.4 2.5 %collective-permute-done.3.early_kv = bf16[128,256]{1,0:T(8,128)(2,1)S(1)} collective-permute-done((bf16[128,256]{1,0:T(8,128)(2,1)S(1)}, bf16[128,256]{1,0:T(8,128)(2,1)S(1)}, u32[]{:S(2)}, u32[]{:S(2)}) %collective-permute-start.3) | collective-permute-done | bytes 65568 | tf_op jit(solution)/shard_map/ppermute | solution.py:313
  17.9 0.5 shard_map.107
  18.4 0.3 collective-permute-start.4
  18.7 1.4 %collective-permute-start.5 = (bf16[128,128]{1,0:T(8,128)(2,1)S(1)}, bf16[128,128]{1,0:T(8,128)(2,1)S(1)}, u32[]{:S(2)}, u32[]{:S(2)}) collective-permute-start(bf16[128,128]{1,0:T(8,128)(2,1)S(1)} %get-tuple-element.60), channel_id=1, source_target_pairs={{0,8},{4,12},{8,0},{12,4},{16,24},{20,28},{24,16},{28,20},{1,9},{5... | collective-permute-start | bytes 98312 | tf_op jit(solution)/shard_map/ppermute | solution.py:313
  20.1 1.9 %collective-permute-start.6 = (bf16[128,128]{1,0:T(8,128)(2,1)S(1)}, bf16[128,128]{1,0:T(8,128)(2,1)S(1)}, u32[]{:S(2)}, u32[]{:S(2)}) collective-permute-start(bf16[128,128]{1,0:T(8,128)(2,1)S(1)} %get-tuple-element.61), channel_id=1, source_target_pairs={{0,12},{4,8},{8,4},{12,0},{16,28},{20,24},{24,20},{28,16},{1,13},{... | collective-permute-start | bytes 98312 | tf_op jit(solution)/shard_map/ppermute | solution.py:313
  22.0 0.4 collective-permute-done.4.refs_1_
  22.4 0.2 collective-permute-done.5.refs_2_
  22.7 2.3 %collective-permute-done.6.refs_3_ = bf16[128,128]{1,0:T(8,128)(2,1)S(1)} collective-permute-done((bf16[128,128]{1,0:T(8,128)(2,1)S(1)}, bf16[128,128]{1,0:T(8,128)(2,1)S(1)}, u32[]{:S(2)}, u32[]{:S(2)}) %collective-permute-start.6) | collective-permute-done | bytes 32800 | tf_op jit(solution)/shard_map/ppermute | solution.py:313
  24.9 0.3 shard_map.108
  25.3 0.1 collective-permute-start.7
  25.3 0.3 shard_map.109.first
  25.7 1.2 %collective-permute-done.7.second = bf16[128,1024]{1,0:T(8,128)(2,1)S(1)} collective-permute-done((bf16[128,1024]{1,0:T(8,128)(2,1)S(1)}, bf16[128,1024]{1,0:T(8,128)(2,1)S(1)}, u32[]{:S(2)}, u32[]{:S(2)}) %collective-permute-start.7) | collective-permute-done | bytes 262176 | tf_op jit(solution)/shard_map/ppermute | solution.py:313
  26.9 1.6 %collective-permute-start.8 = (bf16[128,1024]{1,0:T(8,128)(2,1)S(1)}, bf16[128,1024]{1,0:T(8,128)(2,1)S(1)}, u32[]{:S(2)}, u32[]{:S(2)}) collective-permute-start(bf16[128,1024]{1,0:T(8,128)(2,1)S(1)} %shard_map.110.first), channel_id=1, source_target_pairs={{0,2},{1,3},{2,0},{3,1},{4,6},{5,7},{6,4},{7,5},{8,10},{9,11},{10,... | collective-permute-start | bytes 786440 | tf_op jit(solution)/shard_map/ppermute | solution.py:313
  28.5 0.5 collective-permute-start.11
  29.0 9.1 %collective-permute-done.11.facing = bf16[128,512]{1,0:T(8,128)(2,1)S(1)} collective-permute-done((bf16[128,512]{1,0:T(8,128)(2,1)S(1)}, bf16[128,512]{1,0:T(8,128)(2,1)S(1)}, u32[]{:S(2)}, u32[]{:S(2)}) %collective-permute-start.11) | collective-permute-done | bytes 131104 | tf_op jit(solution)/shard_map/ppermute | solution.py:313
  38.2 0.6 collective-permute-start.9
  38.8 0.5 shard_map.112.acc
  39.3 0.2 collective-permute-done.12.relayed
  39.5 0.5 shard_map.113
  40.0 0.8 %collective-permute-start.13 = (bf16[128,128]{1,0:T(8,128)(2,1)S(1)}, bf16[128,128]{1,0:T(8,128)(2,1)S(1)}, u32[]{:S(2)}, u32[]{:S(2)}) collective-permute-start(bf16[128,128]{1,0:T(8,128)(2,1)S(1)} %get-tuple-element.67), channel_id=1, source_target_pairs={{0,4},{4,0},{8,12},{12,8},{16,20},{20,16},{24,28},{28,24},{1,5},{5... | collective-permute-start | bytes 98312 | tf_op jit(solution)/shard_map/ppermute | solution.py:313
  40.8 1.8 %collective-permute-start.14 = (bf16[128,128]{1,0:T(8,128)(2,1)S(1)}, bf16[128,128]{1,0:T(8,128)(2,1)S(1)}, u32[]{:S(2)}, u32[]{:S(2)}) collective-permute-start(bf16[128,128]{1,0:T(8,128)(2,1)S(1)} %get-tuple-element.68), channel_id=1, source_target_pairs={{0,8},{4,12},{8,0},{12,4},{16,24},{20,28},{24,16},{28,20},{1,9},{5... | collective-permute-start | bytes 98312 | tf_op jit(solution)/shard_map/ppermute | solution.py:313
  42.6 1.0 %collective-permute-start.15 = (bf16[128,128]{1,0:T(8,128)(2,1)S(1)}, bf16[128,128]{1,0:T(8,128)(2,1)S(1)}, u32[]{:S(2)}, u32[]{:S(2)}) collective-permute-start(bf16[128,128]{1,0:T(8,128)(2,1)S(1)} %get-tuple-element.69), channel_id=1, source_target_pairs={{0,12},{4,8},{8,4},{12,0},{16,28},{20,24},{24,20},{28,16},{1,13},{... | collective-permute-start | bytes 98312 | tf_op jit(solution)/shard_map/ppermute | solution.py:313
  43.6 0.4 collective-permute-done.13.refs_1_
  44.0 0.9 %collective-permute-done.14.refs_2_ = bf16[128,128]{1,0:T(8,128)(2,1)S(1)} collective-permute-done((bf16[128,128]{1,0:T(8,128)(2,1)S(1)}, bf16[128,128]{1,0:T(8,128)(2,1)S(1)}, u32[]{:S(2)}, u32[]{:S(2)}) %collective-permute-start.14) | collective-permute-done | bytes 32800 | tf_op jit(solution)/shard_map/ppermute | solution.py:313
  44.9 2.5 %collective-permute-done.15.refs_3_ = bf16[128,128]{1,0:T(8,128)(2,1)S(1)} collective-permute-done((bf16[128,128]{1,0:T(8,128)(2,1)S(1)}, bf16[128,128]{1,0:T(8,128)(2,1)S(1)}, u32[]{:S(2)}, u32[]{:S(2)}) %collective-permute-start.15) | collective-permute-done | bytes 32800 | tf_op jit(solution)/shard_map/ppermute | solution.py:313
  47.4 0.5 shard_map.114
  47.9 2.0 %collective-permute-start.16 = (bf16[128,256]{1,0:T(8,128)(2,1)S(1)}, bf16[128,256]{1,0:T(8,128)(2,1)S(1)}, u32[]{:S(2)}, u32[]{:S(2)}) collective-permute-start(bf16[128,256]{1,0:T(8,128)(2,1)S(1)} %get-tuple-element.81), channel_id=1, source_target_pairs={{0,16},{4,20},{8,24},{12,28},{16,0},{20,4},{24,8},{28,12},{1,17},{... | collective-permute-start | bytes 196616 | tf_op jit(solution)/shard_map/ppermute | solution.py:313
  50.0 0.6 shard_map.115
  50.5 0.9 %shard_map.116 = (f32[512,128]{1,0:T(8,128)S(1)}, f32[512,128]{1,0:T(8,128)S(1)}, f32[512,128]{1,0:T(8,128)S(1)}) custom-call(s32[8,128]{1,0:T(8,128)S(1)} %get-tuple-element.54.po, s32[8,128]{1,0:T(8,128)S(1)} %get-tuple-element.45.fo, f32[512,128]{1,0:T(8,128)S(1)} %get-tuple-element.50.q, f32[512,128]{1,0:T(8,128)S(1)} %get-tuple-element.51.k, ...), custom_call_target="tpu_custom_call" | custom-call | flops 400000000 | tf_op jit(solution)/shard_map/pallas_call | solution.py:554
  51.5 2.1 %collective-permute-done.16.late = bf16[128,256]{1,0:T(8,128)(2,1)S(1)} collective-permute-done((bf16[128,256]{1,0:T(8,128)(2,1)S(1)}, bf16[128,256]{1,0:T(8,128)(2,1)S(1)}, u32[]{:S(2)}, u32[]{:S(2)}) %collective-permute-start.16) | collective-permute-done | bytes 65568 | tf_op jit(solution)/shard_map/ppermute | solution.py:313
  53.5 0.1 shard_map.117
  53.6 0.1 collective-permute-start.17
  53.7 1.6 %collective-permute-start.18 = (bf16[128,384]{1,0:T(8,128)(2,1)S(1)}, bf16[128,384]{1,0:T(8,128)(2,1)S(1)}, u32[]{:S(2)}, u32[]{:S(2)}) collective-permute-start(bf16[128,384]{1,0:T(8,128)(2,1)S(1)} %get-tuple-element.84), channel_id=1, source_target_pairs={{0,8},{4,12},{8,0},{12,4},{16,24},{20,28},{24,16},{28,20},{1,9},{5... | collective-permute-start | bytes 294920 | tf_op jit(solution)/shard_map/ppermute | solution.py:313
  55.3 1.9 %collective-permute-start.19 = (bf16[128,384]{1,0:T(8,128)(2,1)S(1)}, bf16[128,384]{1,0:T(8,128)(2,1)S(1)}, u32[]{:S(2)}, u32[]{:S(2)}) collective-permute-start(bf16[128,384]{1,0:T(8,128)(2,1)S(1)} %get-tuple-element.85), channel_id=1, source_target_pairs={{0,12},{4,8},{8,4},{12,0},{16,28},{20,24},{24,20},{28,16},{1,13},{... | collective-permute-start | bytes 294920 | tf_op jit(solution)/shard_map/ppermute | solution.py:313
  57.2 1.1 %collective-permute-done.17.refs_1_ = bf16[128,384]{1,0:T(8,128)(2,1)S(1)} collective-permute-done((bf16[128,384]{1,0:T(8,128)(2,1)S(1)}, bf16[128,384]{1,0:T(8,128)(2,1)S(1)}, u32[]{:S(2)}, u32[]{:S(2)}) %collective-permute-start.17) | collective-permute-done | bytes 98336 | tf_op jit(solution)/shard_map/ppermute | solution.py:313
  58.3 0.1 collective-permute-done.18.refs_2_
  58.4 2.4 %collective-permute-done.19.refs_3_ = bf16[128,384]{1,0:T(8,128)(2,1)S(1)} collective-permute-done((bf16[128,384]{1,0:T(8,128)(2,1)S(1)}, bf16[128,384]{1,0:T(8,128)(2,1)S(1)}, u32[]{:S(2)}, u32[]{:S(2)}) %collective-permute-start.19) | collective-permute-done | bytes 98336 | tf_op jit(solution)/shard_map/ppermute | solution.py:313
  60.8 1.0 %shard_map.118 = (bf16[128,2048]{1,0:T(8,128)(2,1)}, bf16[128,512]{1,0:T(8,128)(2,1)}, bf16[128,512]{1,0:T(8,128)(2,1)}, bf16[128,512]{1,0:T(8,128)(2,1)}) custom-call(bf16[128,1024]{1,0:T(8,128)(2,1)S(1)} %shard_map.111.mine, bf16[128,1024]{1,0:T(8,128)(2,1)S(1)} %collective-permute-done.9.theirs, bf16[128,384]{1,0:T(8,128)(2,1)S(1)} %get-tuple-element.82.refs_0_, ...), custom_call_target="tpu_custom_call" | custom-call | flops 10000000 | tf_op jit(solution)/shard_map/pallas_call | solution.py:648
  (23 shorter events, 0.4 us)
Async XLA Ops:
  0.6 0.9 %copy-start.2 = (bf16[128,512]{1,0:T(8,128)(2,1)S(1)}, bf16[128,512]{1,0:T(8,128)(2,1)}, u32[]{:S(2)}) copy-start(bf16[128,512]{1,0:T(8,128)(2,1)} %q.1) | copy-start | bytes 393220
  0.6 1.0 %copy-start.3 = (bf16[128,512]{1,0:T(8,128)(2,1)S(1)}, bf16[128,512]{1,0:T(8,128)(2,1)}, u32[]{:S(2)}) copy-start(bf16[128,512]{1,0:T(8,128)(2,1)} %k.1) | copy-start | bytes 393220
  0.7 1.0 %copy-start.4 = (bf16[128,512]{1,0:T(8,128)(2,1)S(1)}, bf16[128,512]{1,0:T(8,128)(2,1)}, u32[]{:S(2)}) copy-start(bf16[128,512]{1,0:T(8,128)(2,1)} %v.1) | copy-start | bytes 393220
  1.7 4.7 %copy-start.5 = (s32[16]{0:T(128)S(1)}, s32[16]{0:T(128)}, u32[]{:S(2)}) copy-start(s32[16]{0:T(128)} %po.1) | copy-start | bytes 196
  1.7 4.7 %copy-start.6 = (s32[16]{0:T(128)S(1)}, s32[16]{0:T(128)}, u32[]{:S(2)}) copy-start(s32[16]{0:T(128)} %fo.1) | copy-start | bytes 196
  1.7 23.2 %copy-start = (bf16[512,2048]{1,0:T(8,128)(2,1)S(1)}, bf16[512,2048]{1,0:T(8,128)(2,1)}, u32[]{:S(2)}) copy-start(bf16[512,2048]{1,0:T(8,128)(2,1)} %w.7) | copy-start | bytes 6291460
  1.8 5.8 %collective-permute-start = (bf16[128,384]{1,0:T(8,128)(2,1)S(1)}, bf16[128,384]{1,0:T(8,128)(2,1)S(1)}, u32[]{:S(2)}, u32[]{:S(2)}) collective-permute-start(bf16[128,384]{1,0:T(8,128)(2,1)S(1)} %get-tuple-element.47), channel_id=1, source_target_pairs={{0,4},{4,0},{8,12},{12,8},{16,20},{20,16},{24,28},{28,24},{1,5},{5... | collective-permute-start | bytes 294920 | tf_op jit(solution)/shard_map/ppermute | solution.py:313
  4.8 5.5 %collective-permute-start.1 = (bf16[128,384]{1,0:T(8,128)(2,1)S(1)}, bf16[128,384]{1,0:T(8,128)(2,1)S(1)}, u32[]{:S(2)}, u32[]{:S(2)}) collective-permute-start(bf16[128,384]{1,0:T(8,128)(2,1)S(1)} %get-tuple-element.48), channel_id=1, source_target_pairs={{0,8},{4,12},{8,0},{12,4},{16,24},{20,28},{24,16},{28,20},{1,9},{5... | collective-permute-start | bytes 294920 | tf_op jit(solution)/shard_map/ppermute | solution.py:313
  6.4 5.5 %collective-permute-start.2 = (bf16[128,384]{1,0:T(8,128)(2,1)S(1)}, bf16[128,384]{1,0:T(8,128)(2,1)S(1)}, u32[]{:S(2)}, u32[]{:S(2)}) collective-permute-start(bf16[128,384]{1,0:T(8,128)(2,1)S(1)} %get-tuple-element.49), channel_id=1, source_target_pairs={{0,12},{4,8},{8,4},{12,0},{16,28},{20,24},{24,20},{28,16},{1,13},{... | collective-permute-start | bytes 294920 | tf_op jit(solution)/shard_map/ppermute | solution.py:313
  12.0 5.9 %collective-permute-start.3 = (bf16[128,256]{1,0:T(8,128)(2,1)S(1)}, bf16[128,256]{1,0:T(8,128)(2,1)S(1)}, u32[]{:S(2)}, u32[]{:S(2)}) collective-permute-start(bf16[128,256]{1,0:T(8,128)(2,1)S(1)} %get-tuple-element.53), channel_id=1, source_target_pairs={{0,16},{4,20},{8,24},{12,28},{16,0},{20,4},{24,8},{28,12},{1,17},{... | collective-permute-start | bytes 196616 | tf_op jit(solution)/shard_map/ppermute | solution.py:313
  18.4 4.0 %collective-permute-start.4 = (bf16[128,128]{1,0:T(8,128)(2,1)S(1)}, bf16[128,128]{1,0:T(8,128)(2,1)S(1)}, u32[]{:S(2)}, u32[]{:S(2)}) collective-permute-start(bf16[128,128]{1,0:T(8,128)(2,1)S(1)} %get-tuple-element.59), channel_id=1, source_target_pairs={{0,4},{4,0},{8,12},{12,8},{16,20},{20,16},{24,28},{28,24},{1,5},{5... | collective-permute-start | bytes 98312 | tf_op jit(solution)/shard_map/ppermute | solution.py:313
  18.7 3.9 %collective-permute-start.5 = (bf16[128,128]{1,0:T(8,128)(2,1)S(1)}, bf16[128,128]{1,0:T(8,128)(2,1)S(1)}, u32[]{:S(2)}, u32[]{:S(2)}) collective-permute-start(bf16[128,128]{1,0:T(8,128)(2,1)S(1)} %get-tuple-element.60), channel_id=1, source_target_pairs={{0,8},{4,12},{8,0},{12,4},{16,24},{20,28},{24,16},{28,20},{1,9},{5... | collective-permute-start | bytes 98312 | tf_op jit(solution)/shard_map/ppermute | solution.py:313
  20.1 4.8 %collective-permute-start.6 = (bf16[128,128]{1,0:T(8,128)(2,1)S(1)}, bf16[128,128]{1,0:T(8,128)(2,1)S(1)}, u32[]{:S(2)}, u32[]{:S(2)}) collective-permute-start(bf16[128,128]{1,0:T(8,128)(2,1)S(1)} %get-tuple-element.61), channel_id=1, source_target_pairs={{0,12},{4,8},{8,4},{12,0},{16,28},{20,24},{24,20},{28,16},{1,13},{... | collective-permute-start | bytes 98312 | tf_op jit(solution)/shard_map/ppermute | solution.py:313
  25.2 3.3 %copy-start.1 = (bf16[128,512]{1,0:T(8,128)(2,1)S(1)}, bf16[128,512]{1,0:T(8,128)(2,1)}, u32[]{:S(2)}) copy-start(bf16[128,512]{1,0:T(8,128)(2,1)} %refs_0_.1) | copy-start | bytes 393220
  25.3 1.6 %collective-permute-start.7 = (bf16[128,1024]{1,0:T(8,128)(2,1)S(1)}, bf16[128,1024]{1,0:T(8,128)(2,1)S(1)}, u32[]{:S(2)}, u32[]{:S(2)}) collective-permute-start(bf16[128,1024]{1,0:T(8,128)(2,1)S(1)} %get-tuple-element.63), channel_id=1, source_target_pairs={{0,1},{1,0},{2,3},{3,2},{4,5},{5,4},{6,7},{7,6},{8,9},{9,8},{10,11... | collective-permute-start | bytes 786440 | tf_op jit(solution)/shard_map/ppermute | solution.py:313
  26.9 11.2 %collective-permute-start.8 = (bf16[128,1024]{1,0:T(8,128)(2,1)S(1)}, bf16[128,1024]{1,0:T(8,128)(2,1)S(1)}, u32[]{:S(2)}, u32[]{:S(2)}) collective-permute-start(bf16[128,1024]{1,0:T(8,128)(2,1)S(1)} %shard_map.110.first), channel_id=1, source_target_pairs={{0,2},{1,3},{2,0},{3,1},{4,6},{5,7},{6,4},{7,5},{8,10},{9,11},{10,... | collective-permute-start | bytes 786440 | tf_op jit(solution)/shard_map/ppermute | solution.py:313
  28.5 9.6 %collective-permute-start.11 = (bf16[128,512]{1,0:T(8,128)(2,1)S(1)}, bf16[128,512]{1,0:T(8,128)(2,1)S(1)}, u32[]{:S(2)}, u32[]{:S(2)}) collective-permute-start(bf16[128,512]{1,0:T(8,128)(2,1)S(1)} %copy-done.1), channel_id=1, source_target_pairs={{0,2},{1,3},{2,0},{3,1},{4,6},{5,7},{6,4},{7,5},{8,10},{9,11},{10,... | collective-permute-start | bytes 393224 | tf_op jit(solution)/shard_map/ppermute | solution.py:313
  29.0 9.8 %collective-permute-start.10 = (bf16[128,512]{1,0:T(8,128)(2,1)S(1)}, bf16[128,512]{1,0:T(8,128)(2,1)S(1)}, u32[]{:S(2)}, u32[]{:S(2)}) collective-permute-start(bf16[128,512]{1,0:T(8,128)(2,1)S(1)} %copy-done.1), channel_id=1, source_target_pairs={{0,1},{1,0},{2,3},{3,2},{4,5},{5,4},{6,7},{7,6},{8,9},{9,8},{10,11... | collective-permute-start | bytes 393224 | tf_op jit(solution)/shard_map/ppermute | solution.py:313
  38.1 1.3 %collective-permute-start.12 = (bf16[128,512]{1,0:T(8,128)(2,1)S(1)}, bf16[128,512]{1,0:T(8,128)(2,1)S(1)}, u32[]{:S(2)}, u32[]{:S(2)}) collective-permute-start(bf16[128,512]{1,0:T(8,128)(2,1)S(1)} %collective-permute-done.11.facing), channel_id=1, source_target_pairs={{0,1},{1,0},{2,3},{3,2},{4,5},{5,4},{6,7},{7,6},{8,9},{9,8},{10,11... | collective-permute-start | bytes 393224 | tf_op jit(solution)/shard_map/ppermute | solution.py:313
  38.2 22.6 %collective-permute-start.9 = (bf16[128,1024]{1,0:T(8,128)(2,1)S(1)}, bf16[128,1024]{1,0:T(8,128)(2,1)S(1)}, u32[]{:S(2)}, u32[]{:S(2)}) collective-permute-start(bf16[128,1024]{1,0:T(8,128)(2,1)S(1)} %shard_map.111.mine), channel_id=1, source_target_pairs={{0,1},{1,0},{2,3},{3,2},{4,5},{5,4},{6,7},{7,6},{8,9},{9,8},{10,11... | collective-permute-start | bytes 786440 | tf_op jit(solution)/shard_map/ppermute | solution.py:313
  40.0 4.0 %collective-permute-start.13 = (bf16[128,128]{1,0:T(8,128)(2,1)S(1)}, bf16[128,128]{1,0:T(8,128)(2,1)S(1)}, u32[]{:S(2)}, u32[]{:S(2)}) collective-permute-start(bf16[128,128]{1,0:T(8,128)(2,1)S(1)} %get-tuple-element.67), channel_id=1, source_target_pairs={{0,4},{4,0},{8,12},{12,8},{16,20},{20,16},{24,28},{28,24},{1,5},{5... | collective-permute-start | bytes 98312 | tf_op jit(solution)/shard_map/ppermute | solution.py:313
  40.8 4.1 %collective-permute-start.14 = (bf16[128,128]{1,0:T(8,128)(2,1)S(1)}, bf16[128,128]{1,0:T(8,128)(2,1)S(1)}, u32[]{:S(2)}, u32[]{:S(2)}) collective-permute-start(bf16[128,128]{1,0:T(8,128)(2,1)S(1)} %get-tuple-element.68), channel_id=1, source_target_pairs={{0,8},{4,12},{8,0},{12,4},{16,24},{20,28},{24,16},{28,20},{1,9},{5... | collective-permute-start | bytes 98312 | tf_op jit(solution)/shard_map/ppermute | solution.py:313
  42.6 4.8 %collective-permute-start.15 = (bf16[128,128]{1,0:T(8,128)(2,1)S(1)}, bf16[128,128]{1,0:T(8,128)(2,1)S(1)}, u32[]{:S(2)}, u32[]{:S(2)}) collective-permute-start(bf16[128,128]{1,0:T(8,128)(2,1)S(1)} %get-tuple-element.69), channel_id=1, source_target_pairs={{0,12},{4,8},{8,4},{12,0},{16,28},{20,24},{24,20},{28,16},{1,13},{... | collective-permute-start | bytes 98312 | tf_op jit(solution)/shard_map/ppermute | solution.py:313
  47.9 5.6 %collective-permute-start.16 = (bf16[128,256]{1,0:T(8,128)(2,1)S(1)}, bf16[128,256]{1,0:T(8,128)(2,1)S(1)}, u32[]{:S(2)}, u32[]{:S(2)}) collective-permute-start(bf16[128,256]{1,0:T(8,128)(2,1)S(1)} %get-tuple-element.81), channel_id=1, source_target_pairs={{0,16},{4,20},{8,24},{12,28},{16,0},{20,4},{24,8},{28,12},{1,17},{... | collective-permute-start | bytes 196616 | tf_op jit(solution)/shard_map/ppermute | solution.py:313
  53.6 4.7 %collective-permute-start.17 = (bf16[128,384]{1,0:T(8,128)(2,1)S(1)}, bf16[128,384]{1,0:T(8,128)(2,1)S(1)}, u32[]{:S(2)}, u32[]{:S(2)}) collective-permute-start(bf16[128,384]{1,0:T(8,128)(2,1)S(1)} %get-tuple-element.83), channel_id=1, source_target_pairs={{0,4},{4,0},{8,12},{12,8},{16,20},{20,16},{24,28},{28,24},{1,5},{5... | collective-permute-start | bytes 294920 | tf_op jit(solution)/shard_map/ppermute | solution.py:313
  53.7 4.7 %collective-permute-start.18 = (bf16[128,384]{1,0:T(8,128)(2,1)S(1)}, bf16[128,384]{1,0:T(8,128)(2,1)S(1)}, u32[]{:S(2)}, u32[]{:S(2)}) collective-permute-start(bf16[128,384]{1,0:T(8,128)(2,1)S(1)} %get-tuple-element.84), channel_id=1, source_target_pairs={{0,8},{4,12},{8,0},{12,4},{16,24},{20,28},{24,16},{28,20},{1,9},{5... | collective-permute-start | bytes 294920 | tf_op jit(solution)/shard_map/ppermute | solution.py:313
  55.3 5.6 %collective-permute-start.19 = (bf16[128,384]{1,0:T(8,128)(2,1)S(1)}, bf16[128,384]{1,0:T(8,128)(2,1)S(1)}, u32[]{:S(2)}, u32[]{:S(2)}) collective-permute-start(bf16[128,384]{1,0:T(8,128)(2,1)S(1)} %get-tuple-element.85), channel_id=1, source_target_pairs={{0,12},{4,8},{8,4},{12,0},{16,28},{20,24},{24,20},{28,16},{1,13},{... | collective-permute-start | bytes 294920 | tf_op jit(solution)/shard_map/ppermute | solution.py:313

commit v4 on v3

--- a/solution.py
+++ b/solution.py
@@ -271,7 +271,7 @@
 TN = ((0,), (0,))
 
 
-def call(body, out_shape, in_specs, scratch=(), flops=0, out_space=pltpu.VMEM, limit=40):
+def call(body, out_shape, in_specs, scratch=(), flops=0, out_space=pltpu.VMEM, limit=40, aliases=None):
     out_spec = pl.BlockSpec(memory_space=out_space)
     return pl.pallas_call(
         body,
@@ -279,6 +279,7 @@
         in_specs=in_specs,
         out_specs=jax.tree.map(lambda _: out_spec, out_shape),
         scratch_shapes=list(scratch),
+        input_output_aliases=aliases or {},
         cost_estimate=pl.CostEstimate(flops=flops, bytes_accessed=0, transcendentals=0),
         compiler_params=pltpu.CompilerParams(vmem_limit_bytes=limit * 2**20 if limit else None),
     )
@@ -427,50 +428,58 @@
     )(far_start, *blocks)
     early_kv = swap(far_kv, "seq", group)
 
-    def forward_near(po, q, k, v, top_all, sum_all, acc):
+    def near_rows(po, q, k, v, out, lse):
         mask = causal((selected, selected))
         for first in range(0, span, selected):
             at = pl.ds(first, selected)
             top, total, numerator = stats(
                 branch_scores(pick(q, at), pick(k, at), mask), pick(v, at)
             )
-            top_all[at, :] = spread_lanes(top)
-            sum_all[at, :] = spread_lanes(total)
-            acc[at, :] = numerator
+            out[at, :] = numerator / total
+            lse[at, :] = spread_lanes(top + jnp.log(total))
+        at = pair_rows(po)
         merge(
-            pair_rows(po),
-            stats(
-                branch_scores(pick(q, pair_rows(po)), pick(k, pair_rows(po)), mask),
-                pick(v, pair_rows(po)),
-            ),
-            (top_all, sum_all, acc),
+            at, stats(branch_scores(pick(q, at), pick(k, at), mask), pick(v, at)), out, lse
         )
 
-    def merge(at, branch, totals):
+    def merge(at, branch, out, lse):
         top, total, numerator = branch
-        top_all, sum_all, acc = totals
-        old_top = top_all[at, :]
-        new_top = jnp.maximum(old_top, spread_lanes(top))
-        old_scale, scale = jnp.exp(old_top - new_top), jnp.exp(top - new_top)
-        top_all[at, :] = new_top
-        sum_all[at, :] = sum_all[at, :] * old_scale + total * scale
-        acc[at, :] = acc[at, :] * old_scale + numerator * scale
-
-    near = call(forward_near, [wide] * 3, [vmem] + [vmem] * 3, flops=2 * 10**8)(
-        pair_start, q, k, v
-    )
-
-    def forward_far(fo, q, k, v, early_kv, near_top, near_sum, near_acc, *refs):
-        outs, (out_wide, lse, top_all, sum_all) = refs[:group], refs[group:]
-        far_at = far_rows(fo)
-        top_all[...] = near_top[...]
-        sum_all[...] = near_sum[...]
-        out_wide[...] = near_acc[...]
-        key, value = with_early(early_kv, 0, k, far_at), with_early(early_kv, 1, v, far_at)
-        branch = stats(branch_scores(pick(q, far_at), key, far_mask()), value)
-        merge(far_at, branch, (top_all, sum_all, out_wide))
-        out_wide[...] = out_wide[...] / sum_all[...]
-        lse[...] = top_all[...] + jnp.log(sum_all[...])
+        old, new = lse[at, :], spread_lanes(top + jnp.log(total))
+        peak = jnp.maximum(old, new)
+        merged = peak + jnp.log(jnp.exp(old - peak) + jnp.exp(new - peak))
+        out[at, :] = out[at, :] * jnp.exp(old - merged) + numerator / total * jnp.exp(new - merged)
+        lse[at, :] = merged
+
+    def forward_near(po, fo, q, k, v, out, lse):
+        @pl.when(late_half() == 0)
+        def _():
+            near_rows(po, q, k, v, out, lse)
+            at = far_rows(fo)
+            scores = branch_scores(pick(q, at), pick(k, at), causal((far_span, far_span)))
+            merge(at, stats(scores, pick(v, at)), out, lse)
+
+    def forward_next(po, q, k, v, _, __, out, lse):
+        @pl.when(late_half() > 0)
+        def _():
+            near_rows(po, q, k, v, out, lse)
+
+    near = call(forward_near, [wide] * 2, [vmem] * 5, flops=2 * 10**8)(
+        pair_start, far_start, q, k, v
+    )
+    near = call(
+        forward_next, [wide] * 2, [vmem] * 6, flops=2 * 10**8, aliases={4: 0, 5: 1}
+    )(pair_start, q, k, v, *near)
+
+    def forward_far(fo, q, k, v, early_kv, _, __, *refs):
+        outs, (out_wide, lse) = refs[:group], refs[group:]
+
+        @pl.when(late_half() > 0)
+        def _():
+            at = far_rows(fo)
+            key, value = with_early(early_kv, 0, k, at), with_early(early_kv, 1, v, at)
+            scores = branch_scores(pick(q, at), key, causal((far_span, 2 * far_span), far_span))
+            merge(at, stats(scores, value), out_wide, lse)
+
         rank = seq_rank()
         for m in dests:
             outs[m][...] = out_wide[rows(rank ^ m, tokens), :].astype(bf16)
@@ -479,9 +488,9 @@
     *out_blocks, out_wide, lse = call(
         forward_far,
         [shape((tokens, HEAD_DIM))] * group + [wide, wide],
-        [vmem] + [vmem] * 7,
-        [scratch] * 2,
+        [vmem] * 7,
         flops=10**8,
+        aliases={5: group, 6: group + 1},
     )(far_start, q, k, v, early_kv, *near)
     attended = swapped(out_blocks)
 
@@ -622,14 +631,10 @@
         for copy in copies:
             copy.wait()
 
-    def close(mine, theirs, *refs):
+    def close(mine, *refs):
         parts, out, outs, sems = refs[:group], refs[group], refs[group + 1 : group + 4], refs[-1]
         rank = seq_rank()
-        copies = [
-            (mine, out.at[:, columns(my_half())]),
-            (theirs, out.at[:, columns(1 - my_half())]),
-        ]
-        copies += [
+        copies = [(mine, out.at[:, columns(my_half())])] + [
             (
                 parts[m].at[:, slot * HEAD_DIM : (slot + 1) * HEAD_DIM],
                 outs[slot].at[:, lanes(rank ^ m)],
@@ -644,16 +649,28 @@
             ]
         )
 
-    return tuple(
-        call(
-            close,
-            [shape((tokens, model))] + [shape((tokens, width))] * 3,
-            [vmem] * (2 + group),
-            [pltpu.SemaphoreType.DMA((2 + 3 * group,))],
-            flops=10**7,
-            out_space=pltpu.HBM,
-        )(total, other, *returned)
-    )
+    half_layer, *gradients = call(
+        close,
+        [shape((tokens, model))] + [shape((tokens, width))] * 3,
+        [vmem] * (1 + group),
+        [pltpu.SemaphoreType.DMA((1 + 3 * group,))],
+        flops=10**7,
+        out_space=pltpu.HBM,
+    )(total, *returned)
+
+    def join(theirs, _, out, sem):
+        copy_all([pltpu.make_async_copy(theirs, out.at[:, columns(1 - my_half())], sem)])
+
+    layer_out = call(
+        join,
+        shape((tokens, model)),
+        [vmem, pl.BlockSpec(memory_space=pltpu.HBM)],
+        [pltpu.SemaphoreType.DMA],
+        flops=10**6,
+        out_space=pltpu.HBM,
+        aliases={1: 0},
+    )(other, half_layer)
+    return (layer_out, *gradients)
 
 
 def local(queries, key_rows, value_rows, out_weight, grad_out, pair_offsets, far_head_offsets):

time: 62 us -> 62.6 us (level)
    pallas_call x1 -> x3, Pallas kernels: 0.78 us -> 1.67 us  [the longest x1 0.92 us: fast_local(): call(forward_near, [wide] * 2, [vmem] * 5, flops=2 * 10 ** 8)]
  transfers between devices with their start and end apart: 20 -> 20, of which waited for: 17 -> 17; matrix products, arithmetic and copies ran while one was open for 0% -> 0% of each run, Pallas kernels for 8% -> 10%
where the time goes in v4:
time: 62.6 us; the launch traced here: 62.4 us
  waiting for transfers between devices  30.2 us (48%)
  starting transfers between devices  23.1 us (37%)
  Pallas kernels  7.22 us (12%)
  local copies, waits for them, and re-layouts  1.02 us (2%)
  between operations  0.84 us (1%)
    ppermute x20, waiting for transfers between devices, swap(): return lax.ppermute(value, axis, pairs)  30.2 us
    ppermute x20, starting transfers between devices, swap(): return lax.ppermute(value, axis, pairs)  23.1 us
  transfers between devices with their start and end apart: 20, of which 17 were waited for; matrix products, arithmetic and copies ran while one was open for 0% of the time, Pallas kernels for 10%

profile of v4, /device:TPU:0, one launch (start us, length us, event | category | flops | bytes accessed | tf_op | source)
XLA Modules:
  0.0 62.4 jit_solution(12948708864476598008)
XLA Ops:
  0.7 0.9 %copy-done.2 = bf16[128,512]{1,0:T(8,128)(2,1)S(1)} copy-done((bf16[128,512]{1,0:T(8,128)(2,1)S(1)}, bf16[128,512]{1,0:T(8,128)(2,1)}, u32[]{:S(2)}) %copy-start.2) | copy-done | bytes 131096
  1.8 3.0 %collective-permute-start = (bf16[128,384]{1,0:T(8,128)(2,1)S(1)}, bf16[128,384]{1,0:T(8,128)(2,1)S(1)}, u32[]{:S(2)}, u32[]{:S(2)}) collective-permute-start(bf16[128,384]{1,0:T(8,128)(2,1)S(1)} %get-tuple-element.52), channel_id=1, source_target_pairs={{0,4},{4,0},{8,12},{12,8},{16,20},{20,16},{24,28},{28,24},{1,5},{5... | collective-permute-start | bytes 294920 | tf_op jit(solution)/shard_map/ppermute | solution.py:314
  4.8 1.6 %collective-permute-start.1 = (bf16[128,384]{1,0:T(8,128)(2,1)S(1)}, bf16[128,384]{1,0:T(8,128)(2,1)S(1)}, u32[]{:S(2)}, u32[]{:S(2)}) collective-permute-start(bf16[128,384]{1,0:T(8,128)(2,1)S(1)} %get-tuple-element.53), channel_id=1, source_target_pairs={{0,8},{4,12},{8,0},{12,4},{16,24},{20,28},{24,16},{28,20},{1,9},{5... | collective-permute-start | bytes 294920 | tf_op jit(solution)/shard_map/ppermute | solution.py:314
  6.4 0.6 shard_map.102
  6.9 0.6 %collective-permute-done.refs_1_ = bf16[128,384]{1,0:T(8,128)(2,1)S(1)} collective-permute-done((bf16[128,384]{1,0:T(8,128)(2,1)S(1)}, bf16[128,384]{1,0:T(8,128)(2,1)S(1)}, u32[]{:S(2)}, u32[]{:S(2)}) %collective-permute-start) | collective-permute-done | bytes 98336 | tf_op jit(solution)/shard_map/ppermute | solution.py:314
  7.6 2.7 %collective-permute-done.1.refs_2_ = bf16[128,384]{1,0:T(8,128)(2,1)S(1)} collective-permute-done((bf16[128,384]{1,0:T(8,128)(2,1)S(1)}, bf16[128,384]{1,0:T(8,128)(2,1)S(1)}, u32[]{:S(2)}, u32[]{:S(2)}) %collective-permute-start.1) | collective-permute-done | bytes 98336 | tf_op jit(solution)/shard_map/ppermute | solution.py:314
  10.3 1.6 %collective-permute-done.2.refs_3_ = bf16[128,384]{1,0:T(8,128)(2,1)S(1)} collective-permute-done((bf16[128,384]{1,0:T(8,128)(2,1)S(1)}, bf16[128,384]{1,0:T(8,128)(2,1)S(1)}, u32[]{:S(2)}, u32[]{:S(2)}) %collective-permute-start.2) | collective-permute-done | bytes 98336 | tf_op jit(solution)/shard_map/ppermute | solution.py:314
  11.9 0.1 shard_map.105
  12.0 2.7 %collective-permute-start.3 = (bf16[128,256]{1,0:T(8,128)(2,1)S(1)}, bf16[128,256]{1,0:T(8,128)(2,1)S(1)}, u32[]{:S(2)}, u32[]{:S(2)}) collective-permute-start(bf16[128,256]{1,0:T(8,128)(2,1)S(1)} %get-tuple-element.58), channel_id=1, source_target_pairs={{0,16},{4,20},{8,24},{12,28},{16,0},{20,4},{24,8},{28,12},{1,17},{... | collective-permute-start | bytes 196616 | tf_op jit(solution)/shard_map/ppermute | solution.py:314
  14.6 0.9 %shard_map.106 = (f32[512,128]{1,0:T(8,128)S(1)}, f32[512,128]{1,0:T(8,128)S(1)}) custom-call(s32[8,128]{1,0:T(8,128)S(1)} %get-tuple-element.59.po, s32[8,128]{1,0:T(8,128)S(1)} %get-tuple-element.50.fo, f32[512,128]{1,0:T(8,128)S(1)} %get-tuple-element.55.q, f32[512,128]{1,0:T(8,128)S(1)} %get-tuple-element.56.k, f32[512,128]{1,0:T(8,128)S(1)} %get-tuple-element.57.v), custom_call_target="tpu_custom_call" | custom-call | flops 200000000 | tf_op jit(solution)/shard_map/pallas_call | solution.py:466
  15.6 2.3 %collective-permute-done.3.early_kv = bf16[128,256]{1,0:T(8,128)(2,1)S(1)} collective-permute-done((bf16[128,256]{1,0:T(8,128)(2,1)S(1)}, bf16[128,256]{1,0:T(8,128)(2,1)S(1)}, u32[]{:S(2)}, u32[]{:S(2)}) %collective-permute-start.3) | collective-permute-done | bytes 65568 | tf_op jit(solution)/shard_map/ppermute | solution.py:314
  17.9 0.3 collective-permute-start.4
  18.2 1.4 %collective-permute-start.5 = (bf16[128,128]{1,0:T(8,128)(2,1)S(1)}, bf16[128,128]{1,0:T(8,128)(2,1)S(1)}, u32[]{:S(2)}, u32[]{:S(2)}) collective-permute-start(bf16[128,128]{1,0:T(8,128)(2,1)S(1)} %get-tuple-element.66), channel_id=1, source_target_pairs={{0,8},{4,12},{8,0},{12,4},{16,24},{20,28},{24,16},{28,20},{1,9},{5... | collective-permute-start | bytes 98312 | tf_op jit(solution)/shard_map/ppermute | solution.py:314
  19.6 1.9 %collective-permute-start.6 = (bf16[128,128]{1,0:T(8,128)(2,1)S(1)}, bf16[128,128]{1,0:T(8,128)(2,1)S(1)}, u32[]{:S(2)}, u32[]{:S(2)}) collective-permute-start(bf16[128,128]{1,0:T(8,128)(2,1)S(1)} %get-tuple-element.67), channel_id=1, source_target_pairs={{0,12},{4,8},{8,4},{12,0},{16,28},{20,24},{24,20},{28,16},{1,13},{... | collective-permute-start | bytes 98312 | tf_op jit(solution)/shard_map/ppermute | solution.py:314
  21.5 0.4 collective-permute-done.4.refs_1_
  21.9 0.2 collective-permute-done.5.refs_2_
  22.2 2.3 %collective-permute-done.6.refs_3_ = bf16[128,128]{1,0:T(8,128)(2,1)S(1)} collective-permute-done((bf16[128,128]{1,0:T(8,128)(2,1)S(1)}, bf16[128,128]{1,0:T(8,128)(2,1)S(1)}, u32[]{:S(2)}, u32[]{:S(2)}) %collective-permute-start.6) | collective-permute-done | bytes 32800 | tf_op jit(solution)/shard_map/ppermute | solution.py:314
  24.4 0.3 shard_map.109
  24.8 0.1 collective-permute-start.7
  24.8 0.3 shard_map.110.first
  25.2 1.2 %collective-permute-done.7.second = bf16[128,1024]{1,0:T(8,128)(2,1)S(1)} collective-permute-done((bf16[128,1024]{1,0:T(8,128)(2,1)S(1)}, bf16[128,1024]{1,0:T(8,128)(2,1)S(1)}, u32[]{:S(2)}, u32[]{:S(2)}) %collective-permute-start.7) | collective-permute-done | bytes 262176 | tf_op jit(solution)/shard_map/ppermute | solution.py:314
  26.4 1.6 %collective-permute-start.8 = (bf16[128,1024]{1,0:T(8,128)(2,1)S(1)}, bf16[128,1024]{1,0:T(8,128)(2,1)S(1)}, u32[]{:S(2)}, u32[]{:S(2)}) collective-permute-start(bf16[128,1024]{1,0:T(8,128)(2,1)S(1)} %shard_map.111.first), channel_id=1, source_target_pairs={{0,2},{1,3},{2,0},{3,1},{4,6},{5,7},{6,4},{7,5},{8,10},{9,11},{10,... | collective-permute-start | bytes 786440 | tf_op jit(solution)/shard_map/ppermute | solution.py:314
  28.0 0.5 collective-permute-start.11
  28.5 9.1 %collective-permute-done.11.facing = bf16[128,512]{1,0:T(8,128)(2,1)S(1)} collective-permute-done((bf16[128,512]{1,0:T(8,128)(2,1)S(1)}, bf16[128,512]{1,0:T(8,128)(2,1)S(1)}, u32[]{:S(2)}, u32[]{:S(2)}) %collective-permute-start.11) | collective-permute-done | bytes 131104 | tf_op jit(solution)/shard_map/ppermute | solution.py:314
  37.7 0.6 collective-permute-start.9
  38.3 0.5 shard_map.113.acc
  38.8 0.2 collective-permute-done.12.relayed
  39.0 0.5 shard_map.114
  39.5 0.8 %collective-permute-start.13 = (bf16[128,128]{1,0:T(8,128)(2,1)S(1)}, bf16[128,128]{1,0:T(8,128)(2,1)S(1)}, u32[]{:S(2)}, u32[]{:S(2)}) collective-permute-start(bf16[128,128]{1,0:T(8,128)(2,1)S(1)} %get-tuple-element.73), channel_id=1, source_target_pairs={{0,4},{4,0},{8,12},{12,8},{16,20},{20,16},{24,28},{28,24},{1,5},{5... | collective-permute-start | bytes 98312 | tf_op jit(solution)/shard_map/ppermute | solution.py:314
  40.3 1.8 %collective-permute-start.14 = (bf16[128,128]{1,0:T(8,128)(2,1)S(1)}, bf16[128,128]{1,0:T(8,128)(2,1)S(1)}, u32[]{:S(2)}, u32[]{:S(2)}) collective-permute-start(bf16[128,128]{1,0:T(8,128)(2,1)S(1)} %get-tuple-element.74), channel_id=1, source_target_pairs={{0,8},{4,12},{8,0},{12,4},{16,24},{20,28},{24,16},{28,20},{1,9},{5... | collective-permute-start | bytes 98312 | tf_op jit(solution)/shard_map/ppermute | solution.py:314
  42.1 1.0 %collective-permute-start.15 = (bf16[128,128]{1,0:T(8,128)(2,1)S(1)}, bf16[128,128]{1,0:T(8,128)(2,1)S(1)}, u32[]{:S(2)}, u32[]{:S(2)}) collective-permute-start(bf16[128,128]{1,0:T(8,128)(2,1)S(1)} %get-tuple-element.75), channel_id=1, source_target_pairs={{0,12},{4,8},{8,4},{12,0},{16,28},{20,24},{24,20},{28,16},{1,13},{... | collective-permute-start | bytes 98312 | tf_op jit(solution)/shard_map/ppermute | solution.py:314
  43.1 0.4 collective-permute-done.13.refs_1_
  43.5 0.8 %collective-permute-done.14.refs_2_ = bf16[128,128]{1,0:T(8,128)(2,1)S(1)} collective-permute-done((bf16[128,128]{1,0:T(8,128)(2,1)S(1)}, bf16[128,128]{1,0:T(8,128)(2,1)S(1)}, u32[]{:S(2)}, u32[]{:S(2)}) %collective-permute-start.14) | collective-permute-done | bytes 32800 | tf_op jit(solution)/shard_map/ppermute | solution.py:314
  44.4 2.5 %collective-permute-done.15.refs_3_ = bf16[128,128]{1,0:T(8,128)(2,1)S(1)} collective-permute-done((bf16[128,128]{1,0:T(8,128)(2,1)S(1)}, bf16[128,128]{1,0:T(8,128)(2,1)S(1)}, u32[]{:S(2)}, u32[]{:S(2)}) %collective-permute-start.15) | collective-permute-done | bytes 32800 | tf_op jit(solution)/shard_map/ppermute | solution.py:314
  46.9 0.5 shard_map.115
  47.4 2.5 %collective-permute-start.16 = (bf16[128,256]{1,0:T(8,128)(2,1)S(1)}, bf16[128,256]{1,0:T(8,128)(2,1)S(1)}, u32[]{:S(2)}, u32[]{:S(2)}) collective-permute-start(bf16[128,256]{1,0:T(8,128)(2,1)S(1)} %get-tuple-element.87), channel_id=1, source_target_pairs={{0,16},{4,20},{8,24},{12,28},{16,0},{20,4},{24,8},{28,12},{1,17},{... | collective-permute-start | bytes 196616 | tf_op jit(solution)/shard_map/ppermute | solution.py:314
  49.9 0.6 shard_map.116
  50.5 0.9 %shard_map.117 = (f32[512,128]{1,0:T(8,128)S(1)}, f32[512,128]{1,0:T(8,128)S(1)}, f32[512,128]{1,0:T(8,128)S(1)}) custom-call(s32[8,128]{1,0:T(8,128)S(1)} %get-tuple-element.59.po, s32[8,128]{1,0:T(8,128)S(1)} %get-tuple-element.50.fo, f32[512,128]{1,0:T(8,128)S(1)} %get-tuple-element.55.q, f32[512,128]{1,0:T(8,128)S(1)} %get-tuple-element.56.k, ...), custom_call_target="tpu_custom_call" | custom-call | flops 400000000 | tf_op jit(solution)/shard_map/pallas_call | solution.py:563
  51.4 1.9 %collective-permute-done.16.late = bf16[128,256]{1,0:T(8,128)(2,1)S(1)} collective-permute-done((bf16[128,256]{1,0:T(8,128)(2,1)S(1)}, bf16[128,256]{1,0:T(8,128)(2,1)S(1)}, u32[]{:S(2)}, u32[]{:S(2)}) %collective-permute-start.16) | collective-permute-done | bytes 65568 | tf_op jit(solution)/shard_map/ppermute | solution.py:314
  53.2 0.1 shard_map.118
  53.4 0.1 collective-permute-start.17
  53.4 1.8 %collective-permute-start.18 = (bf16[128,384]{1,0:T(8,128)(2,1)S(1)}, bf16[128,384]{1,0:T(8,128)(2,1)S(1)}, u32[]{:S(2)}, u32[]{:S(2)}) collective-permute-start(bf16[128,384]{1,0:T(8,128)(2,1)S(1)} %get-tuple-element.90), channel_id=1, source_target_pairs={{0,8},{4,12},{8,0},{12,4},{16,24},{20,28},{24,16},{28,20},{1,9},{5... | collective-permute-start | bytes 294920 | tf_op jit(solution)/shard_map/ppermute | solution.py:314
  55.2 1.7 %collective-permute-start.19 = (bf16[128,384]{1,0:T(8,128)(2,1)S(1)}, bf16[128,384]{1,0:T(8,128)(2,1)S(1)}, u32[]{:S(2)}, u32[]{:S(2)}) collective-permute-start(bf16[128,384]{1,0:T(8,128)(2,1)S(1)} %get-tuple-element.91), channel_id=1, source_target_pairs={{0,12},{4,8},{8,4},{12,0},{16,28},{20,24},{24,20},{28,16},{1,13},{... | collective-permute-start | bytes 294920 | tf_op jit(solution)/shard_map/ppermute | solution.py:314
  56.9 1.1 %collective-permute-done.17.refs_1_ = bf16[128,384]{1,0:T(8,128)(2,1)S(1)} collective-permute-done((bf16[128,384]{1,0:T(8,128)(2,1)S(1)}, bf16[128,384]{1,0:T(8,128)(2,1)S(1)}, u32[]{:S(2)}, u32[]{:S(2)}) %collective-permute-start.17) | collective-permute-done | bytes 98336 | tf_op jit(solution)/shard_map/ppermute | solution.py:314
  58.0 0.1 collective-permute-done.18.refs_2_
  58.1 2.6 %collective-permute-done.19.refs_3_ = bf16[128,384]{1,0:T(8,128)(2,1)S(1)} collective-permute-done((bf16[128,384]{1,0:T(8,128)(2,1)S(1)}, bf16[128,384]{1,0:T(8,128)(2,1)S(1)}, u32[]{:S(2)}, u32[]{:S(2)}) %collective-permute-start.19) | collective-permute-done | bytes 98336 | tf_op jit(solution)/shard_map/ppermute | solution.py:314
  60.7 0.9 %shard_map.119 = (bf16[128,2048]{1,0:T(8,128)(2,1)}, bf16[128,512]{1,0:T(8,128)(2,1)}, bf16[128,512]{1,0:T(8,128)(2,1)}, bf16[128,512]{1,0:T(8,128)(2,1)}) custom-call(bf16[128,1024]{1,0:T(8,128)(2,1)S(1)} %shard_map.112.mine, bf16[128,384]{1,0:T(8,128)(2,1)S(1)} %get-tuple-element.88.refs_0_, bf16[128,384]{1,0:T(8,128)(2,1)S(1)} %collective-permute-done.17.refs_1_, ...), custom_call_target="tpu_custom_call" | custom-call | flops 10000000 | tf_op jit(solution)/shard_map/pallas_call | solution.py:652
  61.7 0.7 %shard_map.120 = bf16[128,2048]{1,0:T(8,128)(2,1)} custom-call(bf16[128,1024]{1,0:T(8,128)(2,1)S(1)} %collective-permute-done.9.theirs, bf16[128,2048]{1,0:T(8,128)(2,1)} %get-tuple-element.92._), custom_call_target="tpu_custom_call", output_to_operand_aliasing={{}: (1, {})} | custom-call | flops 1000000 | tf_op jit(solution)/shard_map/pallas_call | solution.py:664
  (25 shorter events, 0.4 us)
Async XLA Ops:
  0.6 0.9 %copy-start.2 = (bf16[128,512]{1,0:T(8,128)(2,1)S(1)}, bf16[128,512]{1,0:T(8,128)(2,1)}, u32[]{:S(2)}) copy-start(bf16[128,512]{1,0:T(8,128)(2,1)} %q.1) | copy-start | bytes 393220
  0.6 1.0 %copy-start.3 = (bf16[128,512]{1,0:T(8,128)(2,1)S(1)}, bf16[128,512]{1,0:T(8,128)(2,1)}, u32[]{:S(2)}) copy-start(bf16[128,512]{1,0:T(8,128)(2,1)} %k.1) | copy-start | bytes 393220
  0.7 1.0 %copy-start.4 = (bf16[128,512]{1,0:T(8,128)(2,1)S(1)}, bf16[128,512]{1,0:T(8,128)(2,1)}, u32[]{:S(2)}) copy-start(bf16[128,512]{1,0:T(8,128)(2,1)} %v.1) | copy-start | bytes 393220
  1.7 4.7 %copy-start.5 = (s32[16]{0:T(128)S(1)}, s32[16]{0:T(128)}, u32[]{:S(2)}) copy-start(s32[16]{0:T(128)} %po.1) | copy-start | bytes 196
  1.7 4.7 %copy-start.6 = (s32[16]{0:T(128)S(1)}, s32[16]{0:T(128)}, u32[]{:S(2)}) copy-start(s32[16]{0:T(128)} %fo.1) | copy-start | bytes 196
  1.7 22.7 %copy-start = (bf16[512,2048]{1,0:T(8,128)(2,1)S(1)}, bf16[512,2048]{1,0:T(8,128)(2,1)}, u32[]{:S(2)}) copy-start(bf16[512,2048]{1,0:T(8,128)(2,1)} %w.7) | copy-start | bytes 6291460
  1.8 5.8 %collective-permute-start = (bf16[128,384]{1,0:T(8,128)(2,1)S(1)}, bf16[128,384]{1,0:T(8,128)(2,1)S(1)}, u32[]{:S(2)}, u32[]{:S(2)}) collective-permute-start(bf16[128,384]{1,0:T(8,128)(2,1)S(1)} %get-tuple-element.52), channel_id=1, source_target_pairs={{0,4},{4,0},{8,12},{12,8},{16,20},{20,16},{24,28},{28,24},{1,5},{5... | collective-permute-start | bytes 294920 | tf_op jit(solution)/shard_map/ppermute | solution.py:314
  4.8 5.5 %collective-permute-start.1 = (bf16[128,384]{1,0:T(8,128)(2,1)S(1)}, bf16[128,384]{1,0:T(8,128)(2,1)S(1)}, u32[]{:S(2)}, u32[]{:S(2)}) collective-permute-start(bf16[128,384]{1,0:T(8,128)(2,1)S(1)} %get-tuple-element.53), channel_id=1, source_target_pairs={{0,8},{4,12},{8,0},{12,4},{16,24},{20,28},{24,16},{28,20},{1,9},{5... | collective-permute-start | bytes 294920 | tf_op jit(solution)/shard_map/ppermute | solution.py:314
  6.4 5.5 %collective-permute-start.2 = (bf16[128,384]{1,0:T(8,128)(2,1)S(1)}, bf16[128,384]{1,0:T(8,128)(2,1)S(1)}, u32[]{:S(2)}, u32[]{:S(2)}) collective-permute-start(bf16[128,384]{1,0:T(8,128)(2,1)S(1)} %get-tuple-element.54), channel_id=1, source_target_pairs={{0,12},{4,8},{8,4},{12,0},{16,28},{20,24},{24,20},{28,16},{1,13},{... | collective-permute-start | bytes 294920 | tf_op jit(solution)/shard_map/ppermute | solution.py:314
  12.0 5.9 %collective-permute-start.3 = (bf16[128,256]{1,0:T(8,128)(2,1)S(1)}, bf16[128,256]{1,0:T(8,128)(2,1)S(1)}, u32[]{:S(2)}, u32[]{:S(2)}) collective-permute-start(bf16[128,256]{1,0:T(8,128)(2,1)S(1)} %get-tuple-element.58), channel_id=1, source_target_pairs={{0,16},{4,20},{8,24},{12,28},{16,0},{20,4},{24,8},{28,12},{1,17},{... | collective-permute-start | bytes 196616 | tf_op jit(solution)/shard_map/ppermute | solution.py:314
  17.9 4.0 %collective-permute-start.4 = (bf16[128,128]{1,0:T(8,128)(2,1)S(1)}, bf16[128,128]{1,0:T(8,128)(2,1)S(1)}, u32[]{:S(2)}, u32[]{:S(2)}) collective-permute-start(bf16[128,128]{1,0:T(8,128)(2,1)S(1)} %get-tuple-element.65), channel_id=1, source_target_pairs={{0,4},{4,0},{8,12},{12,8},{16,20},{20,16},{24,28},{28,24},{1,5},{5... | collective-permute-start | bytes 98312 | tf_op jit(solution)/shard_map/ppermute | solution.py:314
  18.2 3.9 %collective-permute-start.5 = (bf16[128,128]{1,0:T(8,128)(2,1)S(1)}, bf16[128,128]{1,0:T(8,128)(2,1)S(1)}, u32[]{:S(2)}, u32[]{:S(2)}) collective-permute-start(bf16[128,128]{1,0:T(8,128)(2,1)S(1)} %get-tuple-element.66), channel_id=1, source_target_pairs={{0,8},{4,12},{8,0},{12,4},{16,24},{20,28},{24,16},{28,20},{1,9},{5... | collective-permute-start | bytes 98312 | tf_op jit(solution)/shard_map/ppermute | solution.py:314
  19.6 4.8 %collective-permute-start.6 = (bf16[128,128]{1,0:T(8,128)(2,1)S(1)}, bf16[128,128]{1,0:T(8,128)(2,1)S(1)}, u32[]{:S(2)}, u32[]{:S(2)}) collective-permute-start(bf16[128,128]{1,0:T(8,128)(2,1)S(1)} %get-tuple-element.67), channel_id=1, source_target_pairs={{0,12},{4,8},{8,4},{12,0},{16,28},{20,24},{24,20},{28,16},{1,13},{... | collective-permute-start | bytes 98312 | tf_op jit(solution)/shard_map/ppermute | solution.py:314
  24.8 3.3 %copy-start.1 = (bf16[128,512]{1,0:T(8,128)(2,1)S(1)}, bf16[128,512]{1,0:T(8,128)(2,1)}, u32[]{:S(2)}) copy-start(bf16[128,512]{1,0:T(8,128)(2,1)} %refs_0_.1) | copy-start | bytes 393220
  24.8 1.6 %collective-permute-start.7 = (bf16[128,1024]{1,0:T(8,128)(2,1)S(1)}, bf16[128,1024]{1,0:T(8,128)(2,1)S(1)}, u32[]{:S(2)}, u32[]{:S(2)}) collective-permute-start(bf16[128,1024]{1,0:T(8,128)(2,1)S(1)} %get-tuple-element.69), channel_id=1, source_target_pairs={{0,1},{1,0},{2,3},{3,2},{4,5},{5,4},{6,7},{7,6},{8,9},{9,8},{10,11... | collective-permute-start | bytes 786440 | tf_op jit(solution)/shard_map/ppermute | solution.py:314
  26.4 11.2 %collective-permute-start.8 = (bf16[128,1024]{1,0:T(8,128)(2,1)S(1)}, bf16[128,1024]{1,0:T(8,128)(2,1)S(1)}, u32[]{:S(2)}, u32[]{:S(2)}) collective-permute-start(bf16[128,1024]{1,0:T(8,128)(2,1)S(1)} %shard_map.111.first), channel_id=1, source_target_pairs={{0,2},{1,3},{2,0},{3,1},{4,6},{5,7},{6,4},{7,5},{8,10},{9,11},{10,... | collective-permute-start | bytes 786440 | tf_op jit(solution)/shard_map/ppermute | solution.py:314
  28.0 9.6 %collective-permute-start.11 = (bf16[128,512]{1,0:T(8,128)(2,1)S(1)}, bf16[128,512]{1,0:T(8,128)(2,1)S(1)}, u32[]{:S(2)}, u32[]{:S(2)}) collective-permute-start(bf16[128,512]{1,0:T(8,128)(2,1)S(1)} %copy-done.1), channel_id=1, source_target_pairs={{0,2},{1,3},{2,0},{3,1},{4,6},{5,7},{6,4},{7,5},{8,10},{9,11},{10,... | collective-permute-start | bytes 393224 | tf_op jit(solution)/shard_map/ppermute | solution.py:314
  28.5 9.8 %collective-permute-start.10 = (bf16[128,512]{1,0:T(8,128)(2,1)S(1)}, bf16[128,512]{1,0:T(8,128)(2,1)S(1)}, u32[]{:S(2)}, u32[]{:S(2)}) collective-permute-start(bf16[128,512]{1,0:T(8,128)(2,1)S(1)} %copy-done.1), channel_id=1, source_target_pairs={{0,1},{1,0},{2,3},{3,2},{4,5},{5,4},{6,7},{7,6},{8,9},{9,8},{10,11... | collective-permute-start | bytes 393224 | tf_op jit(solution)/shard_map/ppermute | solution.py:314
  37.7 1.3 %collective-permute-start.12 = (bf16[128,512]{1,0:T(8,128)(2,1)S(1)}, bf16[128,512]{1,0:T(8,128)(2,1)S(1)}, u32[]{:S(2)}, u32[]{:S(2)}) collective-permute-start(bf16[128,512]{1,0:T(8,128)(2,1)S(1)} %collective-permute-done.11.facing), channel_id=1, source_target_pairs={{0,1},{1,0},{2,3},{3,2},{4,5},{5,4},{6,7},{7,6},{8,9},{9,8},{10,11... | collective-permute-start | bytes 393224 | tf_op jit(solution)/shard_map/ppermute | solution.py:314
  37.7 23.9 %collective-permute-start.9 = (bf16[128,1024]{1,0:T(8,128)(2,1)S(1)}, bf16[128,1024]{1,0:T(8,128)(2,1)S(1)}, u32[]{:S(2)}, u32[]{:S(2)}) collective-permute-start(bf16[128,1024]{1,0:T(8,128)(2,1)S(1)} %shard_map.112.mine), channel_id=1, source_target_pairs={{0,1},{1,0},{2,3},{3,2},{4,5},{5,4},{6,7},{7,6},{8,9},{9,8},{10,11... | collective-permute-start | bytes 786440 | tf_op jit(solution)/shard_map/ppermute | solution.py:314
  39.5 4.0 %collective-permute-start.13 = (bf16[128,128]{1,0:T(8,128)(2,1)S(1)}, bf16[128,128]{1,0:T(8,128)(2,1)S(1)}, u32[]{:S(2)}, u32[]{:S(2)}) collective-permute-start(bf16[128,128]{1,0:T(8,128)(2,1)S(1)} %get-tuple-element.73), channel_id=1, source_target_pairs={{0,4},{4,0},{8,12},{12,8},{16,20},{20,16},{24,28},{28,24},{1,5},{5... | collective-permute-start | bytes 98312 | tf_op jit(solution)/shard_map/ppermute | solution.py:314
  40.3 4.1 %collective-permute-start.14 = (bf16[128,128]{1,0:T(8,128)(2,1)S(1)}, bf16[128,128]{1,0:T(8,128)(2,1)S(1)}, u32[]{:S(2)}, u32[]{:S(2)}) collective-permute-start(bf16[128,128]{1,0:T(8,128)(2,1)S(1)} %get-tuple-element.74), channel_id=1, source_target_pairs={{0,8},{4,12},{8,0},{12,4},{16,24},{20,28},{24,16},{28,20},{1,9},{5... | collective-permute-start | bytes 98312 | tf_op jit(solution)/shard_map/ppermute | solution.py:314
  42.1 4.8 %collective-permute-start.15 = (bf16[128,128]{1,0:T(8,128)(2,1)S(1)}, bf16[128,128]{1,0:T(8,128)(2,1)S(1)}, u32[]{:S(2)}, u32[]{:S(2)}) collective-permute-start(bf16[128,128]{1,0:T(8,128)(2,1)S(1)} %get-tuple-element.75), channel_id=1, source_target_pairs={{0,12},{4,8},{8,4},{12,0},{16,28},{20,24},{24,20},{28,16},{1,13},{... | collective-permute-start | bytes 98312 | tf_op jit(solution)/shard_map/ppermute | solution.py:314
  47.4 5.8 %collective-permute-start.16 = (bf16[128,256]{1,0:T(8,128)(2,1)S(1)}, bf16[128,256]{1,0:T(8,128)(2,1)S(1)}, u32[]{:S(2)}, u32[]{:S(2)}) collective-permute-start(bf16[128,256]{1,0:T(8,128)(2,1)S(1)} %get-tuple-element.87), channel_id=1, source_target_pairs={{0,16},{4,20},{8,24},{12,28},{16,0},{20,4},{24,8},{28,12},{1,17},{... | collective-permute-start | bytes 196616 | tf_op jit(solution)/shard_map/ppermute | solution.py:314
  53.4 4.7 %collective-permute-start.17 = (bf16[128,384]{1,0:T(8,128)(2,1)S(1)}, bf16[128,384]{1,0:T(8,128)(2,1)S(1)}, u32[]{:S(2)}, u32[]{:S(2)}) collective-permute-start(bf16[128,384]{1,0:T(8,128)(2,1)S(1)} %get-tuple-element.89), channel_id=1, source_target_pairs={{0,4},{4,0},{8,12},{12,8},{16,20},{20,16},{24,28},{28,24},{1,5},{5... | collective-permute-start | bytes 294920 | tf_op jit(solution)/shard_map/ppermute | solution.py:314
  53.4 4.7 %collective-permute-start.18 = (bf16[128,384]{1,0:T(8,128)(2,1)S(1)}, bf16[128,384]{1,0:T(8,128)(2,1)S(1)}, u32[]{:S(2)}, u32[]{:S(2)}) collective-permute-start(bf16[128,384]{1,0:T(8,128)(2,1)S(1)} %get-tuple-element.90), channel_id=1, source_target_pairs={{0,8},{4,12},{8,0},{12,4},{16,24},{20,28},{24,16},{28,20},{1,9},{5... | collective-permute-start | bytes 294920 | tf_op jit(solution)/shard_map/ppermute | solution.py:314
  55.2 5.5 %collective-permute-start.19 = (bf16[128,384]{1,0:T(8,128)(2,1)S(1)}, bf16[128,384]{1,0:T(8,128)(2,1)S(1)}, u32[]{:S(2)}, u32[]{:S(2)}) collective-permute-start(bf16[128,384]{1,0:T(8,128)(2,1)S(1)} %get-tuple-element.91), channel_id=1, source_target_pairs={{0,12},{4,8},{8,4},{12,0},{16,28},{20,24},{24,20},{28,16},{1,13},{... | collective-permute-start | bytes 294920 | tf_op jit(solution)/shard_map/ppermute | solution.py:314

commit v5 on v4

--- a/solution.py
+++ b/solution.py
@@ -5,6 +5,11 @@
 from jax.experimental.pallas import tpu as pltpu
 from jax.sharding import PartitionSpec as P
 
+SEQ = "seq"
+HEAD = "head"
+TO_KEYS = "hij,hid->hjd"
+TO_ROWS = "hij,hjd->hid"
+TO_SCORES = "hid,hjd->hij"
 HEAD_DIM = 128
 SPAN = 512
 
@@ -46,7 +51,7 @@
 
 
 def masked(query_part, key_part, first_row, first_col, factor):
-    scores = product(query_part, key_part, "hid,hjd->hij") * factor
+    scores = product(query_part, key_part, TO_SCORES) * factor
     row_ids = first_row + lax.broadcasted_iota(jnp.int32, scores.shape, 1)
     col_ids = first_col + lax.broadcasted_iota(jnp.int32, scores.shape, 2)
     return jnp.where(row_ids >= col_ids, scores, masked_score)
@@ -55,13 +60,13 @@
 def branch_stats(scores, value_part):
     branch_max = jnp.max(scores, axis=-1)
     weights = jnp.exp(scores - branch_max[..., None])
-    numerator = product(weights.astype(jnp.bfloat16), value_part, "hij,hjd->hid")
+    numerator = product(weights.astype(jnp.bfloat16), value_part, TO_ROWS)
     return (branch_max, jnp.sum(weights, axis=-1), numerator)
 
 
 def score_grads(scores, row_max, row_sum, grad_part, value_part, row_delta):
     probability = jnp.exp(scores - row_max[..., None]) / row_sum[..., None]
-    prob_grad = product(grad_part, value_part, "hid,hjd->hij")
+    prob_grad = product(grad_part, value_part, TO_SCORES)
     score_grad = (probability * (prob_grad - row_delta[..., None])).astype(jnp.bfloat16)
     return (probability.astype(jnp.bfloat16), score_grad)
 
@@ -70,7 +75,7 @@
     tokens = queries.shape[0]
     head_count = queries.shape[1] // HEAD_DIM
     factor = HEAD_DIM ** (-0.5)
-    seq_count = lax.axis_size("seq")
+    seq_count = lax.axis_size(SEQ)
     total = tokens * seq_count
     selected = min(SPAN, total // 4)
     local_group = selected // tokens
@@ -78,10 +83,10 @@
     dilation = total // selected
     far_rows = tokens // dilation
     half_rows = tokens // 2
-    position = lax.axis_index("seq")
+    position = lax.axis_index(SEQ)
     local_rank = position % local_group
     pair_rank = position % (2 * local_group)
-    head_group = lax.axis_index("head")
+    head_group = lax.axis_index(HEAD)
     pair_branch_shift = lax.dynamic_slice_in_dim(pair_offsets, head_group * head_count, head_count)
     far_branch_shift = lax.dynamic_slice_in_dim(
         far_head_offsets, head_group * head_count, head_count
@@ -111,7 +116,7 @@
             parts,
             jax.tree.map(
                 lambda part, own: part.astype(own.dtype),
-                partner(shortened(parts), "seq", bit),
+                partner(shortened(parts), SEQ, bit),
                 parts,
             ),
             bit,
@@ -127,7 +132,7 @@
         select(segment_value, 2, pair_branch_shift),
     )
     pair_all_key, pair_all_value = joined(
-        nearby, partner((nearby[0], nearby[1]), "seq", local_levels), local_levels
+        nearby, partner((nearby[0], nearby[1]), SEQ, local_levels), local_levels
     )
     pair_scores = masked(pair_query, pair_all_key, pair_rank * half_rows, 0, factor)
     pair_stats = branch_stats(pair_scores, pair_all_value)
@@ -135,8 +140,8 @@
     far_key = select(head_keys, dilation, far_branch_shift)
     far_value = select(head_values, dilation, far_branch_shift)
     every_key, every_value = (
-        lax.all_gather(far_key, "seq", axis=1, tiled=True),
-        lax.all_gather(far_value, "seq", axis=1, tiled=True),
+        lax.all_gather(far_key, SEQ, axis=1, tiled=True),
+        lax.all_gather(far_value, SEQ, axis=1, tiled=True),
     )
     far_scores = masked(far_query, every_key, position * far_rows, 0, factor)
     far_stats = branch_stats(far_scores, every_value)
@@ -160,9 +165,9 @@
     head_out = numerator / row_sum[..., None]
     attended = by_token(head_out).astype(jnp.bfloat16)
     partial_out = jnp.dot(attended, out_weight, preferred_element_type=jnp.float32)
-    layer_out = lax.psum(partial_out.astype(jnp.bfloat16), "head")
+    layer_out = lax.psum(partial_out.astype(jnp.bfloat16), HEAD)
     grad_attended = lax.dot_general(
-        lax.all_gather(grad_out, "head", axis=1, tiled=True),
+        lax.all_gather(grad_out, HEAD, axis=1, tiled=True),
         out_weight,
         (((1,), (1,)), ((), ())),
         preferred_element_type=jnp.float32,
@@ -172,14 +177,14 @@
     _, local_dscore = score_grads(
         local_scores, row_max, row_sum, head_grads, segment_value, row_delta
     )
-    query_grad = product(local_dscore, segment_key, "hij,hjd->hid") * factor
+    query_grad = product(local_dscore, segment_key, TO_ROWS) * factor
     parts = (head_queries, head_grads)
     for bit in range(local_levels):
         parts = joined(
             parts,
             jax.tree.map(
                 lambda part, own: part.astype(own.dtype),
-                partner(shortened(parts), "seq", bit),
+                partner(shortened(parts), SEQ, bit),
                 parts,
             ),
             bit,
@@ -187,14 +192,14 @@
     group_query, group_grad = parts
     parts = (row_max, row_sum, row_delta)
     for bit in range(local_levels):
-        parts = joined(parts, partner(parts, "seq", bit), bit)
+        parts = joined(parts, partner(parts, SEQ, bit), bit)
     group_max, group_sum, group_delta = parts
     back_scores = masked(group_query, head_keys, 0, local_rank * tokens, factor)
     back_prob, back_dscore = score_grads(
         back_scores, group_max, group_sum, group_grad, head_values, group_delta
     )
-    key_grad = product(back_dscore, group_query, "hij,hid->hjd") * factor
-    value_grad = product(back_prob, group_grad, "hij,hid->hjd")
+    key_grad = product(back_dscore, group_query, TO_KEYS) * factor
+    value_grad = product(back_prob, group_grad, TO_KEYS)
     pair_grad = select(head_grads, 2, pair_branch_shift)
     pair_max = select(row_max, 2, pair_branch_shift)
     pair_sum = select(row_sum, 2, pair_branch_shift)
@@ -202,7 +207,7 @@
     _, pair_dscore = score_grads(
         pair_scores, pair_max, pair_sum, pair_grad, pair_all_value, pair_delta
     )
-    pair_dq = product(pair_dscore, pair_all_key, "hij,hjd->hid") * factor
+    pair_dq = product(pair_dscore, pair_all_key, TO_ROWS) * factor
     near_rows = (
         select(group_query, 2, pair_branch_shift),
         select(group_grad, 2, pair_branch_shift),
@@ -213,19 +218,19 @@
         select(group_delta, 2, pair_branch_shift),
     )
     all_query, all_grad = joined(
-        near_rows, partner((near_rows[0], near_rows[1]), "seq", local_levels), local_levels
+        near_rows, partner((near_rows[0], near_rows[1]), SEQ, local_levels), local_levels
     )
     all_max, all_sum, all_delta = joined(
         near_moments,
-        partner((near_moments[0], near_moments[1], near_moments[2]), "seq", local_levels),
+        partner((near_moments[0], near_moments[1], near_moments[2]), SEQ, local_levels),
         local_levels,
     )
     pair_back = masked(all_query, pair_key, 0, pair_rank * half_rows, factor)
     pair_back_prob, pair_back_dscore = score_grads(
         pair_back, all_max, all_sum, all_grad, pair_value, all_delta
     )
-    pair_dk = product(pair_back_dscore, all_query, "hij,hid->hjd") * factor
-    pair_dv = product(pair_back_prob, all_grad, "hij,hid->hjd")
+    pair_dk = product(pair_back_dscore, all_query, TO_KEYS) * factor
+    pair_dv = product(pair_back_prob, all_grad, TO_KEYS)
     query_grad = query_grad + spread(pair_dq, 2, pair_branch_shift, 0.0)
     key_grad = key_grad + spread(pair_dk, 2, pair_branch_shift, 0.0)
     value_grad = value_grad + spread(pair_dv, 2, pair_branch_shift, 0.0)
@@ -236,12 +241,12 @@
     far_prob, far_dscore = score_grads(
         far_scores, far_max, far_sum, far_grad, every_value, far_delta
     )
-    far_dq = product(far_dscore, every_key, "hij,hjd->hid") * factor
-    gathered_dk = product(far_dscore, far_query, "hij,hid->hjd") * factor
-    gathered_dv = product(far_prob, far_grad, "hij,hid->hjd")
+    far_dq = product(far_dscore, every_key, TO_ROWS) * factor
+    gathered_dk = product(far_dscore, far_query, TO_KEYS) * factor
+    gathered_dv = product(far_prob, far_grad, TO_KEYS)
     far_dk, far_dv = (
-        lax.psum_scatter(gathered_dk, "seq", scatter_dimension=1, tiled=True),
-        lax.psum_scatter(gathered_dv, "seq", scatter_dimension=1, tiled=True),
+        lax.psum_scatter(gathered_dk, SEQ, scatter_dimension=1, tiled=True),
+        lax.psum_scatter(gathered_dv, SEQ, scatter_dimension=1, tiled=True),
     )
     query_grad = query_grad + spread(far_dq, dilation, far_branch_shift, 0.0)
     key_grad = key_grad + spread(far_dk, dilation, far_branch_shift, 0.0)
@@ -301,24 +306,24 @@
         return jax.ShapeDtypeStruct(extent, dtype)
 
     def seq_rank():
-        return lax.rem(lax.axis_index("seq"), group)
+        return lax.rem(lax.axis_index(SEQ), group)
 
     def late_half():
-        return lax.axis_index("seq") // group
+        return lax.axis_index(SEQ) // group
 
     def my_head():
-        return lax.axis_index("head") * heads + seq_rank()
+        return lax.axis_index(HEAD) * heads + seq_rank()
 
     def swap(value, axis, mask):
         pairs = [(s, s ^ mask) for s in range(lax.axis_size(axis))]
         return lax.ppermute(value, axis, pairs)
 
     def swapped(blocks):
-        return [blocks[0]] + [swap(blocks[m], "seq", m) for m in dests if m]
-
-    mates = swap(grad_out, "head", 1)
-    facing = swap(grad_out, "head", 2)
-    relayed = swap(facing, "head", 1)
+        return [blocks[0]] + [swap(blocks[m], SEQ, m) for m in dests if m]
+
+    mates = swap(grad_out, HEAD, 1)
+    facing = swap(grad_out, HEAD, 2)
+    relayed = swap(facing, HEAD, 1)
 
     def opening(out):
         out[...] = jnp.zeros_like(out)
@@ -345,7 +350,7 @@
     )(pair_offsets, far_offsets)
 
     def grad_term(w, part, mask):
-        cols = lax.axis_index("head") ^ mask
+        cols = lax.axis_index(HEAD) ^ mask
         return matmul(part[...], w[:, pl.ds(pl.multiple_of(cols * width, width), width)], NT)
 
     def project_grad(w, *refs):
@@ -426,7 +431,7 @@
     q, k, v, far_kv = call(
         assemble, [wide] * 3 + [far_pair], [vmem] + [vmem] * group, flops=10**7
     )(far_start, *blocks)
-    early_kv = swap(far_kv, "seq", group)
+    early_kv = swap(far_kv, SEQ, group)
 
     def near_rows(po, q, k, v, out, lse):
         mask = causal((selected, selected))
@@ -533,7 +538,7 @@
         [vmem] + [vmem] * (6 + group),
         flops=2 * 10**8,
     )(far_start, q, k, v, early_kv, out_wide, lse, *grad_blocks)
-    late = swap(late_kv, "seq", group)
+    late = swap(late_kv, SEQ, group)
 
     def near_grads(q, k, v, grad, lse, delta, at):
         mask = causal((selected, selected))
@@ -592,7 +597,7 @@
         return pl.ds(pl.multiple_of(bit * half, half), half)
 
     def my_half():
-        return lax.rem(lax.axis_index("head"), 2)
+        return lax.rem(lax.axis_index(HEAD), 2)
 
     def project_theirs(w, *refs):
         parts, (both, send) = refs[:group], refs[group:]
@@ -608,7 +613,7 @@
         [vmem] * (1 + group),
         flops=10**8,
     )(out_weight, *attended)
-    mate = swap(theirs, "head", 1)
+    mate = swap(theirs, HEAD, 1)
 
     def project_mine(w, both, out):
         out[...] = matmul(both[...], w[:, columns(my_half())], NN).astype(bf16)
@@ -621,9 +626,9 @@
 
     mine = call(project_mine, half_out, [vmem] * 2, flops=10**8)(out_weight, both)
     pair_sum = call(add_mate, half_out, [vmem] * 2, flops=10**6)(mine, mate)
-    across = swap(pair_sum, "head", 2)
+    across = swap(pair_sum, HEAD, 2)
     total = call(add_across, half_out, [vmem] * 2, flops=10**6)(pair_sum, across)
-    other = swap(total, "head", 1)
+    other = swap(total, HEAD, 1)
 
     def copy_all(copies):
         for copy in copies:
@@ -676,26 +681,26 @@
 def local(queries, key_rows, value_rows, out_weight, grad_out, pair_offsets, far_head_offsets):
     tokens = queries.shape[0]
     heads = queries.shape[1] // HEAD_DIM
-    seq_count = lax.axis_size("seq")
+    seq_count = lax.axis_size(SEQ)
     total = tokens * seq_count
     selected = min(SPAN, total // 4)
     group = 2 * selected // tokens
     operands = (
         queries, key_rows, value_rows, out_weight, grad_out, pair_offsets, far_head_offsets
     )
-    if group == heads and seq_count == 2 * group and lax.axis_size("head") == 4:
-        plan = (tokens, heads, group, selected, total // selected, lax.axis_size("head"))
+    if group == heads and seq_count == 2 * group and lax.axis_size(HEAD) == 4:
+        plan = (tokens, heads, group, selected, total // selected, lax.axis_size(HEAD))
         return fast_local(plan, *operands)
     return exchange_local(*operands)
 
 
 def solution(mesh):
     placed = (
-        P("seq", "head"),
-        P("seq", "head"),
-        P("seq", "head"),
-        P("head", None),
-        P("seq", "head"),
+        P(SEQ, HEAD),
+        P(SEQ, HEAD),
+        P(SEQ, HEAD),
+        P(HEAD, None),
+        P(SEQ, HEAD),
         P(),
         P(),
     )
@@ -703,6 +708,6 @@
         local,
         mesh=mesh,
         in_specs=placed,
-        out_specs=(P("seq", None), P("seq", "head"), P("seq", "head"), P("seq", "head")),
+        out_specs=(P(SEQ, None), P(SEQ, HEAD), P(SEQ, HEAD), P(SEQ, HEAD)),
         check_vma=False,
     )

time: 62.6 us -> 62.6 us (level)
  no operation moved by 1% of the time
where the time goes in v5:
time: 62.6 us; the launch traced here: 62.4 us
  waiting for transfers between devices  30.2 us (48%)
  starting transfers between devices  23.1 us (37%)
  Pallas kernels  7.22 us (12%)
  local copies, waits for them, and re-layouts  1.02 us (2%)
  between operations  0.84 us (1%)
    ppermute x20, waiting for transfers between devices, swap(): return lax.ppermute(value, axis, pairs)  30.2 us
    ppermute x20, starting transfers between devices, swap(): return lax.ppermute(value, axis, pairs)  23.1 us
  transfers between devices with their start and end apart: 20, of which 17 were waited for; matrix products, arithmetic and copies ran while one was open for 0% of the time, Pallas kernels for 10%

profile of v5, /device:TPU:0, one launch (start us, length us, event | category | flops | bytes accessed | tf_op | source)
XLA Modules:
  0.0 62.4 jit_solution(12948708864476598008)
XLA Ops:
  0.7 0.9 %copy-done.2 = bf16[128,512]{1,0:T(8,128)(2,1)S(1)} copy-done((bf16[128,512]{1,0:T(8,128)(2,1)S(1)}, bf16[128,512]{1,0:T(8,128)(2,1)}, u32[]{:S(2)}) %copy-start.2) | copy-done | bytes 131096
  1.8 3.0 %collective-permute-start = (bf16[128,384]{1,0:T(8,128)(2,1)S(1)}, bf16[128,384]{1,0:T(8,128)(2,1)S(1)}, u32[]{:S(2)}, u32[]{:S(2)}) collective-permute-start(bf16[128,384]{1,0:T(8,128)(2,1)S(1)} %get-tuple-element.52), channel_id=1, source_target_pairs={{0,4},{4,0},{8,12},{12,8},{16,20},{20,16},{24,28},{28,24},{1,5},{5... | collective-permute-start | bytes 294920 | tf_op jit(solution)/shard_map/ppermute | solution.py:319
  4.8 1.6 %collective-permute-start.1 = (bf16[128,384]{1,0:T(8,128)(2,1)S(1)}, bf16[128,384]{1,0:T(8,128)(2,1)S(1)}, u32[]{:S(2)}, u32[]{:S(2)}) collective-permute-start(bf16[128,384]{1,0:T(8,128)(2,1)S(1)} %get-tuple-element.53), channel_id=1, source_target_pairs={{0,8},{4,12},{8,0},{12,4},{16,24},{20,28},{24,16},{28,20},{1,9},{5... | collective-permute-start | bytes 294920 | tf_op jit(solution)/shard_map/ppermute | solution.py:319
  6.4 0.6 shard_map.102
  6.9 0.6 %collective-permute-done.refs_1_ = bf16[128,384]{1,0:T(8,128)(2,1)S(1)} collective-permute-done((bf16[128,384]{1,0:T(8,128)(2,1)S(1)}, bf16[128,384]{1,0:T(8,128)(2,1)S(1)}, u32[]{:S(2)}, u32[]{:S(2)}) %collective-permute-start) | collective-permute-done | bytes 98336 | tf_op jit(solution)/shard_map/ppermute | solution.py:319
  7.6 2.7 %collective-permute-done.1.refs_2_ = bf16[128,384]{1,0:T(8,128)(2,1)S(1)} collective-permute-done((bf16[128,384]{1,0:T(8,128)(2,1)S(1)}, bf16[128,384]{1,0:T(8,128)(2,1)S(1)}, u32[]{:S(2)}, u32[]{:S(2)}) %collective-permute-start.1) | collective-permute-done | bytes 98336 | tf_op jit(solution)/shard_map/ppermute | solution.py:319
  10.3 1.6 %collective-permute-done.2.refs_3_ = bf16[128,384]{1,0:T(8,128)(2,1)S(1)} collective-permute-done((bf16[128,384]{1,0:T(8,128)(2,1)S(1)}, bf16[128,384]{1,0:T(8,128)(2,1)S(1)}, u32[]{:S(2)}, u32[]{:S(2)}) %collective-permute-start.2) | collective-permute-done | bytes 98336 | tf_op jit(solution)/shard_map/ppermute | solution.py:319
  11.9 0.1 shard_map.105
  12.0 2.7 %collective-permute-start.3 = (bf16[128,256]{1,0:T(8,128)(2,1)S(1)}, bf16[128,256]{1,0:T(8,128)(2,1)S(1)}, u32[]{:S(2)}, u32[]{:S(2)}) collective-permute-start(bf16[128,256]{1,0:T(8,128)(2,1)S(1)} %get-tuple-element.58), channel_id=1, source_target_pairs={{0,16},{4,20},{8,24},{12,28},{16,0},{20,4},{24,8},{28,12},{1,17},{... | collective-permute-start | bytes 196616 | tf_op jit(solution)/shard_map/ppermute | solution.py:319
  14.6 0.9 %shard_map.106 = (f32[512,128]{1,0:T(8,128)S(1)}, f32[512,128]{1,0:T(8,128)S(1)}) custom-call(s32[8,128]{1,0:T(8,128)S(1)} %get-tuple-element.59.po, s32[8,128]{1,0:T(8,128)S(1)} %get-tuple-element.50.fo, f32[512,128]{1,0:T(8,128)S(1)} %get-tuple-element.55.q, f32[512,128]{1,0:T(8,128)S(1)} %get-tuple-element.56.k, f32[512,128]{1,0:T(8,128)S(1)} %get-tuple-element.57.v), custom_call_target="tpu_custom_call" | custom-call | flops 200000000 | tf_op jit(solution)/shard_map/pallas_call | solution.py:471
  15.6 2.3 %collective-permute-done.3.early_kv = bf16[128,256]{1,0:T(8,128)(2,1)S(1)} collective-permute-done((bf16[128,256]{1,0:T(8,128)(2,1)S(1)}, bf16[128,256]{1,0:T(8,128)(2,1)S(1)}, u32[]{:S(2)}, u32[]{:S(2)}) %collective-permute-start.3) | collective-permute-done | bytes 65568 | tf_op jit(solution)/shard_map/ppermute | solution.py:319
  17.9 0.3 collective-permute-start.4
  18.2 1.4 %collective-permute-start.5 = (bf16[128,128]{1,0:T(8,128)(2,1)S(1)}, bf16[128,128]{1,0:T(8,128)(2,1)S(1)}, u32[]{:S(2)}, u32[]{:S(2)}) collective-permute-start(bf16[128,128]{1,0:T(8,128)(2,1)S(1)} %get-tuple-element.66), channel_id=1, source_target_pairs={{0,8},{4,12},{8,0},{12,4},{16,24},{20,28},{24,16},{28,20},{1,9},{5... | collective-permute-start | bytes 98312 | tf_op jit(solution)/shard_map/ppermute | solution.py:319
  19.6 1.9 %collective-permute-start.6 = (bf16[128,128]{1,0:T(8,128)(2,1)S(1)}, bf16[128,128]{1,0:T(8,128)(2,1)S(1)}, u32[]{:S(2)}, u32[]{:S(2)}) collective-permute-start(bf16[128,128]{1,0:T(8,128)(2,1)S(1)} %get-tuple-element.67), channel_id=1, source_target_pairs={{0,12},{4,8},{8,4},{12,0},{16,28},{20,24},{24,20},{28,16},{1,13},{... | collective-permute-start | bytes 98312 | tf_op jit(solution)/shard_map/ppermute | solution.py:319
  21.5 0.4 collective-permute-done.4.refs_1_
  21.9 0.2 collective-permute-done.5.refs_2_
  22.2 2.3 %collective-permute-done.6.refs_3_ = bf16[128,128]{1,0:T(8,128)(2,1)S(1)} collective-permute-done((bf16[128,128]{1,0:T(8,128)(2,1)S(1)}, bf16[128,128]{1,0:T(8,128)(2,1)S(1)}, u32[]{:S(2)}, u32[]{:S(2)}) %collective-permute-start.6) | collective-permute-done | bytes 32800 | tf_op jit(solution)/shard_map/ppermute | solution.py:319
  24.4 0.3 shard_map.109
  24.8 0.1 collective-permute-start.7
  24.8 0.3 shard_map.110.first
  25.2 1.2 %collective-permute-done.7.second = bf16[128,1024]{1,0:T(8,128)(2,1)S(1)} collective-permute-done((bf16[128,1024]{1,0:T(8,128)(2,1)S(1)}, bf16[128,1024]{1,0:T(8,128)(2,1)S(1)}, u32[]{:S(2)}, u32[]{:S(2)}) %collective-permute-start.7) | collective-permute-done | bytes 262176 | tf_op jit(solution)/shard_map/ppermute | solution.py:319
  26.4 1.6 %collective-permute-start.8 = (bf16[128,1024]{1,0:T(8,128)(2,1)S(1)}, bf16[128,1024]{1,0:T(8,128)(2,1)S(1)}, u32[]{:S(2)}, u32[]{:S(2)}) collective-permute-start(bf16[128,1024]{1,0:T(8,128)(2,1)S(1)} %shard_map.111.first), channel_id=1, source_target_pairs={{0,2},{1,3},{2,0},{3,1},{4,6},{5,7},{6,4},{7,5},{8,10},{9,11},{10,... | collective-permute-start | bytes 786440 | tf_op jit(solution)/shard_map/ppermute | solution.py:319
  28.0 0.5 collective-permute-start.11
  28.5 9.1 %collective-permute-done.11.facing = bf16[128,512]{1,0:T(8,128)(2,1)S(1)} collective-permute-done((bf16[128,512]{1,0:T(8,128)(2,1)S(1)}, bf16[128,512]{1,0:T(8,128)(2,1)S(1)}, u32[]{:S(2)}, u32[]{:S(2)}) %collective-permute-start.11) | collective-permute-done | bytes 131104 | tf_op jit(solution)/shard_map/ppermute | solution.py:319
  37.7 0.6 collective-permute-start.9
  38.3 0.5 shard_map.113.acc
  38.8 0.2 collective-permute-done.12.relayed
  39.0 0.5 shard_map.114
  39.5 0.8 %collective-permute-start.13 = (bf16[128,128]{1,0:T(8,128)(2,1)S(1)}, bf16[128,128]{1,0:T(8,128)(2,1)S(1)}, u32[]{:S(2)}, u32[]{:S(2)}) collective-permute-start(bf16[128,128]{1,0:T(8,128)(2,1)S(1)} %get-tuple-element.73), channel_id=1, source_target_pairs={{0,4},{4,0},{8,12},{12,8},{16,20},{20,16},{24,28},{28,24},{1,5},{5... | collective-permute-start | bytes 98312 | tf_op jit(solution)/shard_map/ppermute | solution.py:319
  40.3 1.8 %collective-permute-start.14 = (bf16[128,128]{1,0:T(8,128)(2,1)S(1)}, bf16[128,128]{1,0:T(8,128)(2,1)S(1)}, u32[]{:S(2)}, u32[]{:S(2)}) collective-permute-start(bf16[128,128]{1,0:T(8,128)(2,1)S(1)} %get-tuple-element.74), channel_id=1, source_target_pairs={{0,8},{4,12},{8,0},{12,4},{16,24},{20,28},{24,16},{28,20},{1,9},{5... | collective-permute-start | bytes 98312 | tf_op jit(solution)/shard_map/ppermute | solution.py:319
  42.1 1.0 %collective-permute-start.15 = (bf16[128,128]{1,0:T(8,128)(2,1)S(1)}, bf16[128,128]{1,0:T(8,128)(2,1)S(1)}, u32[]{:S(2)}, u32[]{:S(2)}) collective-permute-start(bf16[128,128]{1,0:T(8,128)(2,1)S(1)} %get-tuple-element.75), channel_id=1, source_target_pairs={{0,12},{4,8},{8,4},{12,0},{16,28},{20,24},{24,20},{28,16},{1,13},{... | collective-permute-start | bytes 98312 | tf_op jit(solution)/shard_map/ppermute | solution.py:319
  43.1 0.4 collective-permute-done.13.refs_1_
  43.5 0.8 %collective-permute-done.14.refs_2_ = bf16[128,128]{1,0:T(8,128)(2,1)S(1)} collective-permute-done((bf16[128,128]{1,0:T(8,128)(2,1)S(1)}, bf16[128,128]{1,0:T(8,128)(2,1)S(1)}, u32[]{:S(2)}, u32[]{:S(2)}) %collective-permute-start.14) | collective-permute-done | bytes 32800 | tf_op jit(solution)/shard_map/ppermute | solution.py:319
  44.4 2.5 %collective-permute-done.15.refs_3_ = bf16[128,128]{1,0:T(8,128)(2,1)S(1)} collective-permute-done((bf16[128,128]{1,0:T(8,128)(2,1)S(1)}, bf16[128,128]{1,0:T(8,128)(2,1)S(1)}, u32[]{:S(2)}, u32[]{:S(2)}) %collective-permute-start.15) | collective-permute-done | bytes 32800 | tf_op jit(solution)/shard_map/ppermute | solution.py:319
  46.9 0.5 shard_map.115
  47.4 2.5 %collective-permute-start.16 = (bf16[128,256]{1,0:T(8,128)(2,1)S(1)}, bf16[128,256]{1,0:T(8,128)(2,1)S(1)}, u32[]{:S(2)}, u32[]{:S(2)}) collective-permute-start(bf16[128,256]{1,0:T(8,128)(2,1)S(1)} %get-tuple-element.87), channel_id=1, source_target_pairs={{0,16},{4,20},{8,24},{12,28},{16,0},{20,4},{24,8},{28,12},{1,17},{... | collective-permute-start | bytes 196616 | tf_op jit(solution)/shard_map/ppermute | solution.py:319
  49.9 0.6 shard_map.116
  50.5 0.9 %shard_map.117 = (f32[512,128]{1,0:T(8,128)S(1)}, f32[512,128]{1,0:T(8,128)S(1)}, f32[512,128]{1,0:T(8,128)S(1)}) custom-call(s32[8,128]{1,0:T(8,128)S(1)} %get-tuple-element.59.po, s32[8,128]{1,0:T(8,128)S(1)} %get-tuple-element.50.fo, f32[512,128]{1,0:T(8,128)S(1)} %get-tuple-element.55.q, f32[512,128]{1,0:T(8,128)S(1)} %get-tuple-element.56.k, ...), custom_call_target="tpu_custom_call" | custom-call | flops 400000000 | tf_op jit(solution)/shard_map/pallas_call | solution.py:568
  51.4 1.9 %collective-permute-done.16.late = bf16[128,256]{1,0:T(8,128)(2,1)S(1)} collective-permute-done((bf16[128,256]{1,0:T(8,128)(2,1)S(1)}, bf16[128,256]{1,0:T(8,128)(2,1)S(1)}, u32[]{:S(2)}, u32[]{:S(2)}) %collective-permute-start.16) | collective-permute-done | bytes 65568 | tf_op jit(solution)/shard_map/ppermute | solution.py:319
  53.2 0.1 shard_map.118
  53.4 0.1 collective-permute-start.17
  53.4 1.8 %collective-permute-start.18 = (bf16[128,384]{1,0:T(8,128)(2,1)S(1)}, bf16[128,384]{1,0:T(8,128)(2,1)S(1)}, u32[]{:S(2)}, u32[]{:S(2)}) collective-permute-start(bf16[128,384]{1,0:T(8,128)(2,1)S(1)} %get-tuple-element.90), channel_id=1, source_target_pairs={{0,8},{4,12},{8,0},{12,4},{16,24},{20,28},{24,16},{28,20},{1,9},{5... | collective-permute-start | bytes 294920 | tf_op jit(solution)/shard_map/ppermute | solution.py:319
  55.2 1.7 %collective-permute-start.19 = (bf16[128,384]{1,0:T(8,128)(2,1)S(1)}, bf16[128,384]{1,0:T(8,128)(2,1)S(1)}, u32[]{:S(2)}, u32[]{:S(2)}) collective-permute-start(bf16[128,384]{1,0:T(8,128)(2,1)S(1)} %get-tuple-element.91), channel_id=1, source_target_pairs={{0,12},{4,8},{8,4},{12,0},{16,28},{20,24},{24,20},{28,16},{1,13},{... | collective-permute-start | bytes 294920 | tf_op jit(solution)/shard_map/ppermute | solution.py:319
  56.9 1.1 %collective-permute-done.17.refs_1_ = bf16[128,384]{1,0:T(8,128)(2,1)S(1)} collective-permute-done((bf16[128,384]{1,0:T(8,128)(2,1)S(1)}, bf16[128,384]{1,0:T(8,128)(2,1)S(1)}, u32[]{:S(2)}, u32[]{:S(2)}) %collective-permute-start.17) | collective-permute-done | bytes 98336 | tf_op jit(solution)/shard_map/ppermute | solution.py:319
  58.0 0.1 collective-permute-done.18.refs_2_
  58.1 2.6 %collective-permute-done.19.refs_3_ = bf16[128,384]{1,0:T(8,128)(2,1)S(1)} collective-permute-done((bf16[128,384]{1,0:T(8,128)(2,1)S(1)}, bf16[128,384]{1,0:T(8,128)(2,1)S(1)}, u32[]{:S(2)}, u32[]{:S(2)}) %collective-permute-start.19) | collective-permute-done | bytes 98336 | tf_op jit(solution)/shard_map/ppermute | solution.py:319
  60.7 0.9 %shard_map.119 = (bf16[128,2048]{1,0:T(8,128)(2,1)}, bf16[128,512]{1,0:T(8,128)(2,1)}, bf16[128,512]{1,0:T(8,128)(2,1)}, bf16[128,512]{1,0:T(8,128)(2,1)}) custom-call(bf16[128,1024]{1,0:T(8,128)(2,1)S(1)} %shard_map.112.mine, bf16[128,384]{1,0:T(8,128)(2,1)S(1)} %get-tuple-element.88.refs_0_, bf16[128,384]{1,0:T(8,128)(2,1)S(1)} %collective-permute-done.17.refs_1_, ...), custom_call_target="tpu_custom_call" | custom-call | flops 10000000 | tf_op jit(solution)/shard_map/pallas_call | solution.py:657
  61.7 0.7 %shard_map.120 = bf16[128,2048]{1,0:T(8,128)(2,1)} custom-call(bf16[128,1024]{1,0:T(8,128)(2,1)S(1)} %collective-permute-done.9.theirs, bf16[128,2048]{1,0:T(8,128)(2,1)} %get-tuple-element.92._), custom_call_target="tpu_custom_call", output_to_operand_aliasing={{}: (1, {})} | custom-call | flops 1000000 | tf_op jit(solution)/shard_map/pallas_call | solution.py:669
  (25 shorter events, 0.4 us)
Async XLA Ops:
  0.6 0.9 %copy-start.2 = (bf16[128,512]{1,0:T(8,128)(2,1)S(1)}, bf16[128,512]{1,0:T(8,128)(2,1)}, u32[]{:S(2)}) copy-start(bf16[128,512]{1,0:T(8,128)(2,1)} %q.1) | copy-start | bytes 393220
  0.6 1.0 %copy-start.3 = (bf16[128,512]{1,0:T(8,128)(2,1)S(1)}, bf16[128,512]{1,0:T(8,128)(2,1)}, u32[]{:S(2)}) copy-start(bf16[128,512]{1,0:T(8,128)(2,1)} %k.1) | copy-start | bytes 393220
  0.7 1.0 %copy-start.4 = (bf16[128,512]{1,0:T(8,128)(2,1)S(1)}, bf16[128,512]{1,0:T(8,128)(2,1)}, u32[]{:S(2)}) copy-start(bf16[128,512]{1,0:T(8,128)(2,1)} %v.1) | copy-start | bytes 393220
  1.7 4.7 %copy-start.5 = (s32[16]{0:T(128)S(1)}, s32[16]{0:T(128)}, u32[]{:S(2)}) copy-start(s32[16]{0:T(128)} %po.1) | copy-start | bytes 196
  1.7 4.7 %copy-start.6 = (s32[16]{0:T(128)S(1)}, s32[16]{0:T(128)}, u32[]{:S(2)}) copy-start(s32[16]{0:T(128)} %fo.1) | copy-start | bytes 196
  1.7 22.7 %copy-start = (bf16[512,2048]{1,0:T(8,128)(2,1)S(1)}, bf16[512,2048]{1,0:T(8,128)(2,1)}, u32[]{:S(2)}) copy-start(bf16[512,2048]{1,0:T(8,128)(2,1)} %w.7) | copy-start | bytes 6291460
  1.8 5.8 %collective-permute-start = (bf16[128,384]{1,0:T(8,128)(2,1)S(1)}, bf16[128,384]{1,0:T(8,128)(2,1)S(1)}, u32[]{:S(2)}, u32[]{:S(2)}) collective-permute-start(bf16[128,384]{1,0:T(8,128)(2,1)S(1)} %get-tuple-element.52), channel_id=1, source_target_pairs={{0,4},{4,0},{8,12},{12,8},{16,20},{20,16},{24,28},{28,24},{1,5},{5... | collective-permute-start | bytes 294920 | tf_op jit(solution)/shard_map/ppermute | solution.py:319
  4.8 5.5 %collective-permute-start.1 = (bf16[128,384]{1,0:T(8,128)(2,1)S(1)}, bf16[128,384]{1,0:T(8,128)(2,1)S(1)}, u32[]{:S(2)}, u32[]{:S(2)}) collective-permute-start(bf16[128,384]{1,0:T(8,128)(2,1)S(1)} %get-tuple-element.53), channel_id=1, source_target_pairs={{0,8},{4,12},{8,0},{12,4},{16,24},{20,28},{24,16},{28,20},{1,9},{5... | collective-permute-start | bytes 294920 | tf_op jit(solution)/shard_map/ppermute | solution.py:319
  6.4 5.5 %collective-permute-start.2 = (bf16[128,384]{1,0:T(8,128)(2,1)S(1)}, bf16[128,384]{1,0:T(8,128)(2,1)S(1)}, u32[]{:S(2)}, u32[]{:S(2)}) collective-permute-start(bf16[128,384]{1,0:T(8,128)(2,1)S(1)} %get-tuple-element.54), channel_id=1, source_target_pairs={{0,12},{4,8},{8,4},{12,0},{16,28},{20,24},{24,20},{28,16},{1,13},{... | collective-permute-start | bytes 294920 | tf_op jit(solution)/shard_map/ppermute | solution.py:319
  12.0 5.9 %collective-permute-start.3 = (bf16[128,256]{1,0:T(8,128)(2,1)S(1)}, bf16[128,256]{1,0:T(8,128)(2,1)S(1)}, u32[]{:S(2)}, u32[]{:S(2)}) collective-permute-start(bf16[128,256]{1,0:T(8,128)(2,1)S(1)} %get-tuple-element.58), channel_id=1, source_target_pairs={{0,16},{4,20},{8,24},{12,28},{16,0},{20,4},{24,8},{28,12},{1,17},{... | collective-permute-start | bytes 196616 | tf_op jit(solution)/shard_map/ppermute | solution.py:319
  17.9 4.0 %collective-permute-start.4 = (bf16[128,128]{1,0:T(8,128)(2,1)S(1)}, bf16[128,128]{1,0:T(8,128)(2,1)S(1)}, u32[]{:S(2)}, u32[]{:S(2)}) collective-permute-start(bf16[128,128]{1,0:T(8,128)(2,1)S(1)} %get-tuple-element.65), channel_id=1, source_target_pairs={{0,4},{4,0},{8,12},{12,8},{16,20},{20,16},{24,28},{28,24},{1,5},{5... | collective-permute-start | bytes 98312 | tf_op jit(solution)/shard_map/ppermute | solution.py:319
  18.2 3.9 %collective-permute-start.5 = (bf16[128,128]{1,0:T(8,128)(2,1)S(1)}, bf16[128,128]{1,0:T(8,128)(2,1)S(1)}, u32[]{:S(2)}, u32[]{:S(2)}) collective-permute-start(bf16[128,128]{1,0:T(8,128)(2,1)S(1)} %get-tuple-element.66), channel_id=1, source_target_pairs={{0,8},{4,12},{8,0},{12,4},{16,24},{20,28},{24,16},{28,20},{1,9},{5... | collective-permute-start | bytes 98312 | tf_op jit(solution)/shard_map/ppermute | solution.py:319
  19.6 4.8 %collective-permute-start.6 = (bf16[128,128]{1,0:T(8,128)(2,1)S(1)}, bf16[128,128]{1,0:T(8,128)(2,1)S(1)}, u32[]{:S(2)}, u32[]{:S(2)}) collective-permute-start(bf16[128,128]{1,0:T(8,128)(2,1)S(1)} %get-tuple-element.67), channel_id=1, source_target_pairs={{0,12},{4,8},{8,4},{12,0},{16,28},{20,24},{24,20},{28,16},{1,13},{... | collective-permute-start | bytes 98312 | tf_op jit(solution)/shard_map/ppermute | solution.py:319
  24.8 3.3 %copy-start.1 = (bf16[128,512]{1,0:T(8,128)(2,1)S(1)}, bf16[128,512]{1,0:T(8,128)(2,1)}, u32[]{:S(2)}) copy-start(bf16[128,512]{1,0:T(8,128)(2,1)} %refs_0_.1) | copy-start | bytes 393220
  24.8 1.6 %collective-permute-start.7 = (bf16[128,1024]{1,0:T(8,128)(2,1)S(1)}, bf16[128,1024]{1,0:T(8,128)(2,1)S(1)}, u32[]{:S(2)}, u32[]{:S(2)}) collective-permute-start(bf16[128,1024]{1,0:T(8,128)(2,1)S(1)} %get-tuple-element.69), channel_id=1, source_target_pairs={{0,1},{1,0},{2,3},{3,2},{4,5},{5,4},{6,7},{7,6},{8,9},{9,8},{10,11... | collective-permute-start | bytes 786440 | tf_op jit(solution)/shard_map/ppermute | solution.py:319
  26.4 11.2 %collective-permute-start.8 = (bf16[128,1024]{1,0:T(8,128)(2,1)S(1)}, bf16[128,1024]{1,0:T(8,128)(2,1)S(1)}, u32[]{:S(2)}, u32[]{:S(2)}) collective-permute-start(bf16[128,1024]{1,0:T(8,128)(2,1)S(1)} %shard_map.111.first), channel_id=1, source_target_pairs={{0,2},{1,3},{2,0},{3,1},{4,6},{5,7},{6,4},{7,5},{8,10},{9,11},{10,... | collective-permute-start | bytes 786440 | tf_op jit(solution)/shard_map/ppermute | solution.py:319
  28.0 9.6 %collective-permute-start.11 = (bf16[128,512]{1,0:T(8,128)(2,1)S(1)}, bf16[128,512]{1,0:T(8,128)(2,1)S(1)}, u32[]{:S(2)}, u32[]{:S(2)}) collective-permute-start(bf16[128,512]{1,0:T(8,128)(2,1)S(1)} %copy-done.1), channel_id=1, source_target_pairs={{0,2},{1,3},{2,0},{3,1},{4,6},{5,7},{6,4},{7,5},{8,10},{9,11},{10,... | collective-permute-start | bytes 393224 | tf_op jit(solution)/shard_map/ppermute | solution.py:319
  28.5 9.8 %collective-permute-start.10 = (bf16[128,512]{1,0:T(8,128)(2,1)S(1)}, bf16[128,512]{1,0:T(8,128)(2,1)S(1)}, u32[]{:S(2)}, u32[]{:S(2)}) collective-permute-start(bf16[128,512]{1,0:T(8,128)(2,1)S(1)} %copy-done.1), channel_id=1, source_target_pairs={{0,1},{1,0},{2,3},{3,2},{4,5},{5,4},{6,7},{7,6},{8,9},{9,8},{10,11... | collective-permute-start | bytes 393224 | tf_op jit(solution)/shard_map/ppermute | solution.py:319
  37.7 1.3 %collective-permute-start.12 = (bf16[128,512]{1,0:T(8,128)(2,1)S(1)}, bf16[128,512]{1,0:T(8,128)(2,1)S(1)}, u32[]{:S(2)}, u32[]{:S(2)}) collective-permute-start(bf16[128,512]{1,0:T(8,128)(2,1)S(1)} %collective-permute-done.11.facing), channel_id=1, source_target_pairs={{0,1},{1,0},{2,3},{3,2},{4,5},{5,4},{6,7},{7,6},{8,9},{9,8},{10,11... | collective-permute-start | bytes 393224 | tf_op jit(solution)/shard_map/ppermute | solution.py:319
  37.7 23.9 %collective-permute-start.9 = (bf16[128,1024]{1,0:T(8,128)(2,1)S(1)}, bf16[128,1024]{1,0:T(8,128)(2,1)S(1)}, u32[]{:S(2)}, u32[]{:S(2)}) collective-permute-start(bf16[128,1024]{1,0:T(8,128)(2,1)S(1)} %shard_map.112.mine), channel_id=1, source_target_pairs={{0,1},{1,0},{2,3},{3,2},{4,5},{5,4},{6,7},{7,6},{8,9},{9,8},{10,11... | collective-permute-start | bytes 786440 | tf_op jit(solution)/shard_map/ppermute | solution.py:319
  39.5 4.0 %collective-permute-start.13 = (bf16[128,128]{1,0:T(8,128)(2,1)S(1)}, bf16[128,128]{1,0:T(8,128)(2,1)S(1)}, u32[]{:S(2)}, u32[]{:S(2)}) collective-permute-start(bf16[128,128]{1,0:T(8,128)(2,1)S(1)} %get-tuple-element.73), channel_id=1, source_target_pairs={{0,4},{4,0},{8,12},{12,8},{16,20},{20,16},{24,28},{28,24},{1,5},{5... | collective-permute-start | bytes 98312 | tf_op jit(solution)/shard_map/ppermute | solution.py:319
  40.3 4.1 %collective-permute-start.14 = (bf16[128,128]{1,0:T(8,128)(2,1)S(1)}, bf16[128,128]{1,0:T(8,128)(2,1)S(1)}, u32[]{:S(2)}, u32[]{:S(2)}) collective-permute-start(bf16[128,128]{1,0:T(8,128)(2,1)S(1)} %get-tuple-element.74), channel_id=1, source_target_pairs={{0,8},{4,12},{8,0},{12,4},{16,24},{20,28},{24,16},{28,20},{1,9},{5... | collective-permute-start | bytes 98312 | tf_op jit(solution)/shard_map/ppermute | solution.py:319
  42.1 4.8 %collective-permute-start.15 = (bf16[128,128]{1,0:T(8,128)(2,1)S(1)}, bf16[128,128]{1,0:T(8,128)(2,1)S(1)}, u32[]{:S(2)}, u32[]{:S(2)}) collective-permute-start(bf16[128,128]{1,0:T(8,128)(2,1)S(1)} %get-tuple-element.75), channel_id=1, source_target_pairs={{0,12},{4,8},{8,4},{12,0},{16,28},{20,24},{24,20},{28,16},{1,13},{... | collective-permute-start | bytes 98312 | tf_op jit(solution)/shard_map/ppermute | solution.py:319
  47.4 5.8 %collective-permute-start.16 = (bf16[128,256]{1,0:T(8,128)(2,1)S(1)}, bf16[128,256]{1,0:T(8,128)(2,1)S(1)}, u32[]{:S(2)}, u32[]{:S(2)}) collective-permute-start(bf16[128,256]{1,0:T(8,128)(2,1)S(1)} %get-tuple-element.87), channel_id=1, source_target_pairs={{0,16},{4,20},{8,24},{12,28},{16,0},{20,4},{24,8},{28,12},{1,17},{... | collective-permute-start | bytes 196616 | tf_op jit(solution)/shard_map/ppermute | solution.py:319
  53.4 4.7 %collective-permute-start.17 = (bf16[128,384]{1,0:T(8,128)(2,1)S(1)}, bf16[128,384]{1,0:T(8,128)(2,1)S(1)}, u32[]{:S(2)}, u32[]{:S(2)}) collective-permute-start(bf16[128,384]{1,0:T(8,128)(2,1)S(1)} %get-tuple-element.89), channel_id=1, source_target_pairs={{0,4},{4,0},{8,12},{12,8},{16,20},{20,16},{24,28},{28,24},{1,5},{5... | collective-permute-start | bytes 294920 | tf_op jit(solution)/shard_map/ppermute | solution.py:319
  53.4 4.7 %collective-permute-start.18 = (bf16[128,384]{1,0:T(8,128)(2,1)S(1)}, bf16[128,384]{1,0:T(8,128)(2,1)S(1)}, u32[]{:S(2)}, u32[]{:S(2)}) collective-permute-start(bf16[128,384]{1,0:T(8,128)(2,1)S(1)} %get-tuple-element.90), channel_id=1, source_target_pairs={{0,8},{4,12},{8,0},{12,4},{16,24},{20,28},{24,16},{28,20},{1,9},{5... | collective-permute-start | bytes 294920 | tf_op jit(solution)/shard_map/ppermute | solution.py:319
  55.2 5.5 %collective-permute-start.19 = (bf16[128,384]{1,0:T(8,128)(2,1)S(1)}, bf16[128,384]{1,0:T(8,128)(2,1)S(1)}, u32[]{:S(2)}, u32[]{:S(2)}) collective-permute-start(bf16[128,384]{1,0:T(8,128)(2,1)S(1)} %get-tuple-element.91), channel_id=1, source_target_pairs={{0,12},{4,8},{8,4},{12,0},{16,28},{20,24},{24,20},{28,16},{1,13},{... | collective-permute-start | bytes 294920 | tf_op jit(solution)/shard_map/ppermute | solution.py:319

commit v6 on v5

--- a/solution.py
+++ b/solution.py
@@ -546,18 +546,43 @@
             pick(q, at), pick(k, at), pick(v, at), pick(grad, at), lse[at, :], delta[at, :], mask
         )
 
-    def backward_pair(po, q, k, v, grad, lse, delta, *outs):
-        for ref, term in zip(outs, near_grads(q, k, v, grad, lse, delta, pair_rows(po))):
+    def pair_terms(po, refs, outs):
+        for ref, term in zip(outs, near_grads(*refs, pair_rows(po))):
             ref[...] = term
 
+    def backward_pair(po, *refs):
+        @pl.when(late_half() == 0)
+        def _():
+            pair_terms(po, refs[:6], refs[6:])
+
+    def backward_next(po, *refs):
+        @pl.when(late_half() > 0)
+        def _():
+            pair_terms(po, refs[:6], refs[9:])
+
     pair_wide = shape((selected, HEAD_DIM), f32)
-    pair_grads = call(backward_pair, [pair_wide] * 3, [vmem] * 7, flops=2 * 10**8)(
-        pair_start, q, k, v, grad, lse, delta
-    )
-
-    def backward_local(po, fo, q, k, v, grad, lse, delta, *refs):
-        pairs, fars, near = refs[:3], refs[3:6], refs[6:]
-        for first in range(0, span, selected):
+    rows_in = (pair_start, q, k, v, grad, lse, delta)
+    pair_grads = call(backward_pair, [pair_wide] * 3, [vmem] * 7, flops=2 * 10**8)(*rows_in)
+    pair_grads = call(
+        backward_next,
+        [pair_wide] * 3,
+        [vmem] * 10,
+        flops=2 * 10**8,
+        aliases={7: 0, 8: 1, 9: 2},
+    )(*rows_in, *pair_grads)
+
+    def backward_low(q, k, v, grad, lse, delta, *near):
+        half_span = pl.ds(0, selected)
+        for ref, term in zip(near, near_grads(q, k, v, grad, lse, delta, half_span)):
+            ref[half_span, :] = term
+
+    near = call(backward_low, [wide] * 3, [vmem] * 6, flops=2 * 10**8)(
+        q, k, v, grad, lse, delta
+    )
+
+    def backward_high(po, fo, q, k, v, grad, lse, delta, *refs):
+        pairs, fars, near = refs[:3], refs[3:6], refs[9:]
+        for first in range(selected, span, selected):
             at = pl.ds(first, selected)
             for ref, term in zip(near, near_grads(q, k, v, grad, lse, delta, at)):
                 ref[at, :] = term
@@ -565,8 +590,19 @@
             ref[pair_rows(po), :] += pair[...]
             ref[far_rows(fo), :] += far[...]
 
-    dq, dk, dv = call(backward_local, [wide] * 3, [vmem] * 14, flops=4 * 10**8)(
-        pair_start, far_start, q, k, v, grad, lse, delta, *pair_grads, far_dq, far_dk, far_dv
+    dq, dk, dv = call(
+        backward_high,
+        [wide] * 3,
+        [vmem] * 17,
+        flops=4 * 10**8,
+        aliases={14: 0, 15: 1, 16: 2},
+    )(
+        pair_start,
+        far_start,
+        *(q, k, v, grad, lse, delta),
+        *pair_grads,
+        *(far_dq, far_dk, far_dv),
+        *near,
     )
 
     def finish(fo, dq, dk, dv, late, *refs):

time: 62.6 us -> 62.6 us (level)
  no operation moved by 1% of the time
where the time goes in v6:
time: 62.6 us; the launch traced here: 62.4 us
  waiting for transfers between devices  29.9 us (48%)
  starting transfers between devices  23.1 us (37%)
  Pallas kernels  7.5 us (12%)
  local copies, waits for them, and re-layouts  1.02 us (2%)
  between operations  0.85 us (1%)
    ppermute x20, waiting for transfers between devices, swap(): return lax.ppermute(value, axis, pairs)  29.9 us
    ppermute x20, starting transfers between devices, swap(): return lax.ppermute(value, axis, pairs)  23.1 us
  transfers between devices with their start and end apart: 20, of which 17 were waited for; matrix products, arithmetic and copies ran while one was open for 0% of the time, Pallas kernels for 10%

profile of v6, /device:TPU:0, one launch (start us, length us, event | category | flops | bytes accessed | tf_op | source)
XLA Modules:
  0.0 62.4 jit_solution(10999681906394002758)
XLA Ops:
  0.7 0.9 %copy-done.2 = bf16[128,512]{1,0:T(8,128)(2,1)S(1)} copy-done((bf16[128,512]{1,0:T(8,128)(2,1)S(1)}, bf16[128,512]{1,0:T(8,128)(2,1)}, u32[]{:S(2)}) %copy-start.2) | copy-done | bytes 131096
  1.8 3.0 %collective-permute-start = (bf16[128,384]{1,0:T(8,128)(2,1)S(1)}, bf16[128,384]{1,0:T(8,128)(2,1)S(1)}, u32[]{:S(2)}, u32[]{:S(2)}) collective-permute-start(bf16[128,384]{1,0:T(8,128)(2,1)S(1)} %get-tuple-element.58), channel_id=1, source_target_pairs={{0,4},{4,0},{8,12},{12,8},{16,20},{20,16},{24,28},{28,24},{1,5},{5... | collective-permute-start | bytes 294920 | tf_op jit(solution)/shard_map/ppermute | solution.py:319
  4.8 1.6 %collective-permute-start.1 = (bf16[128,384]{1,0:T(8,128)(2,1)S(1)}, bf16[128,384]{1,0:T(8,128)(2,1)S(1)}, u32[]{:S(2)}, u32[]{:S(2)}) collective-permute-start(bf16[128,384]{1,0:T(8,128)(2,1)S(1)} %get-tuple-element.59), channel_id=1, source_target_pairs={{0,8},{4,12},{8,0},{12,4},{16,24},{20,28},{24,16},{28,20},{1,9},{5... | collective-permute-start | bytes 294920 | tf_op jit(solution)/shard_map/ppermute | solution.py:319
  6.4 0.6 shard_map.102
  6.9 0.6 %collective-permute-done.refs_1_ = bf16[128,384]{1,0:T(8,128)(2,1)S(1)} collective-permute-done((bf16[128,384]{1,0:T(8,128)(2,1)S(1)}, bf16[128,384]{1,0:T(8,128)(2,1)S(1)}, u32[]{:S(2)}, u32[]{:S(2)}) %collective-permute-start) | collective-permute-done | bytes 98336 | tf_op jit(solution)/shard_map/ppermute | solution.py:319
  7.6 2.7 %collective-permute-done.1.refs_2_ = bf16[128,384]{1,0:T(8,128)(2,1)S(1)} collective-permute-done((bf16[128,384]{1,0:T(8,128)(2,1)S(1)}, bf16[128,384]{1,0:T(8,128)(2,1)S(1)}, u32[]{:S(2)}, u32[]{:S(2)}) %collective-permute-start.1) | collective-permute-done | bytes 98336 | tf_op jit(solution)/shard_map/ppermute | solution.py:319
  10.3 1.6 %collective-permute-done.2.refs_3_ = bf16[128,384]{1,0:T(8,128)(2,1)S(1)} collective-permute-done((bf16[128,384]{1,0:T(8,128)(2,1)S(1)}, bf16[128,384]{1,0:T(8,128)(2,1)S(1)}, u32[]{:S(2)}, u32[]{:S(2)}) %collective-permute-start.2) | collective-permute-done | bytes 98336 | tf_op jit(solution)/shard_map/ppermute | solution.py:319
  11.9 0.1 shard_map.105
  12.0 2.7 %collective-permute-start.3 = (bf16[128,256]{1,0:T(8,128)(2,1)S(1)}, bf16[128,256]{1,0:T(8,128)(2,1)S(1)}, u32[]{:S(2)}, u32[]{:S(2)}) collective-permute-start(bf16[128,256]{1,0:T(8,128)(2,1)S(1)} %get-tuple-element.64), channel_id=1, source_target_pairs={{0,16},{4,20},{8,24},{12,28},{16,0},{20,4},{24,8},{28,12},{1,17},{... | collective-permute-start | bytes 196616 | tf_op jit(solution)/shard_map/ppermute | solution.py:319
  14.6 0.9 %shard_map.106 = (f32[512,128]{1,0:T(8,128)S(1)}, f32[512,128]{1,0:T(8,128)S(1)}) custom-call(s32[8,128]{1,0:T(8,128)S(1)} %get-tuple-element.65.po, s32[8,128]{1,0:T(8,128)S(1)} %get-tuple-element.56.fo, f32[512,128]{1,0:T(8,128)S(1)} %get-tuple-element.61.q.refs_0_, f32[512,128]{1,0:T(8,128)S(1)} %get-tuple-element.62.k.refs_1_, ...), custom_call_target="tpu_custom_call" | custom-call | flops 200000000 | tf_op jit(solution)/shard_map/pallas_call | solution.py:471
  15.6 2.3 %collective-permute-done.3.early_kv = bf16[128,256]{1,0:T(8,128)(2,1)S(1)} collective-permute-done((bf16[128,256]{1,0:T(8,128)(2,1)S(1)}, bf16[128,256]{1,0:T(8,128)(2,1)S(1)}, u32[]{:S(2)}, u32[]{:S(2)}) %collective-permute-start.3) | collective-permute-done | bytes 65568 | tf_op jit(solution)/shard_map/ppermute | solution.py:319
  17.9 0.3 collective-permute-start.4
  18.2 1.4 %collective-permute-start.5 = (bf16[128,128]{1,0:T(8,128)(2,1)S(1)}, bf16[128,128]{1,0:T(8,128)(2,1)S(1)}, u32[]{:S(2)}, u32[]{:S(2)}) collective-permute-start(bf16[128,128]{1,0:T(8,128)(2,1)S(1)} %get-tuple-element.72), channel_id=1, source_target_pairs={{0,8},{4,12},{8,0},{12,4},{16,24},{20,28},{24,16},{28,20},{1,9},{5... | collective-permute-start | bytes 98312 | tf_op jit(solution)/shard_map/ppermute | solution.py:319
  19.6 1.9 %collective-permute-start.6 = (bf16[128,128]{1,0:T(8,128)(2,1)S(1)}, bf16[128,128]{1,0:T(8,128)(2,1)S(1)}, u32[]{:S(2)}, u32[]{:S(2)}) collective-permute-start(bf16[128,128]{1,0:T(8,128)(2,1)S(1)} %get-tuple-element.73), channel_id=1, source_target_pairs={{0,12},{4,8},{8,4},{12,0},{16,28},{20,24},{24,20},{28,16},{1,13},{... | collective-permute-start | bytes 98312 | tf_op jit(solution)/shard_map/ppermute | solution.py:319
  21.5 0.4 collective-permute-done.4.refs_1_
  21.9 0.2 collective-permute-done.5.refs_2_
  22.2 2.3 %collective-permute-done.6.refs_3_ = bf16[128,128]{1,0:T(8,128)(2,1)S(1)} collective-permute-done((bf16[128,128]{1,0:T(8,128)(2,1)S(1)}, bf16[128,128]{1,0:T(8,128)(2,1)S(1)}, u32[]{:S(2)}, u32[]{:S(2)}) %collective-permute-start.6) | collective-permute-done | bytes 32800 | tf_op jit(solution)/shard_map/ppermute | solution.py:319
  24.4 0.3 shard_map.109
  24.8 0.1 collective-permute-start.7
  24.8 0.3 shard_map.110.first
  25.2 1.2 %collective-permute-done.7.second = bf16[128,1024]{1,0:T(8,128)(2,1)S(1)} collective-permute-done((bf16[128,1024]{1,0:T(8,128)(2,1)S(1)}, bf16[128,1024]{1,0:T(8,128)(2,1)S(1)}, u32[]{:S(2)}, u32[]{:S(2)}) %collective-permute-start.7) | collective-permute-done | bytes 262176 | tf_op jit(solution)/shard_map/ppermute | solution.py:319
  26.4 1.6 %collective-permute-start.8 = (bf16[128,1024]{1,0:T(8,128)(2,1)S(1)}, bf16[128,1024]{1,0:T(8,128)(2,1)S(1)}, u32[]{:S(2)}, u32[]{:S(2)}) collective-permute-start(bf16[128,1024]{1,0:T(8,128)(2,1)S(1)} %shard_map.111.first), channel_id=1, source_target_pairs={{0,2},{1,3},{2,0},{3,1},{4,6},{5,7},{6,4},{7,5},{8,10},{9,11},{10,... | collective-permute-start | bytes 786440 | tf_op jit(solution)/shard_map/ppermute | solution.py:319
  28.0 0.5 collective-permute-start.11
  28.5 9.1 %collective-permute-done.11.facing = bf16[128,512]{1,0:T(8,128)(2,1)S(1)} collective-permute-done((bf16[128,512]{1,0:T(8,128)(2,1)S(1)}, bf16[128,512]{1,0:T(8,128)(2,1)S(1)}, u32[]{:S(2)}, u32[]{:S(2)}) %collective-permute-start.11) | collective-permute-done | bytes 131104 | tf_op jit(solution)/shard_map/ppermute | solution.py:319
  37.7 0.6 collective-permute-start.9
  38.3 0.5 shard_map.113.acc
  38.8 0.2 collective-permute-done.12.relayed
  39.0 0.5 shard_map.114
  39.5 0.8 %collective-permute-start.13 = (bf16[128,128]{1,0:T(8,128)(2,1)S(1)}, bf16[128,128]{1,0:T(8,128)(2,1)S(1)}, u32[]{:S(2)}, u32[]{:S(2)}) collective-permute-start(bf16[128,128]{1,0:T(8,128)(2,1)S(1)} %get-tuple-element.79), channel_id=1, source_target_pairs={{0,4},{4,0},{8,12},{12,8},{16,20},{20,16},{24,28},{28,24},{1,5},{5... | collective-permute-start | bytes 98312 | tf_op jit(solution)/shard_map/ppermute | solution.py:319
  40.3 1.8 %collective-permute-start.14 = (bf16[128,128]{1,0:T(8,128)(2,1)S(1)}, bf16[128,128]{1,0:T(8,128)(2,1)S(1)}, u32[]{:S(2)}, u32[]{:S(2)}) collective-permute-start(bf16[128,128]{1,0:T(8,128)(2,1)S(1)} %get-tuple-element.80), channel_id=1, source_target_pairs={{0,8},{4,12},{8,0},{12,4},{16,24},{20,28},{24,16},{28,20},{1,9},{5... | collective-permute-start | bytes 98312 | tf_op jit(solution)/shard_map/ppermute | solution.py:319
  42.1 1.0 %collective-permute-start.15 = (bf16[128,128]{1,0:T(8,128)(2,1)S(1)}, bf16[128,128]{1,0:T(8,128)(2,1)S(1)}, u32[]{:S(2)}, u32[]{:S(2)}) collective-permute-start(bf16[128,128]{1,0:T(8,128)(2,1)S(1)} %get-tuple-element.81), channel_id=1, source_target_pairs={{0,12},{4,8},{8,4},{12,0},{16,28},{20,24},{24,20},{28,16},{1,13},{... | collective-permute-start | bytes 98312 | tf_op jit(solution)/shard_map/ppermute | solution.py:319
  43.1 0.4 collective-permute-done.13.refs_1_
  43.5 0.9 %collective-permute-done.14.refs_2_ = bf16[128,128]{1,0:T(8,128)(2,1)S(1)} collective-permute-done((bf16[128,128]{1,0:T(8,128)(2,1)S(1)}, bf16[128,128]{1,0:T(8,128)(2,1)S(1)}, u32[]{:S(2)}, u32[]{:S(2)}) %collective-permute-start.14) | collective-permute-done | bytes 32800 | tf_op jit(solution)/shard_map/ppermute | solution.py:319
  44.4 2.5 %collective-permute-done.15.refs_3_ = bf16[128,128]{1,0:T(8,128)(2,1)S(1)} collective-permute-done((bf16[128,128]{1,0:T(8,128)(2,1)S(1)}, bf16[128,128]{1,0:T(8,128)(2,1)S(1)}, u32[]{:S(2)}, u32[]{:S(2)}) %collective-permute-start.15) | collective-permute-done | bytes 32800 | tf_op jit(solution)/shard_map/ppermute | solution.py:319
  46.9 0.5 shard_map.115
  47.4 2.5 %collective-permute-start.16 = (bf16[128,256]{1,0:T(8,128)(2,1)S(1)}, bf16[128,256]{1,0:T(8,128)(2,1)S(1)}, u32[]{:S(2)}, u32[]{:S(2)}) collective-permute-start(bf16[128,256]{1,0:T(8,128)(2,1)S(1)} %get-tuple-element.99), channel_id=1, source_target_pairs={{0,16},{4,20},{8,24},{12,28},{16,0},{20,4},{24,8},{28,12},{1,17},{... | collective-permute-start | bytes 196616 | tf_op jit(solution)/shard_map/ppermute | solution.py:319
  49.9 0.5 shard_map.118
  50.4 0.6 shard_map.116
  51.1 0.6 shard_map.119
  51.7 1.6 %collective-permute-done.16.late = bf16[128,256]{1,0:T(8,128)(2,1)S(1)} collective-permute-done((bf16[128,256]{1,0:T(8,128)(2,1)S(1)}, bf16[128,256]{1,0:T(8,128)(2,1)S(1)}, u32[]{:S(2)}, u32[]{:S(2)}) %collective-permute-start.16) | collective-permute-done | bytes 65568 | tf_op jit(solution)/shard_map/ppermute | solution.py:319
  53.2 0.1 shard_map.120
  53.4 1.8 %collective-permute-start.18 = (bf16[128,384]{1,0:T(8,128)(2,1)S(1)}, bf16[128,384]{1,0:T(8,128)(2,1)S(1)}, u32[]{:S(2)}, u32[]{:S(2)}) collective-permute-start(bf16[128,384]{1,0:T(8,128)(2,1)S(1)} %get-tuple-element.102), channel_id=1, source_target_pairs={{0,8},{4,12},{8,0},{12,4},{16,24},{20,28},{24,16},{28,20},{1,9},{5... | collective-permute-start | bytes 294920 | tf_op jit(solution)/shard_map/ppermute | solution.py:319
  55.2 1.7 %collective-permute-start.19 = (bf16[128,384]{1,0:T(8,128)(2,1)S(1)}, bf16[128,384]{1,0:T(8,128)(2,1)S(1)}, u32[]{:S(2)}, u32[]{:S(2)}) collective-permute-start(bf16[128,384]{1,0:T(8,128)(2,1)S(1)} %get-tuple-element.103), channel_id=1, source_target_pairs={{0,12},{4,8},{8,4},{12,0},{16,28},{20,24},{24,20},{28,16},{1,13},{... | collective-permute-start | bytes 294920 | tf_op jit(solution)/shard_map/ppermute | solution.py:319
  56.9 1.1 %collective-permute-done.17.refs_1_ = bf16[128,384]{1,0:T(8,128)(2,1)S(1)} collective-permute-done((bf16[128,384]{1,0:T(8,128)(2,1)S(1)}, bf16[128,384]{1,0:T(8,128)(2,1)S(1)}, u32[]{:S(2)}, u32[]{:S(2)}) %collective-permute-start.17) | collective-permute-done | bytes 98336 | tf_op jit(solution)/shard_map/ppermute | solution.py:319
  58.0 0.1 collective-permute-done.18.refs_2_
  58.1 2.6 %collective-permute-done.19.refs_3_ = bf16[128,384]{1,0:T(8,128)(2,1)S(1)} collective-permute-done((bf16[128,384]{1,0:T(8,128)(2,1)S(1)}, bf16[128,384]{1,0:T(8,128)(2,1)S(1)}, u32[]{:S(2)}, u32[]{:S(2)}) %collective-permute-start.19) | collective-permute-done | bytes 98336 | tf_op jit(solution)/shard_map/ppermute | solution.py:319
  60.7 0.9 %shard_map.121 = (bf16[128,2048]{1,0:T(8,128)(2,1)}, bf16[128,512]{1,0:T(8,128)(2,1)}, bf16[128,512]{1,0:T(8,128)(2,1)}, bf16[128,512]{1,0:T(8,128)(2,1)}) custom-call(bf16[128,1024]{1,0:T(8,128)(2,1)S(1)} %shard_map.112.mine, bf16[128,384]{1,0:T(8,128)(2,1)S(1)} %get-tuple-element.100.refs_0_, bf16[128,384]{1,0:T(8,128)(2,1)S(1)} %collective-permute-done.17.refs_1_, ...), custom_call_target="tpu_custom_call" | custom-call | flops 10000000 | tf_op jit(solution)/shard_map/pallas_call | solution.py:693
  61.7 0.7 %shard_map.122 = bf16[128,2048]{1,0:T(8,128)(2,1)} custom-call(bf16[128,1024]{1,0:T(8,128)(2,1)S(1)} %collective-permute-done.9.theirs, bf16[128,2048]{1,0:T(8,128)(2,1)} %get-tuple-element.104._), custom_call_target="tpu_custom_call", output_to_operand_aliasing={{}: (1, {})} | custom-call | flops 1000000 | tf_op jit(solution)/shard_map/pallas_call | solution.py:705
  (27 shorter events, 0.5 us)
Async XLA Ops:
  0.6 0.9 %copy-start.2 = (bf16[128,512]{1,0:T(8,128)(2,1)S(1)}, bf16[128,512]{1,0:T(8,128)(2,1)}, u32[]{:S(2)}) copy-start(bf16[128,512]{1,0:T(8,128)(2,1)} %q.1) | copy-start | bytes 393220
  0.6 1.0 %copy-start.3 = (bf16[128,512]{1,0:T(8,128)(2,1)S(1)}, bf16[128,512]{1,0:T(8,128)(2,1)}, u32[]{:S(2)}) copy-start(bf16[128,512]{1,0:T(8,128)(2,1)} %k.1) | copy-start | bytes 393220
  0.7 1.0 %copy-start.4 = (bf16[128,512]{1,0:T(8,128)(2,1)S(1)}, bf16[128,512]{1,0:T(8,128)(2,1)}, u32[]{:S(2)}) copy-start(bf16[128,512]{1,0:T(8,128)(2,1)} %v.1) | copy-start | bytes 393220
  1.7 4.7 %copy-start.5 = (s32[16]{0:T(128)S(1)}, s32[16]{0:T(128)}, u32[]{:S(2)}) copy-start(s32[16]{0:T(128)} %po.1) | copy-start | bytes 196
  1.7 4.7 %copy-start.6 = (s32[16]{0:T(128)S(1)}, s32[16]{0:T(128)}, u32[]{:S(2)}) copy-start(s32[16]{0:T(128)} %fo.1) | copy-start | bytes 196
  1.7 22.7 %copy-start = (bf16[512,2048]{1,0:T(8,128)(2,1)S(1)}, bf16[512,2048]{1,0:T(8,128)(2,1)}, u32[]{:S(2)}) copy-start(bf16[512,2048]{1,0:T(8,128)(2,1)} %w.7) | copy-start | bytes 6291460
  1.8 5.8 %collective-permute-start = (bf16[128,384]{1,0:T(8,128)(2,1)S(1)}, bf16[128,384]{1,0:T(8,128)(2,1)S(1)}, u32[]{:S(2)}, u32[]{:S(2)}) collective-permute-start(bf16[128,384]{1,0:T(8,128)(2,1)S(1)} %get-tuple-element.58), channel_id=1, source_target_pairs={{0,4},{4,0},{8,12},{12,8},{16,20},{20,16},{24,28},{28,24},{1,5},{5... | collective-permute-start | bytes 294920 | tf_op jit(solution)/shard_map/ppermute | solution.py:319
  4.8 5.5 %collective-permute-start.1 = (bf16[128,384]{1,0:T(8,128)(2,1)S(1)}, bf16[128,384]{1,0:T(8,128)(2,1)S(1)}, u32[]{:S(2)}, u32[]{:S(2)}) collective-permute-start(bf16[128,384]{1,0:T(8,128)(2,1)S(1)} %get-tuple-element.59), channel_id=1, source_target_pairs={{0,8},{4,12},{8,0},{12,4},{16,24},{20,28},{24,16},{28,20},{1,9},{5... | collective-permute-start | bytes 294920 | tf_op jit(solution)/shard_map/ppermute | solution.py:319
  6.4 5.5 %collective-permute-start.2 = (bf16[128,384]{1,0:T(8,128)(2,1)S(1)}, bf16[128,384]{1,0:T(8,128)(2,1)S(1)}, u32[]{:S(2)}, u32[]{:S(2)}) collective-permute-start(bf16[128,384]{1,0:T(8,128)(2,1)S(1)} %get-tuple-element.60), channel_id=1, source_target_pairs={{0,12},{4,8},{8,4},{12,0},{16,28},{20,24},{24,20},{28,16},{1,13},{... | collective-permute-start | bytes 294920 | tf_op jit(solution)/shard_map/ppermute | solution.py:319
  12.0 5.9 %collective-permute-start.3 = (bf16[128,256]{1,0:T(8,128)(2,1)S(1)}, bf16[128,256]{1,0:T(8,128)(2,1)S(1)}, u32[]{:S(2)}, u32[]{:S(2)}) collective-permute-start(bf16[128,256]{1,0:T(8,128)(2,1)S(1)} %get-tuple-element.64), channel_id=1, source_target_pairs={{0,16},{4,20},{8,24},{12,28},{16,0},{20,4},{24,8},{28,12},{1,17},{... | collective-permute-start | bytes 196616 | tf_op jit(solution)/shard_map/ppermute | solution.py:319
  17.9 4.0 %collective-permute-start.4 = (bf16[128,128]{1,0:T(8,128)(2,1)S(1)}, bf16[128,128]{1,0:T(8,128)(2,1)S(1)}, u32[]{:S(2)}, u32[]{:S(2)}) collective-permute-start(bf16[128,128]{1,0:T(8,128)(2,1)S(1)} %get-tuple-element.71), channel_id=1, source_target_pairs={{0,4},{4,0},{8,12},{12,8},{16,20},{20,16},{24,28},{28,24},{1,5},{5... | collective-permute-start | bytes 98312 | tf_op jit(solution)/shard_map/ppermute | solution.py:319
  18.2 3.9 %collective-permute-start.5 = (bf16[128,128]{1,0:T(8,128)(2,1)S(1)}, bf16[128,128]{1,0:T(8,128)(2,1)S(1)}, u32[]{:S(2)}, u32[]{:S(2)}) collective-permute-start(bf16[128,128]{1,0:T(8,128)(2,1)S(1)} %get-tuple-element.72), channel_id=1, source_target_pairs={{0,8},{4,12},{8,0},{12,4},{16,24},{20,28},{24,16},{28,20},{1,9},{5... | collective-permute-start | bytes 98312 | tf_op jit(solution)/shard_map/ppermute | solution.py:319
  19.6 4.8 %collective-permute-start.6 = (bf16[128,128]{1,0:T(8,128)(2,1)S(1)}, bf16[128,128]{1,0:T(8,128)(2,1)S(1)}, u32[]{:S(2)}, u32[]{:S(2)}) collective-permute-start(bf16[128,128]{1,0:T(8,128)(2,1)S(1)} %get-tuple-element.73), channel_id=1, source_target_pairs={{0,12},{4,8},{8,4},{12,0},{16,28},{20,24},{24,20},{28,16},{1,13},{... | collective-permute-start | bytes 98312 | tf_op jit(solution)/shard_map/ppermute | solution.py:319
  24.8 3.3 %copy-start.1 = (bf16[128,512]{1,0:T(8,128)(2,1)S(1)}, bf16[128,512]{1,0:T(8,128)(2,1)}, u32[]{:S(2)}) copy-start(bf16[128,512]{1,0:T(8,128)(2,1)} %refs_0_.1) | copy-start | bytes 393220
  24.8 1.6 %collective-permute-start.7 = (bf16[128,1024]{1,0:T(8,128)(2,1)S(1)}, bf16[128,1024]{1,0:T(8,128)(2,1)S(1)}, u32[]{:S(2)}, u32[]{:S(2)}) collective-permute-start(bf16[128,1024]{1,0:T(8,128)(2,1)S(1)} %get-tuple-element.75), channel_id=1, source_target_pairs={{0,1},{1,0},{2,3},{3,2},{4,5},{5,4},{6,7},{7,6},{8,9},{9,8},{10,11... | collective-permute-start | bytes 786440 | tf_op jit(solution)/shard_map/ppermute | solution.py:319
  26.4 11.2 %collective-permute-start.8 = (bf16[128,1024]{1,0:T(8,128)(2,1)S(1)}, bf16[128,1024]{1,0:T(8,128)(2,1)S(1)}, u32[]{:S(2)}, u32[]{:S(2)}) collective-permute-start(bf16[128,1024]{1,0:T(8,128)(2,1)S(1)} %shard_map.111.first), channel_id=1, source_target_pairs={{0,2},{1,3},{2,0},{3,1},{4,6},{5,7},{6,4},{7,5},{8,10},{9,11},{10,... | collective-permute-start | bytes 786440 | tf_op jit(solution)/shard_map/ppermute | solution.py:319
  28.0 9.6 %collective-permute-start.11 = (bf16[128,512]{1,0:T(8,128)(2,1)S(1)}, bf16[128,512]{1,0:T(8,128)(2,1)S(1)}, u32[]{:S(2)}, u32[]{:S(2)}) collective-permute-start(bf16[128,512]{1,0:T(8,128)(2,1)S(1)} %copy-done.1), channel_id=1, source_target_pairs={{0,2},{1,3},{2,0},{3,1},{4,6},{5,7},{6,4},{7,5},{8,10},{9,11},{10,... | collective-permute-start | bytes 393224 | tf_op jit(solution)/shard_map/ppermute | solution.py:319
  28.5 9.8 %collective-permute-start.10 = (bf16[128,512]{1,0:T(8,128)(2,1)S(1)}, bf16[128,512]{1,0:T(8,128)(2,1)S(1)}, u32[]{:S(2)}, u32[]{:S(2)}) collective-permute-start(bf16[128,512]{1,0:T(8,128)(2,1)S(1)} %copy-done.1), channel_id=1, source_target_pairs={{0,1},{1,0},{2,3},{3,2},{4,5},{5,4},{6,7},{7,6},{8,9},{9,8},{10,11... | collective-permute-start | bytes 393224 | tf_op jit(solution)/shard_map/ppermute | solution.py:319
  37.7 1.3 %collective-permute-start.12 = (bf16[128,512]{1,0:T(8,128)(2,1)S(1)}, bf16[128,512]{1,0:T(8,128)(2,1)S(1)}, u32[]{:S(2)}, u32[]{:S(2)}) collective-permute-start(bf16[128,512]{1,0:T(8,128)(2,1)S(1)} %collective-permute-done.11.facing), channel_id=1, source_target_pairs={{0,1},{1,0},{2,3},{3,2},{4,5},{5,4},{6,7},{7,6},{8,9},{9,8},{10,11... | collective-permute-start | bytes 393224 | tf_op jit(solution)/shard_map/ppermute | solution.py:319
  37.7 24.0 %collective-permute-start.9 = (bf16[128,1024]{1,0:T(8,128)(2,1)S(1)}, bf16[128,1024]{1,0:T(8,128)(2,1)S(1)}, u32[]{:S(2)}, u32[]{:S(2)}) collective-permute-start(bf16[128,1024]{1,0:T(8,128)(2,1)S(1)} %shard_map.112.mine), channel_id=1, source_target_pairs={{0,1},{1,0},{2,3},{3,2},{4,5},{5,4},{6,7},{7,6},{8,9},{9,8},{10,11... | collective-permute-start | bytes 786440 | tf_op jit(solution)/shard_map/ppermute | solution.py:319
  39.5 4.0 %collective-permute-start.13 = (bf16[128,128]{1,0:T(8,128)(2,1)S(1)}, bf16[128,128]{1,0:T(8,128)(2,1)S(1)}, u32[]{:S(2)}, u32[]{:S(2)}) collective-permute-start(bf16[128,128]{1,0:T(8,128)(2,1)S(1)} %get-tuple-element.79), channel_id=1, source_target_pairs={{0,4},{4,0},{8,12},{12,8},{16,20},{20,16},{24,28},{28,24},{1,5},{5... | collective-permute-start | bytes 98312 | tf_op jit(solution)/shard_map/ppermute | solution.py:319
  40.3 4.1 %collective-permute-start.14 = (bf16[128,128]{1,0:T(8,128)(2,1)S(1)}, bf16[128,128]{1,0:T(8,128)(2,1)S(1)}, u32[]{:S(2)}, u32[]{:S(2)}) collective-permute-start(bf16[128,128]{1,0:T(8,128)(2,1)S(1)} %get-tuple-element.80), channel_id=1, source_target_pairs={{0,8},{4,12},{8,0},{12,4},{16,24},{20,28},{24,16},{28,20},{1,9},{5... | collective-permute-start | bytes 98312 | tf_op jit(solution)/shard_map/ppermute | solution.py:319
  42.1 4.8 %collective-permute-start.15 = (bf16[128,128]{1,0:T(8,128)(2,1)S(1)}, bf16[128,128]{1,0:T(8,128)(2,1)S(1)}, u32[]{:S(2)}, u32[]{:S(2)}) collective-permute-start(bf16[128,128]{1,0:T(8,128)(2,1)S(1)} %get-tuple-element.81), channel_id=1, source_target_pairs={{0,12},{4,8},{8,4},{12,0},{16,28},{20,24},{24,20},{28,16},{1,13},{... | collective-permute-start | bytes 98312 | tf_op jit(solution)/shard_map/ppermute | solution.py:319
  47.4 5.8 %collective-permute-start.16 = (bf16[128,256]{1,0:T(8,128)(2,1)S(1)}, bf16[128,256]{1,0:T(8,128)(2,1)S(1)}, u32[]{:S(2)}, u32[]{:S(2)}) collective-permute-start(bf16[128,256]{1,0:T(8,128)(2,1)S(1)} %get-tuple-element.99), channel_id=1, source_target_pairs={{0,16},{4,20},{8,24},{12,28},{16,0},{20,4},{24,8},{28,12},{1,17},{... | collective-permute-start | bytes 196616 | tf_op jit(solution)/shard_map/ppermute | solution.py:319
  53.4 4.7 %collective-permute-start.17 = (bf16[128,384]{1,0:T(8,128)(2,1)S(1)}, bf16[128,384]{1,0:T(8,128)(2,1)S(1)}, u32[]{:S(2)}, u32[]{:S(2)}) collective-permute-start(bf16[128,384]{1,0:T(8,128)(2,1)S(1)} %get-tuple-element.101), channel_id=1, source_target_pairs={{0,4},{4,0},{8,12},{12,8},{16,20},{20,16},{24,28},{28,24},{1,5},{5... | collective-permute-start | bytes 294920 | tf_op jit(solution)/shard_map/ppermute | solution.py:319
  53.4 4.7 %collective-permute-start.18 = (bf16[128,384]{1,0:T(8,128)(2,1)S(1)}, bf16[128,384]{1,0:T(8,128)(2,1)S(1)}, u32[]{:S(2)}, u32[]{:S(2)}) collective-permute-start(bf16[128,384]{1,0:T(8,128)(2,1)S(1)} %get-tuple-element.102), channel_id=1, source_target_pairs={{0,8},{4,12},{8,0},{12,4},{16,24},{20,28},{24,16},{28,20},{1,9},{5... | collective-permute-start | bytes 294920 | tf_op jit(solution)/shard_map/ppermute | solution.py:319
  55.2 5.5 %collective-permute-start.19 = (bf16[128,384]{1,0:T(8,128)(2,1)S(1)}, bf16[128,384]{1,0:T(8,128)(2,1)S(1)}, u32[]{:S(2)}, u32[]{:S(2)}) collective-permute-start(bf16[128,384]{1,0:T(8,128)(2,1)S(1)} %get-tuple-element.103), channel_id=1, source_target_pairs={{0,12},{4,8},{8,4},{12,0},{16,28},{20,24},{24,20},{28,16},{1,13},{... | collective-permute-start | bytes 294920 | tf_op jit(solution)/shard_map/ppermute | solution.py:319
